TPU v7x, 32 devices: a whole 2x2x4 slice. The times are simulated.
32 devices in a mesh: group: 2 (over x), dev: 16 (over z, y, core).
Axes of the slice: x: 2, y: 2, z: 4, core: 2. Of those that a mesh axis runs over, the one named last changes fastest.
Arguments:
- teacher: bfloat16 [192, 8192], P(('group', 'dev')), may hold values from -6 to 6
- owner: int32 [2, 16], replicated, may hold values from 0 to 15, each once within a row
- proj_tiles: bfloat16 [8192, 4096], P('dev'), may hold values from -0.0625 to 0.0625
- student_tiles: bfloat16 [192, 4096], P(('group', 'dev')), may hold values from -6 to 6
Outputs:
- grad_proj_tiles: bfloat16 [8192, 4096], P('dev')
- grad_student_tiles: bfloat16 [192, 4096], P(('group', 'dev'))
Inputs may be any that keep to these rules, and one draw needn't show every extreme that they name: Each row of owner is a permutation of 0 to 15.
All inputs are finite; a program needn't handle non-finite values.
Results may differ from a plain program's by a relative error of at most 0.0069.
Values may be sent and summed in bfloat16 or wider, within the bound.
No kernel may reach another device: no remote copies, remote signals or barrier semaphores. Data moves between devices by JAX's collectives and lax.ppermute only.
A program may use at most 64 MiB of HBM per device.

v0:
```python
import functools
import math

import jax
import jax.numpy as jnp
from jax import lax
from jax.experimental import pallas as pl
from jax.experimental.pallas import tpu as pltpu
from jax.sharding import PartitionSpec as P


DS = 4096
FEAT_SPLIT = 16
NEAR = 4


epsilon = 1e-06


def across(value, group_mask, dev_mask):
    groups, devices = lax.axis_size("group"), lax.axis_size("dev")
    pairs = [
        (g * devices + d, (g ^ group_mask) * devices + (d ^ dev_mask))
        for g in range(groups)
        for d in range(devices)
    ]
    return lax.ppermute(value, ("group", "dev"), pairs)


def gather_wide(block, column_index, spread):
    step = 1
    while step < spread:
        arrived = across(block, 0, step * FEAT_SPLIT)
        my_bit = (column_index & step) > 0
        block = jnp.concatenate(
            [jnp.where(my_bit, arrived, block), jnp.where(my_bit, block, arrived)], axis=0
        )
        step *= 2
    return block


def wide_shards(teacher, owner, proj_tiles, student_tiles):
    row_count, width = teacher.shape
    device_count = lax.axis_size("dev")
    spread = device_count // FEAT_SPLIT
    block_teacher = width // FEAT_SPLIT
    block_student = proj_tiles.shape[1]
    unit = spread * row_count
    far = FEAT_SPLIT // NEAR
    dev_index = lax.axis_index("dev")
    feat_index = dev_index % FEAT_SPLIT
    column_index = dev_index // FEAT_SPLIT
    group_index = lax.axis_index("group")

    full_rows = gather_wide(teacher, column_index, spread)
    pieces = full_rows.reshape(unit, FEAT_SPLIT, block_teacher).transpose(1, 0, 2)
    relative = jnp.arange(FEAT_SPLIT)
    pieces = jnp.take(pieces, feat_index ^ relative, axis=0)
    pieces = pieces.reshape(far, NEAR, unit, block_teacher)
    held = jnp.stack(
        [pieces[0]] + [across(pieces[m], 0, m * NEAR) for m in range(1, far)]
    )
    slots = jnp.stack(
        [held[:, 0]] + [across(held[:, m], 0, m) for m in range(1, NEAR)]
    )
    slots = slots.transpose(1, 0, 2, 3).reshape(device_count, row_count, block_teacher)

    place = jnp.array(
        [c | (n << 1) | (f << 2) for c in range(2) for n in range(NEAR // 2) for f in range(far)]
    )
    owner_row = lax.dynamic_index_in_dim(owner, group_index, 0, keepdims=False)
    student_block = ((feat_index ^ place)[:, None] * spread + jnp.arange(spread)[None]).reshape(-1)
    teacher_block = owner_row[student_block]
    slot = ((teacher_block % FEAT_SPLIT) ^ feat_index) * spread + teacher_block // FEAT_SPLIT
    states = jnp.take(slots, slot, axis=0).reshape(device_count * row_count, block_teacher)
    other_states = across(states, 1, 0)

    partial_value = jnp.dot(states, proj_tiles, preferred_element_type=jnp.float32)
    partial_value = partial_value.reshape(2, -1, block_student)
    for mask in (1, 2):
        arrived = across(partial_value[1].astype(jnp.bfloat16), 0, mask)
        partial_value = (partial_value[0] + arrived.astype(jnp.float32)).reshape(
            2, -1, block_student
        )
    partial_value = partial_value.reshape(far, unit, block_student)
    projected = partial_value[0]
    leaving = partial_value.astype(jnp.bfloat16)
    for m in range(1, far):
        projected = projected + across(leaving[m], 0, m * NEAR).astype(jnp.float32)

    target = student_tiles.astype(jnp.float32)
    row_sums = jnp.stack(
        [jnp.sum(projected * projected, axis=1), jnp.sum(target * projected, axis=1)]
    )
    step = 1
    while step < spread:
        row_sums = row_sums + across(row_sums, 0, step * FEAT_SPLIT)
        step *= 2
    root_mean = jnp.sqrt(row_sums[0] / DS + epsilon)
    normed = projected / root_mean[:, None]
    inner_mean = (row_sums[0] / (root_mean * root_mean) - row_sums[1] / root_mean) / DS
    upstream = normed - target
    row_slope = ((upstream - normed * inner_mean[:, None]) / root_mean[:, None]).astype(
        jnp.bfloat16
    )

    line = jnp.concatenate(
        [row_slope] + [across(row_slope, 0, m * NEAR) for m in range(1, far)], axis=0
    )
    own = [line, across(line, 0, 2)]
    other = [across(line, 1, 0), across(line, 1, 2)]
    own, other = jnp.concatenate(own), jnp.concatenate(other)
    slopes = jnp.concatenate([own, across(own, 0, 1), other, across(other, 0, 1)])
    grad_total = lax.dot_general(
        jnp.concatenate([states, other_states]),
        slopes,
        (((0,), (0,)), ((), ())),
        preferred_element_type=jnp.float32,
    )
    scale_factor = 1.0 / math.sqrt(lax.axis_size("group") * states.shape[0])
    return (
        (grad_total * scale_factor).astype(jnp.bfloat16),
        (target - normed).astype(jnp.bfloat16),
    )


LANES = 128
PARTS = (1, 1)
MIB = 1 << 20
IN_VMEM = pl.BlockSpec(memory_space=pltpu.VMEM)
IN_SMEM = pl.BlockSpec(memory_space=pltpu.SMEM)
ANYWHERE = pl.BlockSpec(memory_space=pl.ANY)
IN_HBM = pl.BlockSpec(memory_space=pltpu.HBM)


def local_call(kernel, outs, args, specs=None, scratch=(), flops=0, moved=0, limit=8, **extra):
    return pl.pallas_call(
        kernel,
        out_shape=[jax.ShapeDtypeStruct(shape, kind) for shape, kind in outs],
        in_specs=specs or [IN_VMEM] * len(args),
        out_specs=[IN_VMEM] * len(outs),
        scratch_shapes=list(scratch),
        compiler_params=pltpu.CompilerParams(vmem_limit_bytes=limit * MIB),
        cost_estimate=pl.CostEstimate(flops=flops, bytes_accessed=moved, transcendentals=0),
        **extra,
    )(*args)


def split_kernel(x_ref, near_ref, side_ref, core_ref, sems):
    far, _, part = near_ref.shape
    feat = lax.axis_index("dev")
    copies = []
    for c in range(2):
        for n in range(2):
            for m in range(far):
                out = core_ref.at[n, m] if c else (side_ref if n else near_ref).at[m]
                first = pl.multiple_of((feat ^ (c | (n << 1) | (m << 2))) * part, part)
                copies.append(
                    pltpu.make_async_copy(x_ref.at[:, pl.ds(first, part)], out, sems.at[len(copies)])
                )
    for copy in copies:
        copy.start()
    for copy in copies:
        copy.wait()


def side_kernel(side_ref, core_ref, out_ref):
    out_ref[0] = side_ref[...]
    out_ref[1] = core_ref[1]


def far_kernel(near_ref, core_ref, side_ref, *outs):
    for m, out in enumerate(outs):
        out[0] = near_ref[m]
        out[1] = core_ref[0, m]
        out[2] = side_ref[0, m]
        out[3] = side_ref[1, m]


def fetch(tiles_ref, out_ref, sems, first):
    count = sems.shape[0]
    rows, width = out_ref.shape[0] // count, out_ref.shape[1]
    copies = []
    for i in range(count):
        part = pl.ds(i * rows, rows)
        copies.append(
            pltpu.make_async_copy(
                tiles_ref.at[part, pl.ds(first, width)], out_ref.at[part], sems.at[i]
            )
        )
        copies[-1].start()
    return copies


def first_kernel(place, unit, owner_ref, tiles_ref, pick_ref, out_ref, owner_here, sem, sems):
    order = pltpu.make_async_copy(owner_ref, owner_here, sem)
    order.start()
    copies = fetch(tiles_ref, out_ref, sems, 0)
    feat, group = lax.axis_index("dev"), lax.axis_index("group")
    row = lax.broadcasted_iota(jnp.int32, pick_ref.shape, 0)
    source = lax.broadcasted_iota(jnp.int32, pick_ref.shape, 1)
    wanted = row
    order.wait()
    for p, shift in enumerate(place):
        slot = owner_here[group, feat ^ shift] ^ feat
        wanted = jnp.where(row // unit == p, row + (slot - p) * unit, wanted)
    pick_ref[...] = jnp.where(source == wanted, 1.0, 0.0).astype(jnp.bfloat16)
    for copy in copies:
        copy.wait()


def second_kernel(first, tiles_ref, out_ref, sems):
    for copy in fetch(tiles_ref, out_ref, sems, first):
        copy.wait()


def order_kernel(pick_ref, *refs):
    sources, (first_ref, second_ref) = refs[:-6], refs[-6:-4]
    lhs_ref, leaving_ref, staying_ref, slots = refs[-4:]
    near, unit = sources[0].shape[0], sources[0].shape[1]
    for m, source in enumerate(sources):
        for k in range(near):
            first = (m * near + k) * unit
            slots[first : first + unit, :] = source[k].astype(jnp.float32)
    rows = jnp.dot(
        pick_ref[...], slots[...].astype(jnp.bfloat16), preferred_element_type=jnp.float32
    )
    lhs = rows.astype(jnp.bfloat16)
    lhs_ref[...] = lhs
    half, base = staying_ref.shape[0], 0
    for tiles_ref in (first_ref, second_ref):
        width = tiles_ref.shape[1]
        step = min(width, 512)
        for start in range(0, width, step):
            tiles = tiles_ref[:, start : start + step]
            part = jnp.dot(lhs, tiles, preferred_element_type=jnp.float32)
            cols = slice(base + start, base + start + step)
            staying_ref[:, cols] = part[:half]
            leaving_ref[:, cols] = part[half:].astype(jnp.bfloat16)
        base += width


def halve_kernel(kept_ref, arrived_ref, leaving_ref, staying_ref):
    half = staying_ref.shape[0]
    staying_ref[...] = kept_ref[:half] + arrived_ref[:half].astype(jnp.float32)
    leaving_ref[...] = (kept_ref[half:] + arrived_ref[half:].astype(jnp.float32)).astype(
        jnp.bfloat16
    )


def units_kernel(kept_ref, arrived_ref, own_ref, *refs):
    leaving, lines = refs[:-1], refs[-1]
    count, width = kept_ref.shape
    depth = width // LANES
    size = own_ref.shape[0]
    for t in range(depth):
        cols = slice(t * LANES, (t + 1) * LANES)
        total = kept_ref[:, cols] + arrived_ref[:, cols].astype(jnp.float32)
        lines[pl.ds(t, count, stride=depth), :] = total
    own_ref[...] = lines[:size]
    for m, out in enumerate(leaving):
        out[...] = lines[(m + 1) * size : (m + 2) * size].astype(jnp.bfloat16)


def slope_kernel(unit, own_ref, *refs):
    arrived, (target_ref, slope_ref, grad_ref) = refs[:-3], refs[-3:]
    total = own_ref[...]
    for other in arrived:
        total = total + other[...].astype(jnp.float32)
    total = total.reshape(unit, -1, LANES)
    target = target_ref[...].astype(jnp.float32).reshape(unit, -1, LANES)

    def row_sum(part):
        return jnp.sum(jnp.sum(part, axis=1, keepdims=True), axis=2, keepdims=True)

    squares, products = row_sum(total * total), row_sum(total * target)
    root_mean = jnp.sqrt(squares / DS + epsilon)
    inner_mean = (squares / (root_mean * root_mean) - products / root_mean) / DS
    normed = total / root_mean
    upstream = normed - target
    value = (upstream - normed * inner_mean) / root_mean
    slope_ref[...] = value.reshape(-1, LANES).astype(jnp.bfloat16)
    grad_ref[...] = (target - normed).reshape(-1, LANES)


def rows_kernel(lines_ref, out_ref):
    count = out_ref.shape[0]
    depth = lines_ref.shape[0] // count
    for t in range(depth):
        cols = slice(t * LANES, (t + 1) * LANES)
        out_ref[:, cols] = lines_ref[pl.ds(t, count, stride=depth), :].astype(jnp.bfloat16)


def line_kernel(units, *refs):
    sources, outs, lines = refs[:units], refs[units:-1], refs[-1]
    size = sources[0].shape[0]
    count = outs[0].shape[0]
    depth = lines.shape[0] // count
    for m, source in enumerate(sources):
        lines[m * size : (m + 1) * size, :] = source[...].astype(jnp.float32)
    places = [(out, t) for out in outs for t in range(out.shape[1] // LANES)]
    for source, (out, t) in enumerate(places):
        cols = slice(t * LANES, (t + 1) * LANES)
        out[:, cols] = lines[pl.ds(source, count, stride=depth), :].astype(jnp.bfloat16)


def turn_kernel(own_ref, other_ref, out_ref):
    half = own_ref.shape[0]
    for i, source in enumerate((own_ref, other_ref)):
        out_ref[:, i * half : (i + 1) * half] = source[...].astype(jnp.float32).T.astype(
            jnp.bfloat16
        )


def grad_kernel(scale, step, per, states_ref, *refs):
    slopes, (out_ref, rhs, staged, sems) = refs[:-4], refs[-4:]
    copies, first = [], 0
    for chunk in range(len(slopes) // per):
        pieces = slopes[chunk * per : (chunk + 1) * per]
        count, width = pieces[0].shape
        for start in range(0, width, step):
            j = first // step
            for i, piece in enumerate(pieces):
                rhs[j % 2, i * count : (i + 1) * count, :] = piece[:, start : start + step]
            part = jnp.dot(states_ref[...], rhs[j % 2], preferred_element_type=jnp.float32)
            staged[j] = (part * scale).astype(jnp.bfloat16)
            copies.append(
                pltpu.make_async_copy(staged.at[j], out_ref.at[:, pl.ds(first, step)], sems.at[j])
            )
            copies[-1].start()
            first += step
    for copy in copies:
        copy.wait()


def grad_call(scale, states, slopes, per, shape, step=256):
    block_teacher, rows = states.shape
    count = shape[1] // step
    return pl.pallas_call(
        functools.partial(grad_kernel, scale, step, per),
        out_shape=jax.ShapeDtypeStruct(shape, jnp.bfloat16),
        in_specs=[IN_VMEM] * (len(slopes) + 1),
        out_specs=ANYWHERE,
        scratch_shapes=[
            pltpu.VMEM((2, rows, step), jnp.bfloat16),
            pltpu.VMEM((count, block_teacher, step), jnp.bfloat16),
            pltpu.SemaphoreType.DMA((count,)),
        ],
        compiler_params=pltpu.CompilerParams(vmem_limit_bytes=16 * MIB),
        cost_estimate=pl.CostEstimate(
            flops=2 * rows * block_teacher * shape[1],
            bytes_accessed=2 * block_teacher * shape[1],
            transcendentals=0,
        ),
    )(states, *slopes)


def far_across(values):
    arrived = []
    for m in range(1, len(values)):
        arrived.append(across(values[m], 0, m * NEAR))
    return arrived


def line_shards(teacher, owner, proj_tiles, student_tiles):
    unit, _ = teacher.shape
    block_teacher, block_student = proj_tiles.shape
    near, far = NEAR, FEAT_SPLIT // NEAR
    half = FEAT_SPLIT * unit
    cuts = [block_student * part // sum(PARTS) for part in PARTS]
    depth = block_student // LANES
    size = unit * depth
    bf16, f32 = jnp.bfloat16, jnp.float32

    place = [c | (n << 1) | (m << 2) for c in range(2) for n in range(2) for m in range(far)]

    block = (unit, block_teacher)
    own_near, own_side, leaving = local_call(
        split_kernel,
        [((far, *block), bf16), ((far, *block), bf16), ((2, far, *block), bf16)],
        [pltpu.with_memory_space_constraint(teacher, pltpu.HBM)],
        specs=[IN_HBM],
        scratch=[pltpu.SemaphoreType.DMA((FEAT_SPLIT,))],
    )
    core = across(leaving, 0, 1)
    (leaving,) = local_call(side_kernel, [((2, far, *block), bf16)], [own_side, core])
    side = across(leaving, 0, 2)
    held = local_call(far_kernel, [((near, *block), bf16)] * far, [own_near, core, side])
    held = [held[0]] + far_across(held)

    tiles = pltpu.with_memory_space_constraint(proj_tiles, pltpu.HBM)
    part = (block_teacher, block_student // 2)
    work = dict(flops=block_teacher * half * block_student, moved=block_teacher * block_student)
    pick, first_tiles = local_call(
        functools.partial(first_kernel, place, unit),
        [((half, half), bf16), (part, bf16)],
        [pltpu.with_memory_space_constraint(owner, pltpu.HBM), tiles],
        specs=[IN_HBM] * 2,
        scratch=[
            pltpu.SMEM(owner.shape, owner.dtype),
            pltpu.SemaphoreType.DMA,
            pltpu.SemaphoreType.DMA((8,)),
        ],
        **work,
    )
    (second_tiles,) = local_call(
        functools.partial(second_kernel, part[1]),
        [(part, bf16)],
        [tiles],
        specs=[IN_HBM],
        scratch=[pltpu.SemaphoreType.DMA((8,))],
        **work,
    )
    states, leaving, staying = local_call(
        order_kernel,
        [
            ((half, block_teacher), bf16),
            ((half // 2, block_student), bf16),
            ((half // 2, block_student), f32),
        ],
        [pick, *held, first_tiles, second_tiles],
        scratch=[pltpu.VMEM((half, block_teacher), f32)],
        flops=2 * half * block_teacher * block_student,
    )

    arrived = across(leaving, 0, 1)
    leaving, staying = local_call(
        halve_kernel,
        [((half // 4, block_student), bf16), ((half // 4, block_student), f32)],
        [staying, arrived],
    )
    states_too, leaving = lax.optimization_barrier((states, leaving))
    arrived, other_states = lax.optimization_barrier(
        (across(leaving, 0, 2), across(states_too, 1, 0))
    )
    own, *leaving = local_call(
        units_kernel,
        [((size, LANES), f32)] + [((size, LANES), bf16)] * (far - 1),
        [staying, arrived],
        scratch=[pltpu.VMEM((far * size, LANES), f32)],
    )
    arrived = far_across([None, *leaving])
    slope, grad = local_call(
        functools.partial(slope_kernel, unit),
        [((size, LANES), bf16), ((size, LANES), f32)],
        [own, *arrived, student_tiles.reshape(size, LANES)],
    )
    (grad,) = local_call(rows_kernel, [((unit, block_student), bf16)], [grad])

    line = [slope] + far_across([slope] * far)
    lines = local_call(
        functools.partial(line_kernel, far),
        [((far * unit, cut), bf16) for cut in cuts],
        line,
        scratch=[pltpu.VMEM((far * size, LANES), f32)],
    )
    scale = 1.0 / math.sqrt(lax.axis_size("group") * half)
    first, second = lines
    first_group, second_near = across(first, 1, 0), across(second, 0, 2)
    second_group, first_near = across(second, 1, 0), across(first, 0, 2)
    first_both, second_both = across(first_group, 0, 2), across(second_near, 1, 0)
    (turned,) = local_call(turn_kernel, [((block_teacher, 2 * half), bf16)], [states, other_states])
    pieces = []
    for own, other in (
        ((first, first_near), (first_group, first_both)),
        ((second, second_near), (second_group, second_both)),
    ):
        pieces += [*own, *[across(piece, 0, 1) for piece in own]]
        pieces += [*other, *[across(piece, 0, 1) for piece in other]]
    grad_proj = grad_call(scale, turned, pieces, len(pieces) // 2, (block_teacher, block_student))
    return grad_proj, grad


def shards(*blocks):
    if lax.axis_size("dev") == FEAT_SPLIT:
        return line_shards(*blocks)
    return wide_shards(*blocks)


def solution(mesh):
    placed = (P(("group", "dev"), None), P(), P("dev", None), P(("group", "dev"), None))
    return jax.shard_map(
        shards,
        mesh=mesh,
        in_specs=placed,
        out_specs=(P("dev", None), P(("group", "dev"), None)),
        check_vma=False,
    )
```

profile of v0, /device:TPU:0, one launch (start us, length us, event | category | flops | bytes accessed | tf_op | source)
XLA Modules:
  0.0 62.0 jit_solution(14419402279008679304)
XLA Ops:
  0.6 1.0 %shard_map.60 = (bf16[4,6,512]{2,1,0:T(8,128)(2,1)S(1)}, bf16[4,6,512]{2,1,0:T(8,128)(2,1)S(1)}, bf16[2,4,6,512]{3,2,1,0:T(8,128)(2,1)S(1)}) custom-call(bf16[6,8192]{1,0:T(8,128)(2,1)} %x_ref.1), custom_call_target="tpu_custom_call" | custom-call | tf_op jit(solution)/shard_map/pallas_call | solution.py:137
  1.7 0.6 collective-permute-start
  2.2 0.9 %collective-permute-done.core_ref = bf16[2,4,6,512]{3,2,1,0:T(8,128)(2,1)S(1)} collective-permute-done((bf16[2,4,6,512]{3,2,1,0:T(8,128)(2,1)S(1)}, bf16[2,4,6,512]{3,2,1,0:T(8,128)(2,1)S(1)}, u32[]{:S(2)}, u32[]{:S(2)}) %collective-permute-start) | collective-permute-done | bytes 49184 | tf_op jit(solution)/shard_map/ppermute | solution.py:27
  3.1 2.9 %collective-permute-start.1 = (bf16[2,4,6,512]{3,2,1,0:T(8,128)(2,1)S(1)}, bf16[2,4,6,512]{3,2,1,0:T(8,128)(2,1)S(1)}, u32[]{:S(2)}, u32[]{:S(2)}) collective-permute-start(bf16[2,4,6,512]{3,2,1,0:T(8,128)(2,1)S(1)} %shard_map.61), channel_id=1, source_target_pairs={{0,2},{1,3},{2,0},{3,1},{4,6},{5,7},{6,4},{7,5},{8,10},{9,11},{10,... | collective-permute-start | bytes 147464 | tf_op jit(solution)/shard_map/ppermute | solution.py:27
  6.0 2.4 %collective-permute-done.1.side_ref = bf16[2,4,6,512]{3,2,1,0:T(8,128)(2,1)S(1)} collective-permute-done((bf16[2,4,6,512]{3,2,1,0:T(8,128)(2,1)S(1)}, bf16[2,4,6,512]{3,2,1,0:T(8,128)(2,1)S(1)}, u32[]{:S(2)}, u32[]{:S(2)}) %collective-permute-start.1) | collective-permute-done | bytes 49184 | tf_op jit(solution)/shard_map/ppermute | solution.py:27
  8.4 2.0 %collective-permute-start.2 = (bf16[4,6,512]{2,1,0:T(8,128)(2,1)S(1)}, bf16[4,6,512]{2,1,0:T(8,128)(2,1)S(1)}, u32[]{:S(2)}, u32[]{:S(2)}) collective-permute-start(bf16[4,6,512]{2,1,0:T(8,128)(2,1)S(1)} %get-tuple-element.33), channel_id=1, source_target_pairs={{0,4},{1,5},{2,6},{3,7},{4,0},{5,1},{6,2},{7,3},{8,12},{9,13},{10,... | collective-permute-start | bytes 73736 | tf_op jit(solution)/shard_map/ppermute | solution.py:27
  10.4 2.6 %collective-permute-start.3 = (bf16[4,6,512]{2,1,0:T(8,128)(2,1)S(1)}, bf16[4,6,512]{2,1,0:T(8,128)(2,1)S(1)}, u32[]{:S(2)}, u32[]{:S(2)}) collective-permute-start(bf16[4,6,512]{2,1,0:T(8,128)(2,1)S(1)} %get-tuple-element.34), channel_id=1, source_target_pairs={{0,8},{1,9},{2,10},{3,11},{4,12},{5,13},{6,14},{7,15},{8,0},{9,1},... | collective-permute-start | bytes 73736 | tf_op jit(solution)/shard_map/ppermute | solution.py:27
  13.0 1.6 %shard_map.63.refs_5_ = bf16[512,2048]{1,0:T(8,128)(2,1)S(1)} custom-call(bf16[512,4096]{1,0:T(8,128)(2,1)} %tiles_ref.3), custom_call_target="tpu_custom_call" | custom-call | flops 201326592 | bytes 2097152 | tf_op jit(solution)/shard_map/pallas_call | solution.py:137
  14.6 1.6 %shard_map.59 = (bf16[96,96]{1,0:T(8,128)(2,1)S(1)}, bf16[512,2048]{1,0:T(8,128)(2,1)S(1)}) custom-call(s32[2,16]{1,0:T(2,128)} %owner_ref.1, bf16[512,4096]{1,0:T(8,128)(2,1)} %tiles_ref.3), custom_call_target="tpu_custom_call" | custom-call | flops 201326592 | bytes 2097152 | tf_op jit(solution)/shard_map/pallas_call | solution.py:137
  16.2 2.5 %collective-permute-done.4.refs_3_ = bf16[4,6,512]{2,1,0:T(8,128)(2,1)S(1)} collective-permute-done((bf16[4,6,512]{2,1,0:T(8,128)(2,1)S(1)}, bf16[4,6,512]{2,1,0:T(8,128)(2,1)S(1)}, u32[]{:S(2)}, u32[]{:S(2)}) %collective-permute-start.4) | collective-permute-done | bytes 24608 | tf_op jit(solution)/shard_map/ppermute | solution.py:27
  18.7 0.9 %shard_map.64 = (bf16[96,512]{1,0:T(8,128)(2,1)S(1)}, bf16[48,4096]{1,0:T(8,128)(2,1)S(1)}, f32[48,4096]{1,0:T(8,128)S(1)}) custom-call(bf16[96,96]{1,0:T(8,128)(2,1)S(1)} %get-tuple-element.28.pick_ref, bf16[4,6,512]{2,1,0:T(8,128)(2,1)S(1)} %get-tuple-element.32.refs_0_, bf16[4,6,512]{2,1,0:T(8,128)(2,1)S(1)} %collective-permute-done.2.refs_1_, ...), custom_call_target="tpu_custom_call" | custom-call | flops 402653184 | tf_op jit(solution)/shard_map/pallas_call | solution.py:137
  19.6 0.1 collective-permute-start.5
  19.7 1.7 %collective-permute-done.5.arrived_ref = bf16[48,4096]{1,0:T(8,128)(2,1)S(1)} collective-permute-done((bf16[48,4096]{1,0:T(8,128)(2,1)S(1)}, bf16[48,4096]{1,0:T(8,128)(2,1)S(1)}, u32[]{:S(2)}, u32[]{:S(2)}) %collective-permute-start.5) | collective-permute-done | bytes 393248 | tf_op jit(solution)/shard_map/ppermute | solution.py:27
  21.4 0.1 shard_map.65
  21.5 1.6 %collective-permute-start.6 = (bf16[24,4096]{1,0:T(8,128)(2,1)S(1)}, bf16[24,4096]{1,0:T(8,128)(2,1)S(1)}, u32[]{:S(2)}, u32[]{:S(2)}) collective-permute-start(bf16[24,4096]{1,0:T(8,128)(2,1)S(1)} %get-tuple-element.41), channel_id=1, source_target_pairs={{0,2},{1,3},{2,0},{3,1},{4,6},{5,7},{6,4},{7,5},{8,10},{9,11},{10,... | collective-permute-start | bytes 589832 | tf_op jit(solution)/shard_map/ppermute | solution.py:27
  23.1 1.5 %collective-permute-start.7 = (bf16[96,512]{1,0:T(8,128)(2,1)S(1)}, bf16[96,512]{1,0:T(8,128)(2,1)S(1)}, u32[]{:S(2)}, u32[]{:S(2)}) collective-permute-start(bf16[96,512]{1,0:T(8,128)(2,1)S(1)} %get-tuple-element.42.own_ref), channel_id=1, source_target_pairs={{0,16},{1,17},{2,18},{3,19},{4,20},{5,21},{6,22},{7,23},{8,24},{9,... | collective-permute-start | bytes 294920 | tf_op jit(solution)/shard_map/ppermute | solution.py:27
  24.6 3.1 %collective-permute-done.7.other_ref = bf16[96,512]{1,0:T(8,128)(2,1)S(1)} collective-permute-done((bf16[96,512]{1,0:T(8,128)(2,1)S(1)}, bf16[96,512]{1,0:T(8,128)(2,1)S(1)}, u32[]{:S(2)}, u32[]{:S(2)}) %collective-permute-start.7) | collective-permute-done | bytes 98336 | tf_op jit(solution)/shard_map/ppermute | solution.py:27
  27.7 0.8 %collective-permute-done.6.arrived_ref = bf16[24,4096]{1,0:T(8,128)(2,1)S(1)} collective-permute-done((bf16[24,4096]{1,0:T(8,128)(2,1)S(1)}, bf16[24,4096]{1,0:T(8,128)(2,1)S(1)}, u32[]{:S(2)}, u32[]{:S(2)}) %collective-permute-start.6) | collective-permute-done | bytes 196640 | tf_op jit(solution)/shard_map/ppermute | solution.py:27
  28.5 0.4 shard_map.67
  28.9 0.1 collective-permute-start.8
  29.0 1.9 %collective-permute-start.9 = (bf16[192,128]{1,0:T(8,128)(2,1)S(1)}, bf16[192,128]{1,0:T(8,128)(2,1)S(1)}, u32[]{:S(2)}, u32[]{:S(2)}) collective-permute-start(bf16[192,128]{1,0:T(8,128)(2,1)S(1)} %get-tuple-element.48), channel_id=1, source_target_pairs={{0,8},{1,9},{2,10},{3,11},{4,12},{5,13},{6,14},{7,15},{8,0},{9,1},... | collective-permute-start | bytes 147464 | tf_op jit(solution)/shard_map/ppermute | solution.py:27
  30.9 2.5 %collective-permute-start.10 = (bf16[192,128]{1,0:T(8,128)(2,1)S(1)}, bf16[192,128]{1,0:T(8,128)(2,1)S(1)}, u32[]{:S(2)}, u32[]{:S(2)}) collective-permute-start(bf16[192,128]{1,0:T(8,128)(2,1)S(1)} %get-tuple-element.49), channel_id=1, source_target_pairs={{0,12},{1,13},{2,14},{3,15},{4,8},{5,9},{6,10},{7,11},{8,4},{9,5},... | collective-permute-start | bytes 147464 | tf_op jit(solution)/shard_map/ppermute | solution.py:27
  33.4 0.1 reshape.7.refs_3_
  33.5 0.6 collective-permute-done.9.refs_1_
  34.1 2.8 %collective-permute-done.10.refs_2_ = bf16[192,128]{1,0:T(8,128)(2,1)S(1)} collective-permute-done((bf16[192,128]{1,0:T(8,128)(2,1)S(1)}, bf16[192,128]{1,0:T(8,128)(2,1)S(1)}, u32[]{:S(2)}, u32[]{:S(2)}) %collective-permute-start.10) | collective-permute-done | bytes 49184 | tf_op jit(solution)/shard_map/ppermute | solution.py:27
  36.9 0.1 shard_map.68
  37.0 2.5 %collective-permute-start.13 = (bf16[192,128]{1,0:T(8,128)(2,1)S(1)}, bf16[192,128]{1,0:T(8,128)(2,1)S(1)}, u32[]{:S(2)}, u32[]{:S(2)}) collective-permute-start(bf16[192,128]{1,0:T(8,128)(2,1)S(1)} %get-tuple-element.50.refs_0_), channel_id=1, source_target_pairs={{0,12},{1,13},{2,14},{3,15},{4,8},{5,9},{6,10},{7,11},{8,4},{9,5},... | collective-permute-start | bytes 147464 | tf_op jit(solution)/shard_map/ppermute | solution.py:27
  39.6 1.9 %collective-permute-start.11 = (bf16[192,128]{1,0:T(8,128)(2,1)S(1)}, bf16[192,128]{1,0:T(8,128)(2,1)S(1)}, u32[]{:S(2)}, u32[]{:S(2)}) collective-permute-start(bf16[192,128]{1,0:T(8,128)(2,1)S(1)} %get-tuple-element.50.refs_0_), channel_id=1, source_target_pairs={{0,4},{1,5},{2,6},{3,7},{4,0},{5,1},{6,2},{7,3},{8,12},{9,13},{10,... | collective-permute-start | bytes 147464 | tf_op jit(solution)/shard_map/ppermute | solution.py:27
  41.5 1.5 %collective-permute-done.13.refs_3_ = bf16[192,128]{1,0:T(8,128)(2,1)S(1)} collective-permute-done((bf16[192,128]{1,0:T(8,128)(2,1)S(1)}, bf16[192,128]{1,0:T(8,128)(2,1)S(1)}, u32[]{:S(2)}, u32[]{:S(2)}) %collective-permute-start.13) | collective-permute-done | bytes 49184 | tf_op jit(solution)/shard_map/ppermute | solution.py:27
  43.0 1.6 %collective-permute-done.12.refs_2_ = bf16[192,128]{1,0:T(8,128)(2,1)S(1)} collective-permute-done((bf16[192,128]{1,0:T(8,128)(2,1)S(1)}, bf16[192,128]{1,0:T(8,128)(2,1)S(1)}, u32[]{:S(2)}, u32[]{:S(2)}) %collective-permute-start.12) | collective-permute-done | bytes 49184 | tf_op jit(solution)/shard_map/ppermute | solution.py:27
  44.6 0.3 shard_map.69
  44.8 1.6 %collective-permute-start.17 = (bf16[24,2048]{1,0:T(8,128)(2,1)S(1)}, bf16[24,2048]{1,0:T(8,128)(2,1)S(1)}, u32[]{:S(2)}, u32[]{:S(2)}) collective-permute-start(bf16[24,2048]{1,0:T(8,128)(2,1)S(1)} %get-tuple-element.51.refs_0_), channel_id=1, source_target_pairs={{0,16},{1,17},{2,18},{3,19},{4,20},{5,21},{6,22},{7,23},{8,24},{9,... | collective-permute-start | bytes 294920 | tf_op jit(solution)/shard_map/ppermute | solution.py:27
  46.4 1.5 %collective-permute-start.14 = (bf16[24,2048]{1,0:T(8,128)(2,1)S(1)}, bf16[24,2048]{1,0:T(8,128)(2,1)S(1)}, u32[]{:S(2)}, u32[]{:S(2)}) collective-permute-start(bf16[24,2048]{1,0:T(8,128)(2,1)S(1)} %get-tuple-element.51.refs_0_), channel_id=1, source_target_pairs={{0,2},{1,3},{2,0},{3,1},{4,6},{5,7},{6,4},{7,5},{8,10},{9,11},{10,... | collective-permute-start | bytes 294920 | tf_op jit(solution)/shard_map/ppermute | solution.py:27
  47.9 0.5 collective-permute-start.21
  48.4 0.5 collective-permute-start.24
  48.9 0.6 collective-permute-done.17.refs_4_
  49.5 0.5 collective-permute-start.19
  50.0 2.0 %collective-permute-done.14.refs_1_ = bf16[24,2048]{1,0:T(8,128)(2,1)S(1)} collective-permute-done((bf16[24,2048]{1,0:T(8,128)(2,1)S(1)}, bf16[24,2048]{1,0:T(8,128)(2,1)S(1)}, u32[]{:S(2)}, u32[]{:S(2)}) %collective-permute-start.14) | collective-permute-done | bytes 98336 | tf_op jit(solution)/shard_map/ppermute | solution.py:27
  52.0 1.5 %collective-permute-start.18 = (bf16[24,2048]{1,0:T(8,128)(2,1)S(1)}, bf16[24,2048]{1,0:T(8,128)(2,1)S(1)}, u32[]{:S(2)}, u32[]{:S(2)}) collective-permute-start(bf16[24,2048]{1,0:T(8,128)(2,1)S(1)} %collective-permute-done.17.refs_4_), channel_id=1, source_target_pairs={{0,2},{1,3},{2,0},{3,1},{4,6},{5,7},{6,4},{7,5},{8,10},{9,11},{10,... | collective-permute-start | bytes 294920 | tf_op jit(solution)/shard_map/ppermute | solution.py:27
  53.6 0.1 collective-permute-done.21.refs_9_
  53.7 0.5 collective-permute-start.25
  54.2 0.5 collective-permute-start.16
  54.8 1.8 %collective-permute-done.18.refs_5_ = bf16[24,2048]{1,0:T(8,128)(2,1)S(1)} collective-permute-done((bf16[24,2048]{1,0:T(8,128)(2,1)S(1)}, bf16[24,2048]{1,0:T(8,128)(2,1)S(1)}, u32[]{:S(2)}, u32[]{:S(2)}) %collective-permute-start.18) | collective-permute-done | bytes 98336 | tf_op jit(solution)/shard_map/ppermute | solution.py:27
  56.7 1.6 %collective-permute-done.25.refs_13_ = bf16[24,2048]{1,0:T(8,128)(2,1)S(1)} collective-permute-done((bf16[24,2048]{1,0:T(8,128)(2,1)S(1)}, bf16[24,2048]{1,0:T(8,128)(2,1)S(1)}, u32[]{:S(2)}, u32[]{:S(2)}) %collective-permute-start.25) | collective-permute-done | bytes 98336 | tf_op jit(solution)/shard_map/ppermute | solution.py:27
  58.3 0.3 shard_map.66.states_ref
  58.6 0.7 %shard_map.71 = bf16[6,4096]{1,0:T(8,128)(2,1)} custom-call(f32[192,128]{1,0:T(8,128)S(1)} %get-tuple-element.53.lines_ref), custom_call_target="tpu_custom_call" | custom-call | tf_op jit(solution)/shard_map/pallas_call | solution.py:137
  59.3 0.3 collective-permute-done.27.refs_15_
  59.6 2.4 %shard_map.70 = bf16[512,4096]{1,0:T(8,128)(2,1)} custom-call(bf16[512,192]{1,0:T(8,128)(2,1)S(1)} %shard_map.66.states_ref, bf16[24,2048]{1,0:T(8,128)(2,1)S(1)} %get-tuple-element.51.refs_0_, bf16[24,2048]{1,0:T(8,128)(2,1)S(1)} %collective-permute-done.14.refs_1_, bf16[24,2048]{1,0:T(8,128)(2,1)S(1)} %collective-permute-done.15.refs_2_, ...), custom_call_target="tpu_custom_call" | custom-call | flops 805306368 | bytes 4194304 | tf_op jit(solution)/shard_map/pallas_call | solution.py:339
  (24 shorter events, 0.1 us)
Async XLA Ops:
  1.7 1.5 %collective-permute-start = (bf16[2,4,6,512]{3,2,1,0:T(8,128)(2,1)S(1)}, bf16[2,4,6,512]{3,2,1,0:T(8,128)(2,1)S(1)}, u32[]{:S(2)}, u32[]{:S(2)}) collective-permute-start(bf16[2,4,6,512]{3,2,1,0:T(8,128)(2,1)S(1)} %get-tuple-element.30), channel_id=1, source_target_pairs={{0,1},{1,0},{2,3},{3,2},{4,5},{5,4},{6,7},{7,6},{8,9},{9,8},{10,11... | collective-permute-start | bytes 147464 | tf_op jit(solution)/shard_map/ppermute | solution.py:27
  3.1 5.3 %collective-permute-start.1 = (bf16[2,4,6,512]{3,2,1,0:T(8,128)(2,1)S(1)}, bf16[2,4,6,512]{3,2,1,0:T(8,128)(2,1)S(1)}, u32[]{:S(2)}, u32[]{:S(2)}) collective-permute-start(bf16[2,4,6,512]{3,2,1,0:T(8,128)(2,1)S(1)} %shard_map.61), channel_id=1, source_target_pairs={{0,2},{1,3},{2,0},{3,1},{4,6},{5,7},{6,4},{7,5},{8,10},{9,11},{10,... | collective-permute-start | bytes 147464 | tf_op jit(solution)/shard_map/ppermute | solution.py:27
  8.4 7.8 %collective-permute-start.2 = (bf16[4,6,512]{2,1,0:T(8,128)(2,1)S(1)}, bf16[4,6,512]{2,1,0:T(8,128)(2,1)S(1)}, u32[]{:S(2)}, u32[]{:S(2)}) collective-permute-start(bf16[4,6,512]{2,1,0:T(8,128)(2,1)S(1)} %get-tuple-element.33), channel_id=1, source_target_pairs={{0,4},{1,5},{2,6},{3,7},{4,0},{5,1},{6,2},{7,3},{8,12},{9,13},{10,... | collective-permute-start | bytes 73736 | tf_op jit(solution)/shard_map/ppermute | solution.py:27
  10.4 5.8 %collective-permute-start.3 = (bf16[4,6,512]{2,1,0:T(8,128)(2,1)S(1)}, bf16[4,6,512]{2,1,0:T(8,128)(2,1)S(1)}, u32[]{:S(2)}, u32[]{:S(2)}) collective-permute-start(bf16[4,6,512]{2,1,0:T(8,128)(2,1)S(1)} %get-tuple-element.34), channel_id=1, source_target_pairs={{0,8},{1,9},{2,10},{3,11},{4,12},{5,13},{6,14},{7,15},{8,0},{9,1},... | collective-permute-start | bytes 73736 | tf_op jit(solution)/shard_map/ppermute | solution.py:27
  13.0 5.7 %collective-permute-start.4 = (bf16[4,6,512]{2,1,0:T(8,128)(2,1)S(1)}, bf16[4,6,512]{2,1,0:T(8,128)(2,1)S(1)}, u32[]{:S(2)}, u32[]{:S(2)}) collective-permute-start(bf16[4,6,512]{2,1,0:T(8,128)(2,1)S(1)} %get-tuple-element.35), channel_id=1, source_target_pairs={{0,12},{1,13},{2,14},{3,15},{4,8},{5,9},{6,10},{7,11},{8,4},{9,5},... | collective-permute-start | bytes 73736 | tf_op jit(solution)/shard_map/ppermute | solution.py:27
  14.6 18.8 %copy-start = (bf16[6,4096]{1,0:T(8,128)(2,1)S(1)}, bf16[6,4096]{1,0:T(8,128)(2,1)}, u32[]{:S(2)}) copy-start(bf16[6,4096]{1,0:T(8,128)(2,1)} %param.7) | copy-start | bytes 147460
  19.6 1.8 %collective-permute-start.5 = (bf16[48,4096]{1,0:T(8,128)(2,1)S(1)}, bf16[48,4096]{1,0:T(8,128)(2,1)S(1)}, u32[]{:S(2)}, u32[]{:S(2)}) collective-permute-start(bf16[48,4096]{1,0:T(8,128)(2,1)S(1)} %get-tuple-element.39), channel_id=1, source_target_pairs={{0,1},{1,0},{2,3},{3,2},{4,5},{5,4},{6,7},{7,6},{8,9},{9,8},{10,11... | collective-permute-start | bytes 1179656 | tf_op jit(solution)/shard_map/ppermute | solution.py:27
  21.5 7.0 %collective-permute-start.6 = (bf16[24,4096]{1,0:T(8,128)(2,1)S(1)}, bf16[24,4096]{1,0:T(8,128)(2,1)S(1)}, u32[]{:S(2)}, u32[]{:S(2)}) collective-permute-start(bf16[24,4096]{1,0:T(8,128)(2,1)S(1)} %get-tuple-element.41), channel_id=1, source_target_pairs={{0,2},{1,3},{2,0},{3,1},{4,6},{5,7},{6,4},{7,5},{8,10},{9,11},{10,... | collective-permute-start | bytes 589832 | tf_op jit(solution)/shard_map/ppermute | solution.py:27
  23.1 4.6 %collective-permute-start.7 = (bf16[96,512]{1,0:T(8,128)(2,1)S(1)}, bf16[96,512]{1,0:T(8,128)(2,1)S(1)}, u32[]{:S(2)}, u32[]{:S(2)}) collective-permute-start(bf16[96,512]{1,0:T(8,128)(2,1)S(1)} %get-tuple-element.42.own_ref), channel_id=1, source_target_pairs={{0,16},{1,17},{2,18},{3,19},{4,20},{5,21},{6,22},{7,23},{8,24},{9,... | collective-permute-start | bytes 294920 | tf_op jit(solution)/shard_map/ppermute | solution.py:27
  28.9 4.5 %collective-permute-start.8 = (bf16[192,128]{1,0:T(8,128)(2,1)S(1)}, bf16[192,128]{1,0:T(8,128)(2,1)S(1)}, u32[]{:S(2)}, u32[]{:S(2)}) collective-permute-start(bf16[192,128]{1,0:T(8,128)(2,1)S(1)} %get-tuple-element.47), channel_id=1, source_target_pairs={{0,4},{1,5},{2,6},{3,7},{4,0},{5,1},{6,2},{7,3},{8,12},{9,13},{10,... | collective-permute-start | bytes 147464 | tf_op jit(solution)/shard_map/ppermute | solution.py:27
  29.0 5.1 %collective-permute-start.9 = (bf16[192,128]{1,0:T(8,128)(2,1)S(1)}, bf16[192,128]{1,0:T(8,128)(2,1)S(1)}, u32[]{:S(2)}, u32[]{:S(2)}) collective-permute-start(bf16[192,128]{1,0:T(8,128)(2,1)S(1)} %get-tuple-element.48), channel_id=1, source_target_pairs={{0,8},{1,9},{2,10},{3,11},{4,12},{5,13},{6,14},{7,15},{8,0},{9,1},... | collective-permute-start | bytes 147464 | tf_op jit(solution)/shard_map/ppermute | solution.py:27
  30.9 6.0 %collective-permute-start.10 = (bf16[192,128]{1,0:T(8,128)(2,1)S(1)}, bf16[192,128]{1,0:T(8,128)(2,1)S(1)}, u32[]{:S(2)}, u32[]{:S(2)}) collective-permute-start(bf16[192,128]{1,0:T(8,128)(2,1)S(1)} %get-tuple-element.49), channel_id=1, source_target_pairs={{0,12},{1,13},{2,14},{3,15},{4,8},{5,9},{6,10},{7,11},{8,4},{9,5},... | collective-permute-start | bytes 147464 | tf_op jit(solution)/shard_map/ppermute | solution.py:27
  37.0 6.0 %collective-permute-start.13 = (bf16[192,128]{1,0:T(8,128)(2,1)S(1)}, bf16[192,128]{1,0:T(8,128)(2,1)S(1)}, u32[]{:S(2)}, u32[]{:S(2)}) collective-permute-start(bf16[192,128]{1,0:T(8,128)(2,1)S(1)} %get-tuple-element.50.refs_0_), channel_id=1, source_target_pairs={{0,12},{1,13},{2,14},{3,15},{4,8},{5,9},{6,10},{7,11},{8,4},{9,5},... | collective-permute-start | bytes 147464 | tf_op jit(solution)/shard_map/ppermute | solution.py:27
  39.6 5.0 %collective-permute-start.12 = (bf16[192,128]{1,0:T(8,128)(2,1)S(1)}, bf16[192,128]{1,0:T(8,128)(2,1)S(1)}, u32[]{:S(2)}, u32[]{:S(2)}) collective-permute-start(bf16[192,128]{1,0:T(8,128)(2,1)S(1)} %get-tuple-element.50.refs_0_), channel_id=1, source_target_pairs={{0,8},{1,9},{2,10},{3,11},{4,12},{5,13},{6,14},{7,15},{8,0},{9,1},... | collective-permute-start | bytes 147464 | tf_op jit(solution)/shard_map/ppermute | solution.py:27
  39.6 5.0 %collective-permute-start.11 = (bf16[192,128]{1,0:T(8,128)(2,1)S(1)}, bf16[192,128]{1,0:T(8,128)(2,1)S(1)}, u32[]{:S(2)}, u32[]{:S(2)}) collective-permute-start(bf16[192,128]{1,0:T(8,128)(2,1)S(1)} %get-tuple-element.50.refs_0_), channel_id=1, source_target_pairs={{0,4},{1,5},{2,6},{3,7},{4,0},{5,1},{6,2},{7,3},{8,12},{9,13},{10,... | collective-permute-start | bytes 147464 | tf_op jit(solution)/shard_map/ppermute | solution.py:27
  44.8 4.7 %collective-permute-start.17 = (bf16[24,2048]{1,0:T(8,128)(2,1)S(1)}, bf16[24,2048]{1,0:T(8,128)(2,1)S(1)}, u32[]{:S(2)}, u32[]{:S(2)}) collective-permute-start(bf16[24,2048]{1,0:T(8,128)(2,1)S(1)} %get-tuple-element.51.refs_0_), channel_id=1, source_target_pairs={{0,16},{1,17},{2,18},{3,19},{4,20},{5,21},{6,22},{7,23},{8,24},{9,... | collective-permute-start | bytes 294920 | tf_op jit(solution)/shard_map/ppermute | solution.py:27
  46.4 3.1 %collective-permute-start.15 = (bf16[24,2048]{1,0:T(8,128)(2,1)S(1)}, bf16[24,2048]{1,0:T(8,128)(2,1)S(1)}, u32[]{:S(2)}, u32[]{:S(2)}) collective-permute-start(bf16[24,2048]{1,0:T(8,128)(2,1)S(1)} %get-tuple-element.51.refs_0_), channel_id=1, source_target_pairs={{0,1},{1,0},{2,3},{3,2},{4,5},{5,4},{6,7},{7,6},{8,9},{9,8},{10,11... | collective-permute-start | bytes 294920 | tf_op jit(solution)/shard_map/ppermute | solution.py:27
  46.4 5.7 %collective-permute-start.14 = (bf16[24,2048]{1,0:T(8,128)(2,1)S(1)}, bf16[24,2048]{1,0:T(8,128)(2,1)S(1)}, u32[]{:S(2)}, u32[]{:S(2)}) collective-permute-start(bf16[24,2048]{1,0:T(8,128)(2,1)S(1)} %get-tuple-element.51.refs_0_), channel_id=1, source_target_pairs={{0,2},{1,3},{2,0},{3,1},{4,6},{5,7},{6,4},{7,5},{8,10},{9,11},{10,... | collective-permute-start | bytes 294920 | tf_op jit(solution)/shard_map/ppermute | solution.py:27
  47.9 5.8 %collective-permute-start.21 = (bf16[24,2048]{1,0:T(8,128)(2,1)S(1)}, bf16[24,2048]{1,0:T(8,128)(2,1)S(1)}, u32[]{:S(2)}, u32[]{:S(2)}) collective-permute-start(bf16[24,2048]{1,0:T(8,128)(2,1)S(1)} %get-tuple-element.52.refs_8_), channel_id=1, source_target_pairs={{0,2},{1,3},{2,0},{3,1},{4,6},{5,7},{6,4},{7,5},{8,10},{9,11},{10,... | collective-permute-start | bytes 294920 | tf_op jit(solution)/shard_map/ppermute | solution.py:27
  48.4 5.8 %collective-permute-start.24 = (bf16[24,2048]{1,0:T(8,128)(2,1)S(1)}, bf16[24,2048]{1,0:T(8,128)(2,1)S(1)}, u32[]{:S(2)}, u32[]{:S(2)}) collective-permute-start(bf16[24,2048]{1,0:T(8,128)(2,1)S(1)} %get-tuple-element.52.refs_8_), channel_id=1, source_target_pairs={{0,16},{1,17},{2,18},{3,19},{4,20},{5,21},{6,22},{7,23},{8,24},{9,... | collective-permute-start | bytes 294920 | tf_op jit(solution)/shard_map/ppermute | solution.py:27
  49.5 4.7 %collective-permute-start.22 = (bf16[24,2048]{1,0:T(8,128)(2,1)S(1)}, bf16[24,2048]{1,0:T(8,128)(2,1)S(1)}, u32[]{:S(2)}, u32[]{:S(2)}) collective-permute-start(bf16[24,2048]{1,0:T(8,128)(2,1)S(1)} %get-tuple-element.52.refs_8_), channel_id=1, source_target_pairs={{0,1},{1,0},{2,3},{3,2},{4,5},{5,4},{6,7},{7,6},{8,9},{9,8},{10,11... | collective-permute-start | bytes 294920 | tf_op jit(solution)/shard_map/ppermute | solution.py:27
  49.5 5.2 %collective-permute-start.19 = (bf16[24,2048]{1,0:T(8,128)(2,1)S(1)}, bf16[24,2048]{1,0:T(8,128)(2,1)S(1)}, u32[]{:S(2)}, u32[]{:S(2)}) collective-permute-start(bf16[24,2048]{1,0:T(8,128)(2,1)S(1)} %collective-permute-done.17.refs_4_), channel_id=1, source_target_pairs={{0,1},{1,0},{2,3},{3,2},{4,5},{5,4},{6,7},{7,6},{8,9},{9,8},{10,11... | collective-permute-start | bytes 294920 | tf_op jit(solution)/shard_map/ppermute | solution.py:27
  52.0 4.6 %collective-permute-start.18 = (bf16[24,2048]{1,0:T(8,128)(2,1)S(1)}, bf16[24,2048]{1,0:T(8,128)(2,1)S(1)}, u32[]{:S(2)}, u32[]{:S(2)}) collective-permute-start(bf16[24,2048]{1,0:T(8,128)(2,1)S(1)} %collective-permute-done.17.refs_4_), channel_id=1, source_target_pairs={{0,2},{1,3},{2,0},{3,1},{4,6},{5,7},{6,4},{7,5},{8,10},{9,11},{10,... | collective-permute-start | bytes 294920 | tf_op jit(solution)/shard_map/ppermute | solution.py:27
  53.7 4.6 %collective-permute-start.25 = (bf16[24,2048]{1,0:T(8,128)(2,1)S(1)}, bf16[24,2048]{1,0:T(8,128)(2,1)S(1)}, u32[]{:S(2)}, u32[]{:S(2)}) collective-permute-start(bf16[24,2048]{1,0:T(8,128)(2,1)S(1)} %collective-permute-done.21.refs_9_), channel_id=1, source_target_pairs={{0,16},{1,17},{2,18},{3,19},{4,20},{5,21},{6,22},{7,23},{8,24},{9,... | collective-permute-start | bytes 294920 | tf_op jit(solution)/shard_map/ppermute | solution.py:27
  54.2 5.0 %collective-permute-start.23 = (bf16[24,2048]{1,0:T(8,128)(2,1)S(1)}, bf16[24,2048]{1,0:T(8,128)(2,1)S(1)}, u32[]{:S(2)}, u32[]{:S(2)}) collective-permute-start(bf16[24,2048]{1,0:T(8,128)(2,1)S(1)} %collective-permute-done.21.refs_9_), channel_id=1, source_target_pairs={{0,1},{1,0},{2,3},{3,2},{4,5},{5,4},{6,7},{7,6},{8,9},{9,8},{10,11... | collective-permute-start | bytes 294920 | tf_op jit(solution)/shard_map/ppermute | solution.py:27
  54.2 5.0 %collective-permute-start.16 = (bf16[24,2048]{1,0:T(8,128)(2,1)S(1)}, bf16[24,2048]{1,0:T(8,128)(2,1)S(1)}, u32[]{:S(2)}, u32[]{:S(2)}) collective-permute-start(bf16[24,2048]{1,0:T(8,128)(2,1)S(1)} %collective-permute-done.14.refs_1_), channel_id=1, source_target_pairs={{0,1},{1,0},{2,3},{3,2},{4,5},{5,4},{6,7},{7,6},{8,9},{9,8},{10,11... | collective-permute-start | bytes 294920 | tf_op jit(solution)/shard_map/ppermute | solution.py:27
  54.7 4.5 %collective-permute-start.26 = (bf16[24,2048]{1,0:T(8,128)(2,1)S(1)}, bf16[24,2048]{1,0:T(8,128)(2,1)S(1)}, u32[]{:S(2)}, u32[]{:S(2)}) collective-permute-start(bf16[24,2048]{1,0:T(8,128)(2,1)S(1)} %collective-permute-done.24.refs_12_), channel_id=1, source_target_pairs={{0,1},{1,0},{2,3},{3,2},{4,5},{5,4},{6,7},{7,6},{8,9},{9,8},{10,11... | collective-permute-start | bytes 294920 | tf_op jit(solution)/shard_map/ppermute | solution.py:27
  56.7 2.6 %collective-permute-start.20 = (bf16[24,2048]{1,0:T(8,128)(2,1)S(1)}, bf16[24,2048]{1,0:T(8,128)(2,1)S(1)}, u32[]{:S(2)}, u32[]{:S(2)}) collective-permute-start(bf16[24,2048]{1,0:T(8,128)(2,1)S(1)} %collective-permute-done.18.refs_5_), channel_id=1, source_target_pairs={{0,1},{1,0},{2,3},{3,2},{4,5},{5,4},{6,7},{7,6},{8,9},{9,8},{10,11... | collective-permute-start | bytes 294920 | tf_op jit(solution)/shard_map/ppermute | solution.py:27
  58.3 1.3 %collective-permute-start.27 = (bf16[24,2048]{1,0:T(8,128)(2,1)S(1)}, bf16[24,2048]{1,0:T(8,128)(2,1)S(1)}, u32[]{:S(2)}, u32[]{:S(2)}) collective-permute-start(bf16[24,2048]{1,0:T(8,128)(2,1)S(1)} %collective-permute-done.25.refs_13_), channel_id=1, source_target_pairs={{0,1},{1,0},{2,3},{3,2},{4,5},{5,4},{6,7},{7,6},{8,9},{9,8},{10,11... | collective-permute-start | bytes 294920 | tf_op jit(solution)/shard_map/ppermute | solution.py:27
where the time goes:
time: 62.3 us; the launch traced here: 62 us
  starting transfers between devices  27.3 us (44%)
  waiting for transfers between devices  24.5 us (39%)
  Pallas kernels  9.4 us (15%)
  between operations  0.78 us (1%)
    ppermute x28, starting transfers between devices, across(): return lax.ppermute(value, ('group', 'dev'), pairs)  27.3 us
    ppermute x28, waiting for transfers between devices, across(): return lax.ppermute(value, ('group', 'dev'), pairs)  24.5 us
    pallas_call x12, Pallas kernels, local_call(): pl.pallas_call(kernel, out_shape=[jax.ShapeDtypeStruct(shape, kind) for s...  6.97 us
    pallas_call x1, Pallas kernels, grad_call(): pl.pallas_call(functools.partial(grad_kernel, scale, step, per), out_shap...  2.43 us
  transfers between devices with their start and end apart: 28, of which 16 were waited for; matrix products, arithmetic and copies ran while one was open for 0% of the time, Pallas kernels for 7%

commit v1 on v0

--- a/solution.py
+++ b/solution.py
@@ -125,7 +125,6 @@
 
 
 LANES = 128
-PARTS = (1, 1)
 MIB = 1 << 20
 IN_VMEM = pl.BlockSpec(memory_space=pltpu.VMEM)
 IN_SMEM = pl.BlockSpec(memory_space=pltpu.SMEM)
@@ -146,6 +145,10 @@
     )(*args)
 
 
+def path(core, side, far):
+    return (core ^ side ^ (far > 0)) | (side << 1) | (far << 2)
+
+
 def split_kernel(x_ref, near_ref, side_ref, core_ref, sems):
     far, _, part = near_ref.shape
     feat = lax.axis_index("dev")
@@ -154,7 +157,7 @@
         for n in range(2):
             for m in range(far):
                 out = core_ref.at[n, m] if c else (side_ref if n else near_ref).at[m]
-                first = pl.multiple_of((feat ^ (c | (n << 1) | (m << 2))) * part, part)
+                first = pl.multiple_of((feat ^ path(c, n, m)) * part, part)
                 copies.append(
                     pltpu.make_async_copy(x_ref.at[:, pl.ds(first, part)], out, sems.at[len(copies)])
                 )
@@ -220,7 +223,7 @@
     near, unit = sources[0].shape[0], sources[0].shape[1]
     for m, source in enumerate(sources):
         for k in range(near):
-            first = (m * near + k) * unit
+            first = path(k & 1, k >> 1, m) * unit
             slots[first : first + unit, :] = source[k].astype(jnp.float32)
     rows = jnp.dot(
         pick_ref[...], slots[...].astype(jnp.bfloat16), preferred_element_type=jnp.float32
@@ -241,67 +244,110 @@
 
 
 def halve_kernel(kept_ref, arrived_ref, leaving_ref, staying_ref):
-    half = staying_ref.shape[0]
-    staying_ref[...] = kept_ref[:half] + arrived_ref[:half].astype(jnp.float32)
-    leaving_ref[...] = (kept_ref[half:] + arrived_ref[half:].astype(jnp.float32)).astype(
+    half, width = staying_ref.shape
+    cols = slice(0, width)
+    staying_ref[...] = kept_ref[:half, cols] + arrived_ref[:half, cols].astype(jnp.float32)
+    leaving_ref[...] = (kept_ref[half:, cols] + arrived_ref[half:, cols].astype(jnp.float32)).astype(
         jnp.bfloat16
     )
+
+
+def unit_lines(kept_ref, arrived_ref, first, lines):
+    count = kept_ref.shape[0]
+    depth = lines.shape[0] // count
+    for t in range(depth):
+        cols = slice(first + t * LANES, first + (t + 1) * LANES)
+        total = kept_ref[:, cols] + arrived_ref[:, cols].astype(jnp.float32)
+        lines[pl.ds(t, count, stride=depth), :] = total
+
+
+def far_first_kernel(first, kept_ref, arrived_ref, own_ref, *refs):
+    leaving, lines = refs[:-1], refs[-1]
+    unit_lines(kept_ref, arrived_ref, first, lines)
+    size = own_ref.shape[0] // 2
+    for n in range(2):
+        for m, out in enumerate((own_ref, *leaving)):
+            start = (n * (len(leaving) + 1) + m) * size
+            out[n * size : (n + 1) * size, :] = lines[start : start + size].astype(out.dtype)
 
 
 def units_kernel(kept_ref, arrived_ref, own_ref, *refs):
     leaving, lines = refs[:-1], refs[-1]
-    count, width = kept_ref.shape
-    depth = width // LANES
+    unit_lines(kept_ref, arrived_ref, 0, lines)
     size = own_ref.shape[0]
-    for t in range(depth):
-        cols = slice(t * LANES, (t + 1) * LANES)
-        total = kept_ref[:, cols] + arrived_ref[:, cols].astype(jnp.float32)
-        lines[pl.ds(t, count, stride=depth), :] = total
-    own_ref[...] = lines[:size]
-    for m, out in enumerate(leaving):
-        out[...] = lines[(m + 1) * size : (m + 2) * size].astype(jnp.bfloat16)
-
-
-def slope_kernel(unit, own_ref, *refs):
-    arrived, (target_ref, slope_ref, grad_ref) = refs[:-3], refs[-3:]
+    for m, out in enumerate((own_ref, *leaving)):
+        out[...] = lines[m * size : (m + 1) * size].astype(out.dtype)
+
+
+def far_sum_kernel(*refs):
+    (own_ref, *arrived), (leaving_ref, staying_ref) = refs[:-2], refs[-2:]
+    size = staying_ref.shape[0]
     total = own_ref[...]
     for other in arrived:
         total = total + other[...].astype(jnp.float32)
-    total = total.reshape(unit, -1, LANES)
-    target = target_ref[...].astype(jnp.float32).reshape(unit, -1, LANES)
-
-    def row_sum(part):
-        return jnp.sum(jnp.sum(part, axis=1, keepdims=True), axis=2, keepdims=True)
-
-    squares, products = row_sum(total * total), row_sum(total * target)
+    staying_ref[...] = total[:size]
+    leaving_ref[...] = total[size:].astype(jnp.bfloat16)
+
+
+def target_kernel(rows_ref, out_ref):
+    count, width = rows_ref.shape
+    depth = width // LANES // 2
+    for t in range(2 * depth):
+        base = t // depth * count * depth + t % depth
+        tile = rows_ref[:, t * LANES : (t + 1) * LANES].astype(jnp.float32)
+        out_ref[pl.ds(base, count, stride=depth), :] = tile
+
+
+def slope_kernel(unit, *refs):
+    sums, (target_ref, slope_ref, grad_ref) = refs[:-3], refs[-3:]
+    size = sums[0].shape[0]
+    totals, targets = [], []
+    for half, parts in enumerate((sums[:-2], sums[-2:])):
+        total = parts[0][...]
+        for other in parts[1:]:
+            total = total + other[...].astype(jnp.float32)
+        totals.append(total.reshape(unit, -1, LANES))
+        targets.append(target_ref[half * size : (half + 1) * size].reshape(unit, -1, LANES))
+
+    def row_sum(parts):
+        lines = sum(jnp.sum(part, axis=1, keepdims=True) for part in parts)
+        return jnp.sum(lines, axis=2, keepdims=True)
+
+    squares = row_sum([total * total for total in totals])
+    products = row_sum([total * target for total, target in zip(totals, targets)])
     root_mean = jnp.sqrt(squares / DS + epsilon)
     inner_mean = (squares / (root_mean * root_mean) - products / root_mean) / DS
-    normed = total / root_mean
-    upstream = normed - target
-    value = (upstream - normed * inner_mean) / root_mean
-    slope_ref[...] = value.reshape(-1, LANES).astype(jnp.bfloat16)
-    grad_ref[...] = (target - normed).reshape(-1, LANES)
+    for half, (total, target) in enumerate(zip(totals, targets)):
+        rows = slice(half * size, (half + 1) * size)
+        normed = total / root_mean
+        upstream = normed - target
+        value = (upstream - normed * inner_mean) / root_mean
+        slope_ref[rows, :] = value.reshape(-1, LANES).astype(jnp.bfloat16)
+        grad_ref[rows, :] = (target - normed).reshape(-1, LANES)
 
 
 def rows_kernel(lines_ref, out_ref):
-    count = out_ref.shape[0]
-    depth = lines_ref.shape[0] // count
-    for t in range(depth):
-        cols = slice(t * LANES, (t + 1) * LANES)
-        out_ref[:, cols] = lines_ref[pl.ds(t, count, stride=depth), :].astype(jnp.bfloat16)
+    count, width = out_ref.shape
+    depth = width // LANES // 2
+    for t in range(2 * depth):
+        base = t // depth * count * depth + t % depth
+        tile = lines_ref[pl.ds(base, count, stride=depth), :]
+        out_ref[:, t * LANES : (t + 1) * LANES] = tile.astype(jnp.bfloat16)
 
 
 def line_kernel(units, *refs):
     sources, outs, lines = refs[:units], refs[units:-1], refs[-1]
-    size = sources[0].shape[0]
-    count = outs[0].shape[0]
-    depth = lines.shape[0] // count
+    size = sources[0].shape[0] // 2
+    count, width = outs[0].shape
+    depth = width // LANES
     for m, source in enumerate(sources):
-        lines[m * size : (m + 1) * size, :] = source[...].astype(jnp.float32)
-    places = [(out, t) for out in outs for t in range(out.shape[1] // LANES)]
-    for source, (out, t) in enumerate(places):
-        cols = slice(t * LANES, (t + 1) * LANES)
-        out[:, cols] = lines[pl.ds(source, count, stride=depth), :].astype(jnp.bfloat16)
+        for half in range(2):
+            rows = slice(m * size, (m + 1) * size)
+            lines[half, rows, :] = source[half * size : (half + 1) * size].astype(jnp.float32)
+    for half, out in enumerate(outs):
+        for t in range(depth):
+            tile = lines[half, pl.ds(t, count, stride=depth), :]
+            out[:, t * LANES : (t + 1) * LANES] = tile.astype(jnp.bfloat16)
 
 
 def turn_kernel(own_ref, other_ref, out_ref):
@@ -358,7 +404,7 @@
 def far_across(values):
     arrived = []
     for m in range(1, len(values)):
-        arrived.append(across(values[m], 0, m * NEAR))
+        arrived.append(across(values[m], 0, path(0, 0, m)))
     return arrived
 
 
@@ -367,12 +413,12 @@
     block_teacher, block_student = proj_tiles.shape
     near, far = NEAR, FEAT_SPLIT // NEAR
     half = FEAT_SPLIT * unit
-    cuts = [block_student * part // sum(PARTS) for part in PARTS]
-    depth = block_student // LANES
-    size = unit * depth
+    cut = block_student // 2
+    depth = cut // LANES
+    size = 2 * unit * depth
     bf16, f32 = jnp.bfloat16, jnp.float32
 
-    place = [c | (n << 1) | (m << 2) for c in range(2) for n in range(2) for m in range(far)]
+    place = [path(c, n, m) for c in range(2) for n in range(2) for m in range(far)]
 
     block = (unit, block_teacher)
     own_near, own_side, leaving = local_call(
@@ -384,7 +430,7 @@
     )
     core = across(leaving, 0, 1)
     (leaving,) = local_call(side_kernel, [((2, far, *block), bf16)], [own_side, core])
-    side = across(leaving, 0, 2)
+    side = across(leaving, 0, path(0, 1, 0))
     held = local_call(far_kernel, [((near, *block), bf16)] * far, [own_near, core, side])
     held = [held[0]] + far_across(held)
 
@@ -424,41 +470,52 @@
     )
 
     arrived = across(leaving, 0, 1)
+    small = size // 2
+    kept, swapped = staying, arrived
     leaving, staying = local_call(
-        halve_kernel,
-        [((half // 4, block_student), bf16), ((half // 4, block_student), f32)],
+        halve_kernel, [((half // 4, cut), bf16), ((half // 4, cut), f32)], [kept, swapped]
+    )
+    arrived = across(leaving, 0, path(0, 1, 0))
+    own, *leaving = local_call(
+        functools.partial(far_first_kernel, cut),
+        [((size, LANES), f32)] + [((size, LANES), bf16)] * (far - 1),
+        [kept, swapped],
+        scratch=[pltpu.VMEM((half // 2 * depth, LANES), f32)],
+    )
+    far_b = far_across([own, *leaving])
+    own_a, *leaving = local_call(
+        units_kernel,
+        [((small, LANES), f32)] + [((small, LANES), bf16)] * (far - 1),
         [staying, arrived],
-    )
-    states_too, leaving = lax.optimization_barrier((states, leaving))
-    arrived, other_states = lax.optimization_barrier(
-        (across(leaving, 0, 2), across(states_too, 1, 0))
-    )
-    own, *leaving = local_call(
-        units_kernel,
-        [((size, LANES), f32)] + [((size, LANES), bf16)] * (far - 1),
-        [staying, arrived],
-        scratch=[pltpu.VMEM((far * size, LANES), f32)],
-    )
-    arrived = far_across([None, *leaving])
+        scratch=[pltpu.VMEM((half // 4 * depth, LANES), f32)],
+    )
+    far_a = far_across([own_a, *leaving])
+    leaving, own_b = local_call(
+        far_sum_kernel, [((small, LANES), bf16), ((small, LANES), f32)], [own, *far_b]
+    )
+    near_b = across(leaving, 0, path(0, 1, 0))
+    (target,) = local_call(target_kernel, [((size, LANES), f32)], [student_tiles])
     slope, grad = local_call(
         functools.partial(slope_kernel, unit),
         [((size, LANES), bf16), ((size, LANES), f32)],
-        [own, *arrived, student_tiles.reshape(size, LANES)],
+        [own_a, *far_a, own_b, near_b, target],
     )
     (grad,) = local_call(rows_kernel, [((unit, block_student), bf16)], [grad])
+    states_too, _ = lax.optimization_barrier((states, slope))
+    other_states = across(states_too, 1, 0)
 
     line = [slope] + far_across([slope] * far)
     lines = local_call(
         functools.partial(line_kernel, far),
-        [((far * unit, cut), bf16) for cut in cuts],
+        [((far * unit, cut), bf16)] * 2,
         line,
-        scratch=[pltpu.VMEM((far * size, LANES), f32)],
+        scratch=[pltpu.VMEM((2, far * small, LANES), f32)],
     )
     scale = 1.0 / math.sqrt(lax.axis_size("group") * half)
     first, second = lines
-    first_group, second_near = across(first, 1, 0), across(second, 0, 2)
-    second_group, first_near = across(second, 1, 0), across(first, 0, 2)
-    first_both, second_both = across(first_group, 0, 2), across(second_near, 1, 0)
+    first_group, second_near = across(first, 1, 1), across(second, 0, 3)
+    second_group, first_near = across(second, 1, 1), across(first, 0, 3)
+    first_both, second_both = across(first_group, 0, 3), across(second_near, 1, 1)
     (turned,) = local_call(turn_kernel, [((block_teacher, 2 * half), bf16)], [states, other_states])
     pieces = []
     for own, other in (
@@ -466,7 +523,7 @@
         ((second, second_near), (second_group, second_both)),
     ):
         pieces += [*own, *[across(piece, 0, 1) for piece in own]]
-        pieces += [*other, *[across(piece, 0, 1) for piece in other]]
+        pieces += [*[across(piece, 0, 1) for piece in other], *other]
     grad_proj = grad_call(scale, turned, pieces, len(pieces) // 2, (block_teacher, block_student))
     return grad_proj, grad
 

time: 62.3 us -> 63.1 us (1.013)
  starting transfers between devices: 27.3 us -> 31.3 us
  waiting for transfers between devices: 24.5 us -> 21.5 us
    ppermute x28 -> x32, starting transfers between devices: 27.3 us -> 31.3 us  [across(): return lax.ppermute(value, ('group', 'dev'), pairs)]
    ppermute x28 -> x32, waiting for transfers between devices: 24.5 us -> 21.5 us  [across(): return lax.ppermute(value, ('group', 'dev'), pairs)]
    pallas_call x12 -> x15, Pallas kernels: 6.97 us -> 6.76 us  [local_call(): pl.pallas_call(kernel, out_shape=[jax.ShapeDtypeStruct(shape, kind) for s...]
  transfers between devices with their start and end apart: 28 -> 32, of which waited for: 16 -> 14; matrix products, arithmetic and copies ran while one was open for 0% -> 0% of each run, Pallas kernels for 7% -> 7%
where the time goes in v1:
time: 63.1 us; the launch traced here: 62.8 us
  starting transfers between devices  31.3 us (50%)
  waiting for transfers between devices  21.5 us (34%)
  Pallas kernels  9.19 us (15%)
  between operations  0.82 us (1%)
    ppermute x32, starting transfers between devices, across(): return lax.ppermute(value, ('group', 'dev'), pairs)  31.3 us
    ppermute x32, waiting for transfers between devices, across(): return lax.ppermute(value, ('group', 'dev'), pairs)  21.5 us
    pallas_call x15, Pallas kernels, local_call(): pl.pallas_call(kernel, out_shape=[jax.ShapeDtypeStruct(shape, kind) for s...  6.76 us
    pallas_call x1, Pallas kernels, grad_call(): pl.pallas_call(functools.partial(grad_kernel, scale, step, per), out_shap...  2.43 us
  transfers between devices with their start and end apart: 32, of which 14 were waited for; matrix products, arithmetic and copies ran while one was open for 0% of the time, Pallas kernels for 7%

profile of v1, /device:TPU:0, one launch (start us, length us, event | category | flops | bytes accessed | tf_op | source)
XLA Modules:
  0.0 62.8 jit_solution(12603549189907994679)
XLA Ops:
  0.6 1.0 %shard_map.60 = (bf16[4,6,512]{2,1,0:T(8,128)(2,1)S(1)}, bf16[4,6,512]{2,1,0:T(8,128)(2,1)S(1)}, bf16[2,4,6,512]{3,2,1,0:T(8,128)(2,1)S(1)}) custom-call(bf16[6,8192]{1,0:T(8,128)(2,1)} %x_ref.1), custom_call_target="tpu_custom_call" | custom-call | tf_op jit(solution)/shard_map/pallas_call | solution.py:136
  1.7 0.6 collective-permute-start
  2.2 0.9 %collective-permute-done.core_ref = bf16[2,4,6,512]{3,2,1,0:T(8,128)(2,1)S(1)} collective-permute-done((bf16[2,4,6,512]{3,2,1,0:T(8,128)(2,1)S(1)}, bf16[2,4,6,512]{3,2,1,0:T(8,128)(2,1)S(1)}, u32[]{:S(2)}, u32[]{:S(2)}) %collective-permute-start) | collective-permute-done | bytes 49184 | tf_op jit(solution)/shard_map/ppermute | solution.py:27
  3.1 2.6 %collective-permute-start.1 = (bf16[2,4,6,512]{3,2,1,0:T(8,128)(2,1)S(1)}, bf16[2,4,6,512]{3,2,1,0:T(8,128)(2,1)S(1)}, u32[]{:S(2)}, u32[]{:S(2)}) collective-permute-start(bf16[2,4,6,512]{3,2,1,0:T(8,128)(2,1)S(1)} %shard_map.61), channel_id=1, source_target_pairs={{0,3},{1,2},{2,1},{3,0},{4,7},{5,6},{6,5},{7,4},{8,11},{9,10},{10,... | collective-permute-start | bytes 147464 | tf_op jit(solution)/shard_map/ppermute | solution.py:27
  5.7 2.1 %collective-permute-done.1.side_ref = bf16[2,4,6,512]{3,2,1,0:T(8,128)(2,1)S(1)} collective-permute-done((bf16[2,4,6,512]{3,2,1,0:T(8,128)(2,1)S(1)}, bf16[2,4,6,512]{3,2,1,0:T(8,128)(2,1)S(1)}, u32[]{:S(2)}, u32[]{:S(2)}) %collective-permute-start.1) | collective-permute-done | bytes 49184 | tf_op jit(solution)/shard_map/ppermute | solution.py:27
  7.9 2.0 %collective-permute-start.2 = (bf16[4,6,512]{2,1,0:T(8,128)(2,1)S(1)}, bf16[4,6,512]{2,1,0:T(8,128)(2,1)S(1)}, u32[]{:S(2)}, u32[]{:S(2)}) collective-permute-start(bf16[4,6,512]{2,1,0:T(8,128)(2,1)S(1)} %get-tuple-element.36), channel_id=1, source_target_pairs={{0,5},{1,4},{2,7},{3,6},{4,1},{5,0},{6,3},{7,2},{8,13},{9,12},{10,... | collective-permute-start | bytes 73736 | tf_op jit(solution)/shard_map/ppermute | solution.py:27
  9.9 2.5 %collective-permute-start.3 = (bf16[4,6,512]{2,1,0:T(8,128)(2,1)S(1)}, bf16[4,6,512]{2,1,0:T(8,128)(2,1)S(1)}, u32[]{:S(2)}, u32[]{:S(2)}) collective-permute-start(bf16[4,6,512]{2,1,0:T(8,128)(2,1)S(1)} %get-tuple-element.37), channel_id=1, source_target_pairs={{0,9},{1,8},{2,11},{3,10},{4,13},{5,12},{6,15},{7,14},{8,1},{9,0},... | collective-permute-start | bytes 73736 | tf_op jit(solution)/shard_map/ppermute | solution.py:27
  12.5 1.6 %shard_map.63.refs_5_ = bf16[512,2048]{1,0:T(8,128)(2,1)S(1)} custom-call(bf16[512,4096]{1,0:T(8,128)(2,1)} %tiles_ref.3), custom_call_target="tpu_custom_call" | custom-call | flops 201326592 | bytes 2097152 | tf_op jit(solution)/shard_map/pallas_call | solution.py:136
  14.1 1.6 %shard_map.59 = (bf16[96,96]{1,0:T(8,128)(2,1)S(1)}, bf16[512,2048]{1,0:T(8,128)(2,1)S(1)}) custom-call(s32[2,16]{1,0:T(2,128)} %owner_ref.1, bf16[512,4096]{1,0:T(8,128)(2,1)} %tiles_ref.3), custom_call_target="tpu_custom_call" | custom-call | flops 201326592 | bytes 2097152 | tf_op jit(solution)/shard_map/pallas_call | solution.py:136
  15.7 1.9 %collective-permute-done.4.refs_3_ = bf16[4,6,512]{2,1,0:T(8,128)(2,1)S(1)} collective-permute-done((bf16[4,6,512]{2,1,0:T(8,128)(2,1)S(1)}, bf16[4,6,512]{2,1,0:T(8,128)(2,1)S(1)}, u32[]{:S(2)}, u32[]{:S(2)}) %collective-permute-start.4) | collective-permute-done | bytes 24608 | tf_op jit(solution)/shard_map/ppermute | solution.py:27
  17.6 0.9 %shard_map.64 = (bf16[96,512]{1,0:T(8,128)(2,1)S(1)}, bf16[48,4096]{1,0:T(8,128)(2,1)S(1)}, f32[48,4096]{1,0:T(8,128)S(1)}) custom-call(bf16[96,96]{1,0:T(8,128)(2,1)S(1)} %get-tuple-element.31.pick_ref, bf16[4,6,512]{2,1,0:T(8,128)(2,1)S(1)} %get-tuple-element.35.refs_0_, bf16[4,6,512]{2,1,0:T(8,128)(2,1)S(1)} %collective-permute-done.2.refs_1_, ...), custom_call_target="tpu_custom_call" | custom-call | flops 402653184 | tf_op jit(solution)/shard_map/pallas_call | solution.py:136
  18.6 0.2 collective-permute-start.5
  18.8 1.6 %collective-permute-done.5.arrived_ref = bf16[48,4096]{1,0:T(8,128)(2,1)S(1)} collective-permute-done((bf16[48,4096]{1,0:T(8,128)(2,1)S(1)}, bf16[48,4096]{1,0:T(8,128)(2,1)S(1)}, u32[]{:S(2)}, u32[]{:S(2)}) %collective-permute-start.5) | collective-permute-done | bytes 393248 | tf_op jit(solution)/shard_map/ppermute | solution.py:27
  20.4 1.3 %collective-permute-start.6 = (bf16[24,2048]{1,0:T(8,128)(2,1)S(1)}, bf16[24,2048]{1,0:T(8,128)(2,1)S(1)}, u32[]{:S(2)}, u32[]{:S(2)}) collective-permute-start(bf16[24,2048]{1,0:T(8,128)(2,1)S(1)} %get-tuple-element.44), channel_id=1, source_target_pairs={{0,3},{1,2},{2,1},{3,0},{4,7},{5,6},{6,5},{7,4},{8,11},{9,10},{10,... | collective-permute-start | bytes 294920 | tf_op jit(solution)/shard_map/ppermute | solution.py:27
  21.8 0.2 shard_map.67
  22.1 2.1 %collective-permute-start.11 = (bf16[192,128]{1,0:T(8,128)(2,1)S(1)}, bf16[192,128]{1,0:T(8,128)(2,1)S(1)}, u32[]{:S(2)}, u32[]{:S(2)}) collective-permute-start(bf16[192,128]{1,0:T(8,128)(2,1)S(1)} %get-tuple-element.51), channel_id=1, source_target_pairs={{0,9},{1,8},{2,11},{3,10},{4,13},{5,12},{6,15},{7,14},{8,1},{9,0},... | collective-permute-start | bytes 147464 | tf_op jit(solution)/shard_map/ppermute | solution.py:27
  24.2 1.9 %collective-permute-start.12 = (bf16[192,128]{1,0:T(8,128)(2,1)S(1)}, bf16[192,128]{1,0:T(8,128)(2,1)S(1)}, u32[]{:S(2)}, u32[]{:S(2)}) collective-permute-start(bf16[192,128]{1,0:T(8,128)(2,1)S(1)} %get-tuple-element.52), channel_id=1, source_target_pairs={{0,13},{1,12},{2,15},{3,14},{4,9},{5,8},{6,11},{7,10},{8,5},{9,4},... | collective-permute-start | bytes 147464 | tf_op jit(solution)/shard_map/ppermute | solution.py:27
  26.1 0.5 collective-permute-done.11.refs_2_
  26.6 3.2 %collective-permute-done.12.refs_3_ = bf16[192,128]{1,0:T(8,128)(2,1)S(1)} collective-permute-done((bf16[192,128]{1,0:T(8,128)(2,1)S(1)}, bf16[192,128]{1,0:T(8,128)(2,1)S(1)}, u32[]{:S(2)}, u32[]{:S(2)}) %collective-permute-start.12) | collective-permute-done | bytes 49184 | tf_op jit(solution)/shard_map/ppermute | solution.py:27
  29.8 0.3 collective-permute-start.13
  30.3 0.3 collective-permute-start.7
  30.5 2.1 %collective-permute-start.8 = (bf16[96,128]{1,0:T(8,128)(2,1)S(1)}, bf16[96,128]{1,0:T(8,128)(2,1)S(1)}, u32[]{:S(2)}, u32[]{:S(2)}) collective-permute-start(bf16[96,128]{1,0:T(8,128)(2,1)S(1)} %get-tuple-element.47), channel_id=1, source_target_pairs={{0,9},{1,8},{2,11},{3,10},{4,13},{5,12},{6,15},{7,14},{8,1},{9,0},... | collective-permute-start | bytes 73736 | tf_op jit(solution)/shard_map/ppermute | solution.py:27
  32.6 1.8 %collective-permute-start.9 = (bf16[96,128]{1,0:T(8,128)(2,1)S(1)}, bf16[96,128]{1,0:T(8,128)(2,1)S(1)}, u32[]{:S(2)}, u32[]{:S(2)}) collective-permute-start(bf16[96,128]{1,0:T(8,128)(2,1)S(1)} %get-tuple-element.48), channel_id=1, source_target_pairs={{0,13},{1,12},{2,15},{3,14},{4,9},{5,8},{6,11},{7,10},{8,5},{9,4},... | collective-permute-start | bytes 73736 | tf_op jit(solution)/shard_map/ppermute | solution.py:27
  34.4 0.2 collective-permute-done.8.refs_2_
  34.7 3.0 %collective-permute-done.9.refs_3_ = bf16[96,128]{1,0:T(8,128)(2,1)S(1)} collective-permute-done((bf16[96,128]{1,0:T(8,128)(2,1)S(1)}, bf16[96,128]{1,0:T(8,128)(2,1)S(1)}, u32[]{:S(2)}, u32[]{:S(2)}) %collective-permute-start.9) | collective-permute-done | bytes 24608 | tf_op jit(solution)/shard_map/ppermute | solution.py:27
  37.8 1.9 %collective-permute-start.17 = (bf16[192,128]{1,0:T(8,128)(2,1)S(1)}, bf16[192,128]{1,0:T(8,128)(2,1)S(1)}, u32[]{:S(2)}, u32[]{:S(2)}) collective-permute-start(bf16[192,128]{1,0:T(8,128)(2,1)S(1)} %get-tuple-element.55.refs_0_), channel_id=1, source_target_pairs={{0,13},{1,12},{2,15},{3,14},{4,9},{5,8},{6,11},{7,10},{8,5},{9,4},... | collective-permute-start | bytes 147464 | tf_op jit(solution)/shard_map/ppermute | solution.py:27
  39.6 2.1 %collective-permute-start.15 = (bf16[192,128]{1,0:T(8,128)(2,1)S(1)}, bf16[192,128]{1,0:T(8,128)(2,1)S(1)}, u32[]{:S(2)}, u32[]{:S(2)}) collective-permute-start(bf16[192,128]{1,0:T(8,128)(2,1)S(1)} %get-tuple-element.55.refs_0_), channel_id=1, source_target_pairs={{0,5},{1,4},{2,7},{3,6},{4,1},{5,0},{6,3},{7,2},{8,13},{9,12},{10,... | collective-permute-start | bytes 147464 | tf_op jit(solution)/shard_map/ppermute | solution.py:27
  41.7 1.5 %collective-permute-start.14 = (bf16[96,512]{1,0:T(8,128)(2,1)S(1)}, bf16[96,512]{1,0:T(8,128)(2,1)S(1)}, u32[]{:S(2)}, u32[]{:S(2)}) collective-permute-start(bf16[96,512]{1,0:T(8,128)(2,1)S(1)} %get-tuple-element.56.own_ref), channel_id=1, source_target_pairs={{0,16},{1,17},{2,18},{3,19},{4,20},{5,21},{6,22},{7,23},{8,24},{9,... | collective-permute-start | bytes 294920 | tf_op jit(solution)/shard_map/ppermute | solution.py:27
  43.4 2.4 %collective-permute-done.16.refs_2_ = bf16[192,128]{1,0:T(8,128)(2,1)S(1)} collective-permute-done((bf16[192,128]{1,0:T(8,128)(2,1)S(1)}, bf16[192,128]{1,0:T(8,128)(2,1)S(1)}, u32[]{:S(2)}, u32[]{:S(2)}) %collective-permute-start.16) | collective-permute-done | bytes 49184 | tf_op jit(solution)/shard_map/ppermute | solution.py:27
  45.9 1.3 %collective-permute-start.21 = (bf16[24,2048]{1,0:T(8,128)(2,1)S(1)}, bf16[24,2048]{1,0:T(8,128)(2,1)S(1)}, u32[]{:S(2)}, u32[]{:S(2)}) collective-permute-start(bf16[24,2048]{1,0:T(8,128)(2,1)S(1)} %get-tuple-element.57.refs_0_), channel_id=1, source_target_pairs={{0,17},{1,16},{2,19},{3,18},{4,21},{5,20},{6,23},{7,22},{8,25},{9,... | collective-permute-start | bytes 294920 | tf_op jit(solution)/shard_map/ppermute | solution.py:27
  47.2 0.4 collective-permute-start.19
  47.6 1.2 %collective-permute-start.18 = (bf16[24,2048]{1,0:T(8,128)(2,1)S(1)}, bf16[24,2048]{1,0:T(8,128)(2,1)S(1)}, u32[]{:S(2)}, u32[]{:S(2)}) collective-permute-start(bf16[24,2048]{1,0:T(8,128)(2,1)S(1)} %get-tuple-element.57.refs_0_), channel_id=1, source_target_pairs={{0,3},{1,2},{2,1},{3,0},{4,7},{5,6},{6,5},{7,4},{8,11},{9,10},{10,... | collective-permute-start | bytes 294920 | tf_op jit(solution)/shard_map/ppermute | solution.py:27
  48.8 0.5 collective-permute-start.25
  49.3 0.3 collective-permute-start.28
  49.6 1.2 %collective-permute-done.21.refs_6_ = bf16[24,2048]{1,0:T(8,128)(2,1)S(1)} collective-permute-done((bf16[24,2048]{1,0:T(8,128)(2,1)S(1)}, bf16[24,2048]{1,0:T(8,128)(2,1)S(1)}, u32[]{:S(2)}, u32[]{:S(2)}) %collective-permute-start.21) | collective-permute-done | bytes 98336 | tf_op jit(solution)/shard_map/ppermute | solution.py:27
  50.8 0.4 collective-permute-start.26
  51.2 1.2 %collective-permute-start.23 = (bf16[24,2048]{1,0:T(8,128)(2,1)S(1)}, bf16[24,2048]{1,0:T(8,128)(2,1)S(1)}, u32[]{:S(2)}, u32[]{:S(2)}) collective-permute-start(bf16[24,2048]{1,0:T(8,128)(2,1)S(1)} %collective-permute-done.21.refs_6_), channel_id=1, source_target_pairs={{0,3},{1,2},{2,1},{3,0},{4,7},{5,6},{6,5},{7,4},{8,11},{9,10},{10,... | collective-permute-start | bytes 294920 | tf_op jit(solution)/shard_map/ppermute | solution.py:27
  52.4 0.7 %collective-permute-start.22 = (bf16[24,2048]{1,0:T(8,128)(2,1)S(1)}, bf16[24,2048]{1,0:T(8,128)(2,1)S(1)}, u32[]{:S(2)}, u32[]{:S(2)}) collective-permute-start(bf16[24,2048]{1,0:T(8,128)(2,1)S(1)} %collective-permute-done.21.refs_6_), channel_id=1, source_target_pairs={{0,1},{1,0},{2,3},{3,2},{4,5},{5,4},{6,7},{7,6},{8,9},{9,8},{10,11... | collective-permute-start | bytes 294920 | tf_op jit(solution)/shard_map/ppermute | solution.py:27
  53.1 1.4 %collective-permute-done.25.refs_9_ = bf16[24,2048]{1,0:T(8,128)(2,1)S(1)} collective-permute-done((bf16[24,2048]{1,0:T(8,128)(2,1)S(1)}, bf16[24,2048]{1,0:T(8,128)(2,1)S(1)}, u32[]{:S(2)}, u32[]{:S(2)}) %collective-permute-start.25) | collective-permute-done | bytes 98336 | tf_op jit(solution)/shard_map/ppermute | solution.py:27
  54.5 0.3 collective-permute-start.30
  54.8 0.5 collective-permute-start.27
  55.3 1.3 %collective-permute-done.23.refs_7_ = bf16[24,2048]{1,0:T(8,128)(2,1)S(1)} collective-permute-done((bf16[24,2048]{1,0:T(8,128)(2,1)S(1)}, bf16[24,2048]{1,0:T(8,128)(2,1)S(1)}, u32[]{:S(2)}, u32[]{:S(2)}) %collective-permute-start.23) | collective-permute-done | bytes 98336 | tf_op jit(solution)/shard_map/ppermute | solution.py:27
  56.7 0.4 collective-permute-start.24
  57.1 1.6 %collective-permute-done.30.refs_15_ = bf16[24,2048]{1,0:T(8,128)(2,1)S(1)} collective-permute-done((bf16[24,2048]{1,0:T(8,128)(2,1)S(1)}, bf16[24,2048]{1,0:T(8,128)(2,1)S(1)}, u32[]{:S(2)}, u32[]{:S(2)}) %collective-permute-start.30) | collective-permute-done | bytes 98336 | tf_op jit(solution)/shard_map/ppermute | solution.py:27
  58.7 0.7 %collective-permute-start.31 = (bf16[24,2048]{1,0:T(8,128)(2,1)S(1)}, bf16[24,2048]{1,0:T(8,128)(2,1)S(1)}, u32[]{:S(2)}, u32[]{:S(2)}) collective-permute-start(bf16[24,2048]{1,0:T(8,128)(2,1)S(1)} %collective-permute-done.30.refs_15_), channel_id=1, source_target_pairs={{0,1},{1,0},{2,3},{3,2},{4,5},{5,4},{6,7},{7,6},{8,9},{9,8},{10,11... | collective-permute-start | bytes 294920 | tf_op jit(solution)/shard_map/ppermute | solution.py:27
  59.4 0.7 %shard_map.74 = bf16[6,4096]{1,0:T(8,128)(2,1)} custom-call(f32[192,128]{1,0:T(8,128)S(1)} %get-tuple-element.59.lines_ref), custom_call_target="tpu_custom_call" | custom-call | tf_op jit(solution)/shard_map/pallas_call | solution.py:136
  60.1 0.3 shard_map.71.states_ref
  60.4 2.4 %shard_map.73 = bf16[512,4096]{1,0:T(8,128)(2,1)} custom-call(bf16[512,192]{1,0:T(8,128)(2,1)S(1)} %shard_map.71.states_ref, bf16[24,2048]{1,0:T(8,128)(2,1)S(1)} %get-tuple-element.57.refs_0_, bf16[24,2048]{1,0:T(8,128)(2,1)S(1)} %collective-permute-done.18.refs_1_, bf16[24,2048]{1,0:T(8,128)(2,1)S(1)} %collective-permute-done.19.refs_2_, ...), custom_call_target="tpu_custom_call" | custom-call | flops 805306368 | bytes 4194304 | tf_op jit(solution)/shard_map/pallas_call | solution.py:385
  (34 shorter events, 1.0 us)
Async XLA Ops:
  1.7 1.5 %collective-permute-start = (bf16[2,4,6,512]{3,2,1,0:T(8,128)(2,1)S(1)}, bf16[2,4,6,512]{3,2,1,0:T(8,128)(2,1)S(1)}, u32[]{:S(2)}, u32[]{:S(2)}) collective-permute-start(bf16[2,4,6,512]{3,2,1,0:T(8,128)(2,1)S(1)} %get-tuple-element.33), channel_id=1, source_target_pairs={{0,1},{1,0},{2,3},{3,2},{4,5},{5,4},{6,7},{7,6},{8,9},{9,8},{10,11... | collective-permute-start | bytes 147464 | tf_op jit(solution)/shard_map/ppermute | solution.py:27
  3.1 4.8 %collective-permute-start.1 = (bf16[2,4,6,512]{3,2,1,0:T(8,128)(2,1)S(1)}, bf16[2,4,6,512]{3,2,1,0:T(8,128)(2,1)S(1)}, u32[]{:S(2)}, u32[]{:S(2)}) collective-permute-start(bf16[2,4,6,512]{3,2,1,0:T(8,128)(2,1)S(1)} %shard_map.61), channel_id=1, source_target_pairs={{0,3},{1,2},{2,1},{3,0},{4,7},{5,6},{6,5},{7,4},{8,11},{9,10},{10,... | collective-permute-start | bytes 147464 | tf_op jit(solution)/shard_map/ppermute | solution.py:27
  7.9 7.8 %collective-permute-start.2 = (bf16[4,6,512]{2,1,0:T(8,128)(2,1)S(1)}, bf16[4,6,512]{2,1,0:T(8,128)(2,1)S(1)}, u32[]{:S(2)}, u32[]{:S(2)}) collective-permute-start(bf16[4,6,512]{2,1,0:T(8,128)(2,1)S(1)} %get-tuple-element.36), channel_id=1, source_target_pairs={{0,5},{1,4},{2,7},{3,6},{4,1},{5,0},{6,3},{7,2},{8,13},{9,12},{10,... | collective-permute-start | bytes 73736 | tf_op jit(solution)/shard_map/ppermute | solution.py:27
  9.9 5.7 %collective-permute-start.3 = (bf16[4,6,512]{2,1,0:T(8,128)(2,1)S(1)}, bf16[4,6,512]{2,1,0:T(8,128)(2,1)S(1)}, u32[]{:S(2)}, u32[]{:S(2)}) collective-permute-start(bf16[4,6,512]{2,1,0:T(8,128)(2,1)S(1)} %get-tuple-element.37), channel_id=1, source_target_pairs={{0,9},{1,8},{2,11},{3,10},{4,13},{5,12},{6,15},{7,14},{8,1},{9,0},... | collective-permute-start | bytes 73736 | tf_op jit(solution)/shard_map/ppermute | solution.py:27
  12.5 5.1 %collective-permute-start.4 = (bf16[4,6,512]{2,1,0:T(8,128)(2,1)S(1)}, bf16[4,6,512]{2,1,0:T(8,128)(2,1)S(1)}, u32[]{:S(2)}, u32[]{:S(2)}) collective-permute-start(bf16[4,6,512]{2,1,0:T(8,128)(2,1)S(1)} %get-tuple-element.38), channel_id=1, source_target_pairs={{0,13},{1,12},{2,15},{3,14},{4,9},{5,8},{6,11},{7,10},{8,5},{9,4},... | collective-permute-start | bytes 73736 | tf_op jit(solution)/shard_map/ppermute | solution.py:27
  15.7 18.7 %copy-start = (bf16[6,4096]{1,0:T(8,128)(2,1)S(1)}, bf16[6,4096]{1,0:T(8,128)(2,1)}, u32[]{:S(2)}) copy-start(bf16[6,4096]{1,0:T(8,128)(2,1)} %rows_ref.1) | copy-start | bytes 147460
  18.6 1.8 %collective-permute-start.5 = (bf16[48,4096]{1,0:T(8,128)(2,1)S(1)}, bf16[48,4096]{1,0:T(8,128)(2,1)S(1)}, u32[]{:S(2)}, u32[]{:S(2)}) collective-permute-start(bf16[48,4096]{1,0:T(8,128)(2,1)S(1)} %get-tuple-element.42), channel_id=1, source_target_pairs={{0,1},{1,0},{2,3},{3,2},{4,5},{5,4},{6,7},{7,6},{8,9},{9,8},{10,11... | collective-permute-start | bytes 1179656 | tf_op jit(solution)/shard_map/ppermute | solution.py:27
  20.4 9.8 %collective-permute-start.6 = (bf16[24,2048]{1,0:T(8,128)(2,1)S(1)}, bf16[24,2048]{1,0:T(8,128)(2,1)S(1)}, u32[]{:S(2)}, u32[]{:S(2)}) collective-permute-start(bf16[24,2048]{1,0:T(8,128)(2,1)S(1)} %get-tuple-element.44), channel_id=1, source_target_pairs={{0,3},{1,2},{2,1},{3,0},{4,7},{5,6},{6,5},{7,4},{8,11},{9,10},{10,... | collective-permute-start | bytes 294920 | tf_op jit(solution)/shard_map/ppermute | solution.py:27
  22.0 4.1 %collective-permute-start.10 = (bf16[192,128]{1,0:T(8,128)(2,1)S(1)}, bf16[192,128]{1,0:T(8,128)(2,1)S(1)}, u32[]{:S(2)}, u32[]{:S(2)}) collective-permute-start(bf16[192,128]{1,0:T(8,128)(2,1)S(1)} %get-tuple-element.50), channel_id=1, source_target_pairs={{0,5},{1,4},{2,7},{3,6},{4,1},{5,0},{6,3},{7,2},{8,13},{9,12},{10,... | collective-permute-start | bytes 147464 | tf_op jit(solution)/shard_map/ppermute | solution.py:27
  22.1 4.6 %collective-permute-start.11 = (bf16[192,128]{1,0:T(8,128)(2,1)S(1)}, bf16[192,128]{1,0:T(8,128)(2,1)S(1)}, u32[]{:S(2)}, u32[]{:S(2)}) collective-permute-start(bf16[192,128]{1,0:T(8,128)(2,1)S(1)} %get-tuple-element.51), channel_id=1, source_target_pairs={{0,9},{1,8},{2,11},{3,10},{4,13},{5,12},{6,15},{7,14},{8,1},{9,0},... | collective-permute-start | bytes 147464 | tf_op jit(solution)/shard_map/ppermute | solution.py:27
  24.2 5.6 %collective-permute-start.12 = (bf16[192,128]{1,0:T(8,128)(2,1)S(1)}, bf16[192,128]{1,0:T(8,128)(2,1)S(1)}, u32[]{:S(2)}, u32[]{:S(2)}) collective-permute-start(bf16[192,128]{1,0:T(8,128)(2,1)S(1)} %get-tuple-element.52), channel_id=1, source_target_pairs={{0,13},{1,12},{2,15},{3,14},{4,9},{5,8},{6,11},{7,10},{8,5},{9,4},... | collective-permute-start | bytes 147464 | tf_op jit(solution)/shard_map/ppermute | solution.py:27
  29.8 4.6 %collective-permute-start.13 = (bf16[96,128]{1,0:T(8,128)(2,1)S(1)}, bf16[96,128]{1,0:T(8,128)(2,1)S(1)}, u32[]{:S(2)}, u32[]{:S(2)}) collective-permute-start(bf16[96,128]{1,0:T(8,128)(2,1)S(1)} %get-tuple-element.54), channel_id=1, source_target_pairs={{0,3},{1,2},{2,1},{3,0},{4,7},{5,6},{6,5},{7,4},{8,11},{9,10},{10,... | collective-permute-start | bytes 73736 | tf_op jit(solution)/shard_map/ppermute | solution.py:27
  30.3 4.2 %collective-permute-start.7 = (bf16[96,128]{1,0:T(8,128)(2,1)S(1)}, bf16[96,128]{1,0:T(8,128)(2,1)S(1)}, u32[]{:S(2)}, u32[]{:S(2)}) collective-permute-start(bf16[96,128]{1,0:T(8,128)(2,1)S(1)} %get-tuple-element.46), channel_id=1, source_target_pairs={{0,5},{1,4},{2,7},{3,6},{4,1},{5,0},{6,3},{7,2},{8,13},{9,12},{10,... | collective-permute-start | bytes 73736 | tf_op jit(solution)/shard_map/ppermute | solution.py:27
  30.5 4.2 %collective-permute-start.8 = (bf16[96,128]{1,0:T(8,128)(2,1)S(1)}, bf16[96,128]{1,0:T(8,128)(2,1)S(1)}, u32[]{:S(2)}, u32[]{:S(2)}) collective-permute-start(bf16[96,128]{1,0:T(8,128)(2,1)S(1)} %get-tuple-element.47), channel_id=1, source_target_pairs={{0,9},{1,8},{2,11},{3,10},{4,13},{5,12},{6,15},{7,14},{8,1},{9,0},... | collective-permute-start | bytes 73736 | tf_op jit(solution)/shard_map/ppermute | solution.py:27
  32.6 5.0 %collective-permute-start.9 = (bf16[96,128]{1,0:T(8,128)(2,1)S(1)}, bf16[96,128]{1,0:T(8,128)(2,1)S(1)}, u32[]{:S(2)}, u32[]{:S(2)}) collective-permute-start(bf16[96,128]{1,0:T(8,128)(2,1)S(1)} %get-tuple-element.48), channel_id=1, source_target_pairs={{0,13},{1,12},{2,15},{3,14},{4,9},{5,8},{6,11},{7,10},{8,5},{9,4},... | collective-permute-start | bytes 73736 | tf_op jit(solution)/shard_map/ppermute | solution.py:27
  37.8 5.6 %collective-permute-start.17 = (bf16[192,128]{1,0:T(8,128)(2,1)S(1)}, bf16[192,128]{1,0:T(8,128)(2,1)S(1)}, u32[]{:S(2)}, u32[]{:S(2)}) collective-permute-start(bf16[192,128]{1,0:T(8,128)(2,1)S(1)} %get-tuple-element.55.refs_0_), channel_id=1, source_target_pairs={{0,13},{1,12},{2,15},{3,14},{4,9},{5,8},{6,11},{7,10},{8,5},{9,4},... | collective-permute-start | bytes 147464 | tf_op jit(solution)/shard_map/ppermute | solution.py:27
  39.6 6.1 %collective-permute-start.16 = (bf16[192,128]{1,0:T(8,128)(2,1)S(1)}, bf16[192,128]{1,0:T(8,128)(2,1)S(1)}, u32[]{:S(2)}, u32[]{:S(2)}) collective-permute-start(bf16[192,128]{1,0:T(8,128)(2,1)S(1)} %get-tuple-element.55.refs_0_), channel_id=1, source_target_pairs={{0,9},{1,8},{2,11},{3,10},{4,13},{5,12},{6,15},{7,14},{8,1},{9,0},... | collective-permute-start | bytes 147464 | tf_op jit(solution)/shard_map/ppermute | solution.py:27
  39.6 6.1 %collective-permute-start.15 = (bf16[192,128]{1,0:T(8,128)(2,1)S(1)}, bf16[192,128]{1,0:T(8,128)(2,1)S(1)}, u32[]{:S(2)}, u32[]{:S(2)}) collective-permute-start(bf16[192,128]{1,0:T(8,128)(2,1)S(1)} %get-tuple-element.55.refs_0_), channel_id=1, source_target_pairs={{0,5},{1,4},{2,7},{3,6},{4,1},{5,0},{6,3},{7,2},{8,13},{9,12},{10,... | collective-permute-start | bytes 147464 | tf_op jit(solution)/shard_map/ppermute | solution.py:27
  41.7 7.6 %collective-permute-start.14 = (bf16[96,512]{1,0:T(8,128)(2,1)S(1)}, bf16[96,512]{1,0:T(8,128)(2,1)S(1)}, u32[]{:S(2)}, u32[]{:S(2)}) collective-permute-start(bf16[96,512]{1,0:T(8,128)(2,1)S(1)} %get-tuple-element.56.own_ref), channel_id=1, source_target_pairs={{0,16},{1,17},{2,18},{3,19},{4,20},{5,21},{6,22},{7,23},{8,24},{9,... | collective-permute-start | bytes 294920 | tf_op jit(solution)/shard_map/ppermute | solution.py:27
  45.9 4.9 %collective-permute-start.21 = (bf16[24,2048]{1,0:T(8,128)(2,1)S(1)}, bf16[24,2048]{1,0:T(8,128)(2,1)S(1)}, u32[]{:S(2)}, u32[]{:S(2)}) collective-permute-start(bf16[24,2048]{1,0:T(8,128)(2,1)S(1)} %get-tuple-element.57.refs_0_), channel_id=1, source_target_pairs={{0,17},{1,16},{2,19},{3,18},{4,21},{5,20},{6,23},{7,22},{8,25},{9,... | collective-permute-start | bytes 294920 | tf_op jit(solution)/shard_map/ppermute | solution.py:27
  47.2 4.0 %collective-permute-start.19 = (bf16[24,2048]{1,0:T(8,128)(2,1)S(1)}, bf16[24,2048]{1,0:T(8,128)(2,1)S(1)}, u32[]{:S(2)}, u32[]{:S(2)}) collective-permute-start(bf16[24,2048]{1,0:T(8,128)(2,1)S(1)} %get-tuple-element.57.refs_0_), channel_id=1, source_target_pairs={{0,1},{1,0},{2,3},{3,2},{4,5},{5,4},{6,7},{7,6},{8,9},{9,8},{10,11... | collective-permute-start | bytes 294920 | tf_op jit(solution)/shard_map/ppermute | solution.py:27
  47.6 4.8 %collective-permute-start.18 = (bf16[24,2048]{1,0:T(8,128)(2,1)S(1)}, bf16[24,2048]{1,0:T(8,128)(2,1)S(1)}, u32[]{:S(2)}, u32[]{:S(2)}) collective-permute-start(bf16[24,2048]{1,0:T(8,128)(2,1)S(1)} %get-tuple-element.57.refs_0_), channel_id=1, source_target_pairs={{0,3},{1,2},{2,1},{3,0},{4,7},{5,6},{6,5},{7,4},{8,11},{9,10},{10,... | collective-permute-start | bytes 294920 | tf_op jit(solution)/shard_map/ppermute | solution.py:27
  48.8 5.7 %collective-permute-start.25 = (bf16[24,2048]{1,0:T(8,128)(2,1)S(1)}, bf16[24,2048]{1,0:T(8,128)(2,1)S(1)}, u32[]{:S(2)}, u32[]{:S(2)}) collective-permute-start(bf16[24,2048]{1,0:T(8,128)(2,1)S(1)} %get-tuple-element.58.refs_8_), channel_id=1, source_target_pairs={{0,3},{1,2},{2,1},{3,0},{4,7},{5,6},{6,5},{7,4},{8,11},{9,10},{10,... | collective-permute-start | bytes 294920 | tf_op jit(solution)/shard_map/ppermute | solution.py:27
  49.3 5.4 %collective-permute-start.28 = (bf16[24,2048]{1,0:T(8,128)(2,1)S(1)}, bf16[24,2048]{1,0:T(8,128)(2,1)S(1)}, u32[]{:S(2)}, u32[]{:S(2)}) collective-permute-start(bf16[24,2048]{1,0:T(8,128)(2,1)S(1)} %get-tuple-element.58.refs_8_), channel_id=1, source_target_pairs={{0,17},{1,16},{2,19},{3,18},{4,21},{5,20},{6,23},{7,22},{8,25},{9,... | collective-permute-start | bytes 294920 | tf_op jit(solution)/shard_map/ppermute | solution.py:27
  50.8 4.4 %collective-permute-start.26 = (bf16[24,2048]{1,0:T(8,128)(2,1)S(1)}, bf16[24,2048]{1,0:T(8,128)(2,1)S(1)}, u32[]{:S(2)}, u32[]{:S(2)}) collective-permute-start(bf16[24,2048]{1,0:T(8,128)(2,1)S(1)} %get-tuple-element.58.refs_8_), channel_id=1, source_target_pairs={{0,1},{1,0},{2,3},{3,2},{4,5},{5,4},{6,7},{7,6},{8,9},{9,8},{10,11... | collective-permute-start | bytes 294920 | tf_op jit(solution)/shard_map/ppermute | solution.py:27
  51.2 5.4 %collective-permute-start.23 = (bf16[24,2048]{1,0:T(8,128)(2,1)S(1)}, bf16[24,2048]{1,0:T(8,128)(2,1)S(1)}, u32[]{:S(2)}, u32[]{:S(2)}) collective-permute-start(bf16[24,2048]{1,0:T(8,128)(2,1)S(1)} %collective-permute-done.21.refs_6_), channel_id=1, source_target_pairs={{0,3},{1,2},{2,1},{3,0},{4,7},{5,6},{6,5},{7,4},{8,11},{9,10},{10,... | collective-permute-start | bytes 294920 | tf_op jit(solution)/shard_map/ppermute | solution.py:27
  52.4 4.3 %collective-permute-start.22 = (bf16[24,2048]{1,0:T(8,128)(2,1)S(1)}, bf16[24,2048]{1,0:T(8,128)(2,1)S(1)}, u32[]{:S(2)}, u32[]{:S(2)}) collective-permute-start(bf16[24,2048]{1,0:T(8,128)(2,1)S(1)} %collective-permute-done.21.refs_6_), channel_id=1, source_target_pairs={{0,1},{1,0},{2,3},{3,2},{4,5},{5,4},{6,7},{7,6},{8,9},{9,8},{10,11... | collective-permute-start | bytes 294920 | tf_op jit(solution)/shard_map/ppermute | solution.py:27
  54.5 4.2 %collective-permute-start.30 = (bf16[24,2048]{1,0:T(8,128)(2,1)S(1)}, bf16[24,2048]{1,0:T(8,128)(2,1)S(1)}, u32[]{:S(2)}, u32[]{:S(2)}) collective-permute-start(bf16[24,2048]{1,0:T(8,128)(2,1)S(1)} %collective-permute-done.25.refs_9_), channel_id=1, source_target_pairs={{0,17},{1,16},{2,19},{3,18},{4,21},{5,20},{6,23},{7,22},{8,25},{9,... | collective-permute-start | bytes 294920 | tf_op jit(solution)/shard_map/ppermute | solution.py:27
  54.8 5.6 %collective-permute-start.27 = (bf16[24,2048]{1,0:T(8,128)(2,1)S(1)}, bf16[24,2048]{1,0:T(8,128)(2,1)S(1)}, u32[]{:S(2)}, u32[]{:S(2)}) collective-permute-start(bf16[24,2048]{1,0:T(8,128)(2,1)S(1)} %collective-permute-done.25.refs_9_), channel_id=1, source_target_pairs={{0,1},{1,0},{2,3},{3,2},{4,5},{5,4},{6,7},{7,6},{8,9},{9,8},{10,11... | collective-permute-start | bytes 294920 | tf_op jit(solution)/shard_map/ppermute | solution.py:27
  55.2 5.1 %collective-permute-start.20 = (bf16[24,2048]{1,0:T(8,128)(2,1)S(1)}, bf16[24,2048]{1,0:T(8,128)(2,1)S(1)}, u32[]{:S(2)}, u32[]{:S(2)}) collective-permute-start(bf16[24,2048]{1,0:T(8,128)(2,1)S(1)} %collective-permute-done.18.refs_1_), channel_id=1, source_target_pairs={{0,1},{1,0},{2,3},{3,2},{4,5},{5,4},{6,7},{7,6},{8,9},{9,8},{10,11... | collective-permute-start | bytes 294920 | tf_op jit(solution)/shard_map/ppermute | solution.py:27
  56.6 3.7 %collective-permute-start.29 = (bf16[24,2048]{1,0:T(8,128)(2,1)S(1)}, bf16[24,2048]{1,0:T(8,128)(2,1)S(1)}, u32[]{:S(2)}, u32[]{:S(2)}) collective-permute-start(bf16[24,2048]{1,0:T(8,128)(2,1)S(1)} %collective-permute-done.28.refs_14_), channel_id=1, source_target_pairs={{0,1},{1,0},{2,3},{3,2},{4,5},{5,4},{6,7},{7,6},{8,9},{9,8},{10,11... | collective-permute-start | bytes 294920 | tf_op jit(solution)/shard_map/ppermute | solution.py:27
  56.7 3.6 %collective-permute-start.24 = (bf16[24,2048]{1,0:T(8,128)(2,1)S(1)}, bf16[24,2048]{1,0:T(8,128)(2,1)S(1)}, u32[]{:S(2)}, u32[]{:S(2)}) collective-permute-start(bf16[24,2048]{1,0:T(8,128)(2,1)S(1)} %collective-permute-done.23.refs_7_), channel_id=1, source_target_pairs={{0,1},{1,0},{2,3},{3,2},{4,5},{5,4},{6,7},{7,6},{8,9},{9,8},{10,11... | collective-permute-start | bytes 294920 | tf_op jit(solution)/shard_map/ppermute | solution.py:27
  58.7 1.7 %collective-permute-start.31 = (bf16[24,2048]{1,0:T(8,128)(2,1)S(1)}, bf16[24,2048]{1,0:T(8,128)(2,1)S(1)}, u32[]{:S(2)}, u32[]{:S(2)}) collective-permute-start(bf16[24,2048]{1,0:T(8,128)(2,1)S(1)} %collective-permute-done.30.refs_15_), channel_id=1, source_target_pairs={{0,1},{1,0},{2,3},{3,2},{4,5},{5,4},{6,7},{7,6},{8,9},{9,8},{10,11... | collective-permute-start | bytes 294920 | tf_op jit(solution)/shard_map/ppermute | solution.py:27

commit v2 on v1

--- a/solution.py
+++ b/solution.py
@@ -149,35 +149,32 @@
     return (core ^ side ^ (far > 0)) | (side << 1) | (far << 2)
 
 
-def split_kernel(x_ref, near_ref, side_ref, core_ref, sems):
-    far, _, part = near_ref.shape
+def split_kernel(x_ref, *refs):
+    outs, sems = refs[:-1], refs[-1]
+    far, _, part = outs[0].shape
     feat = lax.axis_index("dev")
     copies = []
-    for c in range(2):
-        for n in range(2):
-            for m in range(far):
-                out = core_ref.at[n, m] if c else (side_ref if n else near_ref).at[m]
-                first = pl.multiple_of((feat ^ path(c, n, m)) * part, part)
-                copies.append(
-                    pltpu.make_async_copy(x_ref.at[:, pl.ds(first, part)], out, sems.at[len(copies)])
+    for s, out in enumerate(outs):
+        for m in range(far):
+            first = pl.multiple_of((feat ^ s ^ path(0, 0, m)) * part, part)
+            copies.append(
+                pltpu.make_async_copy(
+                    x_ref.at[:, pl.ds(first, part)], out.at[m], sems.at[len(copies)]
                 )
+            )
     for copy in copies:
         copy.start()
     for copy in copies:
         copy.wait()
 
 
-def side_kernel(side_ref, core_ref, out_ref):
-    out_ref[0] = side_ref[...]
-    out_ref[1] = core_ref[1]
-
-
-def far_kernel(near_ref, core_ref, side_ref, *outs):
+def far_kernel(near, *refs):
+    sources, outs, rows = refs[:near], refs[near:-1], refs[-1]
+    unit = sources[0].shape[1]
     for m, out in enumerate(outs):
-        out[0] = near_ref[m]
-        out[1] = core_ref[0, m]
-        out[2] = side_ref[0, m]
-        out[3] = side_ref[1, m]
+        for s, source in enumerate(sources):
+            rows[m, s * unit : (s + 1) * unit, :] = source[m].astype(jnp.float32)
+        out[...] = rows[m].astype(jnp.bfloat16)
 
 
 def fetch(tiles_ref, out_ref, sems, first):
@@ -206,6 +203,7 @@
     order.wait()
     for p, shift in enumerate(place):
         slot = owner_here[group, feat ^ shift] ^ feat
+        slot = slot ^ jnp.where(slot >= NEAR, 1, 0)
         wanted = jnp.where(row // unit == p, row + (slot - p) * unit, wanted)
     pick_ref[...] = jnp.where(source == wanted, 1.0, 0.0).astype(jnp.bfloat16)
     for copy in copies:
@@ -217,30 +215,28 @@
         copy.wait()
 
 
+def product(lhs, tiles_ref, leaving_ref, staying_ref):
+    half, width = staying_ref.shape
+    step = min(width, 512)
+    for start in range(0, width, step):
+        cols = slice(start, start + step)
+        part = jnp.dot(lhs, tiles_ref[:, cols], preferred_element_type=jnp.float32)
+        staying_ref[:, cols] = part[:half]
+        leaving_ref[:, cols] = part[half:].astype(jnp.bfloat16)
+
+
 def order_kernel(pick_ref, *refs):
-    sources, (first_ref, second_ref) = refs[:-6], refs[-6:-4]
-    lhs_ref, leaving_ref, staying_ref, slots = refs[-4:]
-    near, unit = sources[0].shape[0], sources[0].shape[1]
+    sources, (tiles_ref, lhs_ref, leaving_ref, staying_ref, slots) = refs[:-5], refs[-5:]
+    count = sources[0].shape[0]
     for m, source in enumerate(sources):
-        for k in range(near):
-            first = path(k & 1, k >> 1, m) * unit
-            slots[first : first + unit, :] = source[k].astype(jnp.float32)
-    rows = jnp.dot(
-        pick_ref[...], slots[...].astype(jnp.bfloat16), preferred_element_type=jnp.float32
-    )
-    lhs = rows.astype(jnp.bfloat16)
+        slots[m * count : (m + 1) * count, :] = source[...]
+    lhs = jnp.dot(pick_ref[...], slots[...], preferred_element_type=jnp.float32).astype(jnp.bfloat16)
     lhs_ref[...] = lhs
-    half, base = staying_ref.shape[0], 0
-    for tiles_ref in (first_ref, second_ref):
-        width = tiles_ref.shape[1]
-        step = min(width, 512)
-        for start in range(0, width, step):
-            tiles = tiles_ref[:, start : start + step]
-            part = jnp.dot(lhs, tiles, preferred_element_type=jnp.float32)
-            cols = slice(base + start, base + start + step)
-            staying_ref[:, cols] = part[:half]
-            leaving_ref[:, cols] = part[half:].astype(jnp.bfloat16)
-        base += width
+    product(lhs, tiles_ref, leaving_ref, staying_ref)
+
+
+def rest_kernel(lhs_ref, tiles_ref, leaving_ref, staying_ref):
+    product(lhs_ref[...], tiles_ref, leaving_ref, staying_ref)
 
 
 def halve_kernel(kept_ref, arrived_ref, leaving_ref, staying_ref):
@@ -252,18 +248,18 @@
     )
 
 
-def unit_lines(kept_ref, arrived_ref, first, lines):
+def unit_lines(kept_ref, arrived_ref, lines):
     count = kept_ref.shape[0]
     depth = lines.shape[0] // count
     for t in range(depth):
-        cols = slice(first + t * LANES, first + (t + 1) * LANES)
+        cols = slice(t * LANES, (t + 1) * LANES)
         total = kept_ref[:, cols] + arrived_ref[:, cols].astype(jnp.float32)
         lines[pl.ds(t, count, stride=depth), :] = total
 
 
-def far_first_kernel(first, kept_ref, arrived_ref, own_ref, *refs):
+def far_first_kernel(kept_ref, arrived_ref, own_ref, *refs):
     leaving, lines = refs[:-1], refs[-1]
-    unit_lines(kept_ref, arrived_ref, first, lines)
+    unit_lines(kept_ref, arrived_ref, lines)
     size = own_ref.shape[0] // 2
     for n in range(2):
         for m, out in enumerate((own_ref, *leaving)):
@@ -273,7 +269,7 @@
 
 def units_kernel(kept_ref, arrived_ref, own_ref, *refs):
     leaving, lines = refs[:-1], refs[-1]
-    unit_lines(kept_ref, arrived_ref, 0, lines)
+    unit_lines(kept_ref, arrived_ref, lines)
     size = own_ref.shape[0]
     for m, out in enumerate((own_ref, *leaving)):
         out[...] = lines[m * size : (m + 1) * size].astype(out.dtype)
@@ -379,7 +375,7 @@
         copy.wait()
 
 
-def grad_call(scale, states, slopes, per, shape, step=256):
+def grad_call(scale, states, slopes, per, shape, step=512):
     block_teacher, rows = states.shape
     count = shape[1] // step
     return pl.pallas_call(
@@ -421,17 +417,22 @@
     place = [path(c, n, m) for c in range(2) for n in range(2) for m in range(far)]
 
     block = (unit, block_teacher)
-    own_near, own_side, leaving = local_call(
+    packed = local_call(
         split_kernel,
-        [((far, *block), bf16), ((far, *block), bf16), ((2, far, *block), bf16)],
+        [((far, *block), bf16)] * near,
         [pltpu.with_memory_space_constraint(teacher, pltpu.HBM)],
         specs=[IN_HBM],
         scratch=[pltpu.SemaphoreType.DMA((FEAT_SPLIT,))],
     )
-    core = across(leaving, 0, 1)
-    (leaving,) = local_call(side_kernel, [((2, far, *block), bf16)], [own_side, core])
-    side = across(leaving, 0, path(0, 1, 0))
-    held = local_call(far_kernel, [((near, *block), bf16)] * far, [own_near, core, side])
+    slots = [packed[0]]
+    for k in range(1, near):
+        slots.append(across(packed[k], 0, k))
+    held = local_call(
+        functools.partial(far_kernel, near),
+        [((near * unit, block_teacher), bf16)] * far,
+        slots,
+        scratch=[pltpu.VMEM((far, near * unit, block_teacher), f32)],
+    )
     held = [held[0]] + far_across(held)
 
     tiles = pltpu.with_memory_space_constraint(proj_tiles, pltpu.HBM)
@@ -457,29 +458,26 @@
         scratch=[pltpu.SemaphoreType.DMA((8,))],
         **work,
     )
-    states, leaving, staying = local_call(
+    halves = [((half // 2, cut), bf16), ((half // 2, cut), f32)]
+    states, leaving, kept = local_call(
         order_kernel,
-        [
-            ((half, block_teacher), bf16),
-            ((half // 2, block_student), bf16),
-            ((half // 2, block_student), f32),
-        ],
-        [pick, *held, first_tiles, second_tiles],
-        scratch=[pltpu.VMEM((half, block_teacher), f32)],
-        flops=2 * half * block_teacher * block_student,
-    )
-
-    arrived = across(leaving, 0, 1)
+        [((half, block_teacher), bf16), *halves],
+        [pick, *held, first_tiles],
+        scratch=[pltpu.VMEM((half, block_teacher), bf16)],
+        **work,
+    )
+    swapped = across(leaving, 0, 1)
+    leaving, kept_b = local_call(rest_kernel, halves, [states, second_tiles], **work)
+    swapped_b = across(leaving, 0, 1)
     small = size // 2
-    kept, swapped = staying, arrived
     leaving, staying = local_call(
         halve_kernel, [((half // 4, cut), bf16), ((half // 4, cut), f32)], [kept, swapped]
     )
     arrived = across(leaving, 0, path(0, 1, 0))
     own, *leaving = local_call(
-        functools.partial(far_first_kernel, cut),
+        far_first_kernel,
         [((size, LANES), f32)] + [((size, LANES), bf16)] * (far - 1),
-        [kept, swapped],
+        [kept_b, swapped_b],
         scratch=[pltpu.VMEM((half // 2 * depth, LANES), f32)],
     )
     far_b = far_across([own, *leaving])

time: 63.1 us -> 63.1 us (level)
  starting transfers between devices: 31.3 us -> 30.5 us
  waiting for transfers between devices: 21.5 us -> 22.3 us
    ppermute x32 -> x34, starting transfers between devices: 31.3 us -> 30.5 us  [across(): return lax.ppermute(value, ('group', 'dev'), pairs)]
    ppermute x32 -> x34, waiting for transfers between devices: 21.5 us -> 22.3 us  [across(): return lax.ppermute(value, ('group', 'dev'), pairs)]
  transfers between devices with their start and end apart: 32 -> 34, of which waited for: 14 -> 16; matrix products, arithmetic and copies ran while one was open for 0% -> 0% of each run, Pallas kernels for 7% -> 8%
where the time goes in v2:
time: 63.1 us; the launch traced here: 62.8 us
  starting transfers between devices  30.5 us (48%)
  waiting for transfers between devices  22.3 us (35%)
  Pallas kernels  9.23 us (15%)
  between operations  0.81 us (1%)
    ppermute x34, starting transfers between devices, across(): return lax.ppermute(value, ('group', 'dev'), pairs)  30.5 us
    ppermute x34, waiting for transfers between devices, across(): return lax.ppermute(value, ('group', 'dev'), pairs)  22.3 us
    pallas_call x15, Pallas kernels, local_call(): pl.pallas_call(kernel, out_shape=[jax.ShapeDtypeStruct(shape, kind) for s...  6.86 us
    pallas_call x1, Pallas kernels, grad_call(): pl.pallas_call(functools.partial(grad_kernel, scale, step, per), out_shap...  2.37 us
  transfers between devices with their start and end apart: 34, of which 16 were waited for; matrix products, arithmetic and copies ran while one was open for 0% of the time, Pallas kernels for 8%

profile of v2, /device:TPU:0, one launch (start us, length us, event | category | flops | bytes accessed | tf_op | source)
XLA Modules:
  0.0 62.8 jit_solution(17919733607203773785)
XLA Ops:
  0.6 1.0 %shard_map.60 = (bf16[4,6,512]{2,1,0:T(8,128)(2,1)S(1)}, bf16[4,6,512]{2,1,0:T(8,128)(2,1)S(1)}, bf16[4,6,512]{2,1,0:T(8,128)(2,1)S(1)}, bf16[4,6,512]{2,1,0:T(8,128)(2,1)S(1)}) custom-call(bf16[6,8192]{1,0:T(8,128)(2,1)} %x_ref.1), custom_call_target="tpu_custom_call" | custom-call | tf_op jit(solution)/shard_map/pallas_call | solution.py:136
  1.7 0.6 collective-permute-start
  2.2 2.6 %collective-permute-start.1 = (bf16[4,6,512]{2,1,0:T(8,128)(2,1)S(1)}, bf16[4,6,512]{2,1,0:T(8,128)(2,1)S(1)}, u32[]{:S(2)}, u32[]{:S(2)}) collective-permute-start(bf16[4,6,512]{2,1,0:T(8,128)(2,1)S(1)} %get-tuple-element.37), channel_id=1, source_target_pairs={{0,2},{1,3},{2,0},{3,1},{4,6},{5,7},{6,4},{7,5},{8,10},{9,11},{10,... | collective-permute-start | bytes 73736 | tf_op jit(solution)/shard_map/ppermute | solution.py:27
  4.8 1.9 %collective-permute-done.1.refs_2_ = bf16[4,6,512]{2,1,0:T(8,128)(2,1)S(1)} collective-permute-done((bf16[4,6,512]{2,1,0:T(8,128)(2,1)S(1)}, bf16[4,6,512]{2,1,0:T(8,128)(2,1)S(1)}, u32[]{:S(2)}, u32[]{:S(2)}) %collective-permute-start.1) | collective-permute-done | bytes 24608 | tf_op jit(solution)/shard_map/ppermute | solution.py:27
  6.8 1.4 %collective-permute-done.2.refs_3_ = bf16[4,6,512]{2,1,0:T(8,128)(2,1)S(1)} collective-permute-done((bf16[4,6,512]{2,1,0:T(8,128)(2,1)S(1)}, bf16[4,6,512]{2,1,0:T(8,128)(2,1)S(1)}, u32[]{:S(2)}, u32[]{:S(2)}) %collective-permute-start.2) | collective-permute-done | bytes 24608 | tf_op jit(solution)/shard_map/ppermute | solution.py:27
  8.2 1.4 %collective-permute-start.3 = (bf16[24,512]{1,0:T(8,128)(2,1)S(1)}, bf16[24,512]{1,0:T(8,128)(2,1)S(1)}, u32[]{:S(2)}, u32[]{:S(2)}) collective-permute-start(bf16[24,512]{1,0:T(8,128)(2,1)S(1)} %get-tuple-element.40), channel_id=1, source_target_pairs={{0,5},{1,4},{2,7},{3,6},{4,1},{5,0},{6,3},{7,2},{8,13},{9,12},{10,... | collective-permute-start | bytes 73736 | tf_op jit(solution)/shard_map/ppermute | solution.py:27
  9.6 2.5 %collective-permute-start.4 = (bf16[24,512]{1,0:T(8,128)(2,1)S(1)}, bf16[24,512]{1,0:T(8,128)(2,1)S(1)}, u32[]{:S(2)}, u32[]{:S(2)}) collective-permute-start(bf16[24,512]{1,0:T(8,128)(2,1)S(1)} %get-tuple-element.41), channel_id=1, source_target_pairs={{0,9},{1,8},{2,11},{3,10},{4,13},{5,12},{6,15},{7,14},{8,1},{9,0},... | collective-permute-start | bytes 73736 | tf_op jit(solution)/shard_map/ppermute | solution.py:27
  12.1 1.6 %shard_map.59 = (bf16[96,96]{1,0:T(8,128)(2,1)S(1)}, bf16[512,2048]{1,0:T(8,128)(2,1)S(1)}) custom-call(s32[2,16]{1,0:T(2,128)} %owner_ref.1, bf16[512,4096]{1,0:T(8,128)(2,1)} %tiles_ref.3), custom_call_target="tpu_custom_call" | custom-call | flops 201326592 | bytes 2097152 | tf_op jit(solution)/shard_map/pallas_call | solution.py:136
  13.7 0.3 collective-permute-done.4.refs_2_
  14.0 3.2 %collective-permute-done.5.refs_3_ = bf16[24,512]{1,0:T(8,128)(2,1)S(1)} collective-permute-done((bf16[24,512]{1,0:T(8,128)(2,1)S(1)}, bf16[24,512]{1,0:T(8,128)(2,1)S(1)}, u32[]{:S(2)}, u32[]{:S(2)}) %collective-permute-start.5) | collective-permute-done | bytes 24608 | tf_op jit(solution)/shard_map/ppermute | solution.py:27
  17.2 0.6 shard_map.62
  18.0 1.6 %shard_map.65.tiles_ref = bf16[512,2048]{1,0:T(8,128)(2,1)S(1)} custom-call(bf16[512,4096]{1,0:T(8,128)(2,1)} %tiles_ref.3), custom_call_target="tpu_custom_call" | custom-call | flops 201326592 | bytes 2097152 | tf_op jit(solution)/shard_map/pallas_call | solution.py:136
  19.6 0.5 shard_map.66
  20.1 0.4 collective-permute-start.11
  20.5 0.7 %collective-permute-start.7 = (bf16[24,2048]{1,0:T(8,128)(2,1)S(1)}, bf16[24,2048]{1,0:T(8,128)(2,1)S(1)}, u32[]{:S(2)}, u32[]{:S(2)}) collective-permute-start(bf16[24,2048]{1,0:T(8,128)(2,1)S(1)} %get-tuple-element.48), channel_id=1, source_target_pairs={{0,3},{1,2},{2,1},{3,0},{4,7},{5,6},{6,5},{7,4},{8,11},{9,10},{10,... | collective-permute-start | bytes 294920 | tf_op jit(solution)/shard_map/ppermute | solution.py:27
  21.2 0.4 collective-permute-done.11.arrived_ref
  21.9 0.9 %collective-permute-start.13 = (bf16[192,128]{1,0:T(8,128)(2,1)S(1)}, bf16[192,128]{1,0:T(8,128)(2,1)S(1)}, u32[]{:S(2)}, u32[]{:S(2)}) collective-permute-start(bf16[192,128]{1,0:T(8,128)(2,1)S(1)} %get-tuple-element.57), channel_id=1, source_target_pairs={{0,9},{1,8},{2,11},{3,10},{4,13},{5,12},{6,15},{7,14},{8,1},{9,0},... | collective-permute-start | bytes 147464 | tf_op jit(solution)/shard_map/ppermute | solution.py:27
  22.7 3.2 %collective-permute-start.14 = (bf16[192,128]{1,0:T(8,128)(2,1)S(1)}, bf16[192,128]{1,0:T(8,128)(2,1)S(1)}, u32[]{:S(2)}, u32[]{:S(2)}) collective-permute-start(bf16[192,128]{1,0:T(8,128)(2,1)S(1)} %get-tuple-element.58), channel_id=1, source_target_pairs={{0,13},{1,12},{2,15},{3,14},{4,9},{5,8},{6,11},{7,10},{8,5},{9,4},... | collective-permute-start | bytes 147464 | tf_op jit(solution)/shard_map/ppermute | solution.py:27
  25.9 0.5 collective-permute-done.13.refs_2_
  26.4 2.6 %collective-permute-done.14.refs_3_ = bf16[192,128]{1,0:T(8,128)(2,1)S(1)} collective-permute-done((bf16[192,128]{1,0:T(8,128)(2,1)S(1)}, bf16[192,128]{1,0:T(8,128)(2,1)S(1)}, u32[]{:S(2)}, u32[]{:S(2)}) %collective-permute-start.14) | collective-permute-done | bytes 49184 | tf_op jit(solution)/shard_map/ppermute | solution.py:27
  29.1 0.8 %collective-permute-start.15 = (bf16[96,128]{1,0:T(8,128)(2,1)S(1)}, bf16[96,128]{1,0:T(8,128)(2,1)S(1)}, u32[]{:S(2)}, u32[]{:S(2)}) collective-permute-start(bf16[96,128]{1,0:T(8,128)(2,1)S(1)} %get-tuple-element.60), channel_id=1, source_target_pairs={{0,3},{1,2},{2,1},{3,0},{4,7},{5,6},{6,5},{7,4},{8,11},{9,10},{10,... | collective-permute-start | bytes 73736 | tf_op jit(solution)/shard_map/ppermute | solution.py:27
  30.0 0.9 %collective-permute-start.8 = (bf16[96,128]{1,0:T(8,128)(2,1)S(1)}, bf16[96,128]{1,0:T(8,128)(2,1)S(1)}, u32[]{:S(2)}, u32[]{:S(2)}) collective-permute-start(bf16[96,128]{1,0:T(8,128)(2,1)S(1)} %get-tuple-element.50), channel_id=1, source_target_pairs={{0,5},{1,4},{2,7},{3,6},{4,1},{5,0},{6,3},{7,2},{8,13},{9,12},{10,... | collective-permute-start | bytes 73736 | tf_op jit(solution)/shard_map/ppermute | solution.py:27
  30.9 1.7 %collective-permute-start.9 = (bf16[96,128]{1,0:T(8,128)(2,1)S(1)}, bf16[96,128]{1,0:T(8,128)(2,1)S(1)}, u32[]{:S(2)}, u32[]{:S(2)}) collective-permute-start(bf16[96,128]{1,0:T(8,128)(2,1)S(1)} %get-tuple-element.51), channel_id=1, source_target_pairs={{0,9},{1,8},{2,11},{3,10},{4,13},{5,12},{6,15},{7,14},{8,1},{9,0},... | collective-permute-start | bytes 73736 | tf_op jit(solution)/shard_map/ppermute | solution.py:27
  32.6 1.3 %collective-permute-start.10 = (bf16[96,128]{1,0:T(8,128)(2,1)S(1)}, bf16[96,128]{1,0:T(8,128)(2,1)S(1)}, u32[]{:S(2)}, u32[]{:S(2)}) collective-permute-start(bf16[96,128]{1,0:T(8,128)(2,1)S(1)} %get-tuple-element.52), channel_id=1, source_target_pairs={{0,13},{1,12},{2,15},{3,14},{4,9},{5,8},{6,11},{7,10},{8,5},{9,4},... | collective-permute-start | bytes 73736 | tf_op jit(solution)/shard_map/ppermute | solution.py:27
  34.0 1.0 %collective-permute-done.9.refs_2_ = bf16[96,128]{1,0:T(8,128)(2,1)S(1)} collective-permute-done((bf16[96,128]{1,0:T(8,128)(2,1)S(1)}, bf16[96,128]{1,0:T(8,128)(2,1)S(1)}, u32[]{:S(2)}, u32[]{:S(2)}) %collective-permute-start.9) | collective-permute-done | bytes 24608 | tf_op jit(solution)/shard_map/ppermute | solution.py:27
  35.1 2.6 %collective-permute-done.10.refs_3_ = bf16[96,128]{1,0:T(8,128)(2,1)S(1)} collective-permute-done((bf16[96,128]{1,0:T(8,128)(2,1)S(1)}, bf16[96,128]{1,0:T(8,128)(2,1)S(1)}, u32[]{:S(2)}, u32[]{:S(2)}) %collective-permute-start.10) | collective-permute-done | bytes 24608 | tf_op jit(solution)/shard_map/ppermute | solution.py:27
  37.8 1.4 %collective-permute-start.19 = (bf16[192,128]{1,0:T(8,128)(2,1)S(1)}, bf16[192,128]{1,0:T(8,128)(2,1)S(1)}, u32[]{:S(2)}, u32[]{:S(2)}) collective-permute-start(bf16[192,128]{1,0:T(8,128)(2,1)S(1)} %get-tuple-element.61.refs_0_), channel_id=1, source_target_pairs={{0,13},{1,12},{2,15},{3,14},{4,9},{5,8},{6,11},{7,10},{8,5},{9,4},... | collective-permute-start | bytes 147464 | tf_op jit(solution)/shard_map/ppermute | solution.py:27
  39.2 2.5 %collective-permute-start.17 = (bf16[192,128]{1,0:T(8,128)(2,1)S(1)}, bf16[192,128]{1,0:T(8,128)(2,1)S(1)}, u32[]{:S(2)}, u32[]{:S(2)}) collective-permute-start(bf16[192,128]{1,0:T(8,128)(2,1)S(1)} %get-tuple-element.61.refs_0_), channel_id=1, source_target_pairs={{0,5},{1,4},{2,7},{3,6},{4,1},{5,0},{6,3},{7,2},{8,13},{9,12},{10,... | collective-permute-start | bytes 147464 | tf_op jit(solution)/shard_map/ppermute | solution.py:27
  41.8 1.5 %collective-permute-start.16 = (bf16[96,512]{1,0:T(8,128)(2,1)S(1)}, bf16[96,512]{1,0:T(8,128)(2,1)S(1)}, u32[]{:S(2)}, u32[]{:S(2)}) collective-permute-start(bf16[96,512]{1,0:T(8,128)(2,1)S(1)} %get-tuple-element.62.lhs_ref.own_ref), channel_id=1, source_target_pairs={{0,16},{1,17},{2,18},{3,19},{4,20},{5,21},{6,22},{7,23},{8,24},{9,... | collective-permute-start | bytes 294920 | tf_op jit(solution)/shard_map/ppermute | solution.py:27
  43.4 2.3 %collective-permute-done.18.refs_2_ = bf16[192,128]{1,0:T(8,128)(2,1)S(1)} collective-permute-done((bf16[192,128]{1,0:T(8,128)(2,1)S(1)}, bf16[192,128]{1,0:T(8,128)(2,1)S(1)}, u32[]{:S(2)}, u32[]{:S(2)}) %collective-permute-start.18) | collective-permute-done | bytes 49184 | tf_op jit(solution)/shard_map/ppermute | solution.py:27
  45.9 1.3 %collective-permute-start.23 = (bf16[24,2048]{1,0:T(8,128)(2,1)S(1)}, bf16[24,2048]{1,0:T(8,128)(2,1)S(1)}, u32[]{:S(2)}, u32[]{:S(2)}) collective-permute-start(bf16[24,2048]{1,0:T(8,128)(2,1)S(1)} %get-tuple-element.63.refs_0_), channel_id=1, source_target_pairs={{0,17},{1,16},{2,19},{3,18},{4,21},{5,20},{6,23},{7,22},{8,25},{9,... | collective-permute-start | bytes 294920 | tf_op jit(solution)/shard_map/ppermute | solution.py:27
  47.2 0.4 collective-permute-start.21
  47.6 0.9 %collective-permute-start.20 = (bf16[24,2048]{1,0:T(8,128)(2,1)S(1)}, bf16[24,2048]{1,0:T(8,128)(2,1)S(1)}, u32[]{:S(2)}, u32[]{:S(2)}) collective-permute-start(bf16[24,2048]{1,0:T(8,128)(2,1)S(1)} %get-tuple-element.63.refs_0_), channel_id=1, source_target_pairs={{0,3},{1,2},{2,1},{3,0},{4,7},{5,6},{6,5},{7,4},{8,11},{9,10},{10,... | collective-permute-start | bytes 294920 | tf_op jit(solution)/shard_map/ppermute | solution.py:27
  48.5 0.8 %collective-permute-start.27 = (bf16[24,2048]{1,0:T(8,128)(2,1)S(1)}, bf16[24,2048]{1,0:T(8,128)(2,1)S(1)}, u32[]{:S(2)}, u32[]{:S(2)}) collective-permute-start(bf16[24,2048]{1,0:T(8,128)(2,1)S(1)} %get-tuple-element.64.refs_8_), channel_id=1, source_target_pairs={{0,3},{1,2},{2,1},{3,0},{4,7},{5,6},{6,5},{7,4},{8,11},{9,10},{10,... | collective-permute-start | bytes 294920 | tf_op jit(solution)/shard_map/ppermute | solution.py:27
  49.6 1.2 %collective-permute-done.23.refs_6_ = bf16[24,2048]{1,0:T(8,128)(2,1)S(1)} collective-permute-done((bf16[24,2048]{1,0:T(8,128)(2,1)S(1)}, bf16[24,2048]{1,0:T(8,128)(2,1)S(1)}, u32[]{:S(2)}, u32[]{:S(2)}) %collective-permute-start.23) | collective-permute-done | bytes 98336 | tf_op jit(solution)/shard_map/ppermute | solution.py:27
  50.8 0.4 collective-permute-start.28
  51.2 0.9 %collective-permute-start.25 = (bf16[24,2048]{1,0:T(8,128)(2,1)S(1)}, bf16[24,2048]{1,0:T(8,128)(2,1)S(1)}, u32[]{:S(2)}, u32[]{:S(2)}) collective-permute-start(bf16[24,2048]{1,0:T(8,128)(2,1)S(1)} %collective-permute-done.23.refs_6_), channel_id=1, source_target_pairs={{0,3},{1,2},{2,1},{3,0},{4,7},{5,6},{6,5},{7,4},{8,11},{9,10},{10,... | collective-permute-start | bytes 294920 | tf_op jit(solution)/shard_map/ppermute | solution.py:27
  52.1 0.3 collective-permute-done.20.refs_1_
  52.4 0.7 %collective-permute-start.24 = (bf16[24,2048]{1,0:T(8,128)(2,1)S(1)}, bf16[24,2048]{1,0:T(8,128)(2,1)S(1)}, u32[]{:S(2)}, u32[]{:S(2)}) collective-permute-start(bf16[24,2048]{1,0:T(8,128)(2,1)S(1)} %collective-permute-done.23.refs_6_), channel_id=1, source_target_pairs={{0,1},{1,0},{2,3},{3,2},{4,5},{5,4},{6,7},{7,6},{8,9},{9,8},{10,11... | collective-permute-start | bytes 294920 | tf_op jit(solution)/shard_map/ppermute | solution.py:27
  53.1 1.4 %collective-permute-done.27.refs_9_ = bf16[24,2048]{1,0:T(8,128)(2,1)S(1)} collective-permute-done((bf16[24,2048]{1,0:T(8,128)(2,1)S(1)}, bf16[24,2048]{1,0:T(8,128)(2,1)S(1)}, u32[]{:S(2)}, u32[]{:S(2)}) %collective-permute-start.27) | collective-permute-done | bytes 98336 | tf_op jit(solution)/shard_map/ppermute | solution.py:27
  54.5 0.3 collective-permute-start.32
  54.8 0.4 collective-permute-start.29
  55.3 1.3 %collective-permute-done.25.refs_7_ = bf16[24,2048]{1,0:T(8,128)(2,1)S(1)} collective-permute-done((bf16[24,2048]{1,0:T(8,128)(2,1)S(1)}, bf16[24,2048]{1,0:T(8,128)(2,1)S(1)}, u32[]{:S(2)}, u32[]{:S(2)}) %collective-permute-start.25) | collective-permute-done | bytes 98336 | tf_op jit(solution)/shard_map/ppermute | solution.py:27
  56.7 0.4 collective-permute-start.26
  57.1 1.6 %collective-permute-done.32.refs_15_ = bf16[24,2048]{1,0:T(8,128)(2,1)S(1)} collective-permute-done((bf16[24,2048]{1,0:T(8,128)(2,1)S(1)}, bf16[24,2048]{1,0:T(8,128)(2,1)S(1)}, u32[]{:S(2)}, u32[]{:S(2)}) %collective-permute-start.32) | collective-permute-done | bytes 98336 | tf_op jit(solution)/shard_map/ppermute | solution.py:27
  58.7 0.7 %collective-permute-start.33 = (bf16[24,2048]{1,0:T(8,128)(2,1)S(1)}, bf16[24,2048]{1,0:T(8,128)(2,1)S(1)}, u32[]{:S(2)}, u32[]{:S(2)}) collective-permute-start(bf16[24,2048]{1,0:T(8,128)(2,1)S(1)} %collective-permute-done.32.refs_15_), channel_id=1, source_target_pairs={{0,1},{1,0},{2,3},{3,2},{4,5},{5,4},{6,7},{7,6},{8,9},{9,8},{10,11... | collective-permute-start | bytes 294920 | tf_op jit(solution)/shard_map/ppermute | solution.py:27
  59.4 0.7 %shard_map.74 = bf16[6,4096]{1,0:T(8,128)(2,1)} custom-call(f32[192,128]{1,0:T(8,128)S(1)} %get-tuple-element.65.lines_ref), custom_call_target="tpu_custom_call" | custom-call | tf_op jit(solution)/shard_map/pallas_call | solution.py:136
  60.4 2.4 %shard_map.73 = bf16[512,4096]{1,0:T(8,128)(2,1)} custom-call(bf16[512,192]{1,0:T(8,128)(2,1)S(1)} %shard_map.71.states_ref, bf16[24,2048]{1,0:T(8,128)(2,1)S(1)} %get-tuple-element.63.refs_0_, bf16[24,2048]{1,0:T(8,128)(2,1)S(1)} %collective-permute-done.20.refs_1_, bf16[24,2048]{1,0:T(8,128)(2,1)S(1)} %collective-permute-done.21.refs_2_, ...), custom_call_target="tpu_custom_call" | custom-call | flops 805306368 | bytes 4194304 | tf_op jit(solution)/shard_map/pallas_call | solution.py:381
  (38 shorter events, 2.0 us)
Async XLA Ops:
  1.7 3.2 %collective-permute-start = (bf16[4,6,512]{2,1,0:T(8,128)(2,1)S(1)}, bf16[4,6,512]{2,1,0:T(8,128)(2,1)S(1)}, u32[]{:S(2)}, u32[]{:S(2)}) collective-permute-start(bf16[4,6,512]{2,1,0:T(8,128)(2,1)S(1)} %get-tuple-element.36), channel_id=1, source_target_pairs={{0,1},{1,0},{2,3},{3,2},{4,5},{5,4},{6,7},{7,6},{8,9},{9,8},{10,11... | collective-permute-start | bytes 73736 | tf_op jit(solution)/shard_map/ppermute | solution.py:27
  2.2 4.6 %collective-permute-start.1 = (bf16[4,6,512]{2,1,0:T(8,128)(2,1)S(1)}, bf16[4,6,512]{2,1,0:T(8,128)(2,1)S(1)}, u32[]{:S(2)}, u32[]{:S(2)}) collective-permute-start(bf16[4,6,512]{2,1,0:T(8,128)(2,1)S(1)} %get-tuple-element.37), channel_id=1, source_target_pairs={{0,2},{1,3},{2,0},{3,1},{4,6},{5,7},{6,4},{7,5},{8,10},{9,11},{10,... | collective-permute-start | bytes 73736 | tf_op jit(solution)/shard_map/ppermute | solution.py:27
  4.8 3.4 %collective-permute-start.2 = (bf16[4,6,512]{2,1,0:T(8,128)(2,1)S(1)}, bf16[4,6,512]{2,1,0:T(8,128)(2,1)S(1)}, u32[]{:S(2)}, u32[]{:S(2)}) collective-permute-start(bf16[4,6,512]{2,1,0:T(8,128)(2,1)S(1)} %get-tuple-element.38), channel_id=1, source_target_pairs={{0,3},{1,2},{2,1},{3,0},{4,7},{5,6},{6,5},{7,4},{8,11},{9,10},{10,... | collective-permute-start | bytes 73736 | tf_op jit(solution)/shard_map/ppermute | solution.py:27
  8.2 5.5 %collective-permute-start.3 = (bf16[24,512]{1,0:T(8,128)(2,1)S(1)}, bf16[24,512]{1,0:T(8,128)(2,1)S(1)}, u32[]{:S(2)}, u32[]{:S(2)}) collective-permute-start(bf16[24,512]{1,0:T(8,128)(2,1)S(1)} %get-tuple-element.40), channel_id=1, source_target_pairs={{0,5},{1,4},{2,7},{3,6},{4,1},{5,0},{6,3},{7,2},{8,13},{9,12},{10,... | collective-permute-start | bytes 73736 | tf_op jit(solution)/shard_map/ppermute | solution.py:27
  9.6 4.4 %collective-permute-start.4 = (bf16[24,512]{1,0:T(8,128)(2,1)S(1)}, bf16[24,512]{1,0:T(8,128)(2,1)S(1)}, u32[]{:S(2)}, u32[]{:S(2)}) collective-permute-start(bf16[24,512]{1,0:T(8,128)(2,1)S(1)} %get-tuple-element.41), channel_id=1, source_target_pairs={{0,9},{1,8},{2,11},{3,10},{4,13},{5,12},{6,15},{7,14},{8,1},{9,0},... | collective-permute-start | bytes 73736 | tf_op jit(solution)/shard_map/ppermute | solution.py:27
  12.1 5.0 %collective-permute-start.5 = (bf16[24,512]{1,0:T(8,128)(2,1)S(1)}, bf16[24,512]{1,0:T(8,128)(2,1)S(1)}, u32[]{:S(2)}, u32[]{:S(2)}) collective-permute-start(bf16[24,512]{1,0:T(8,128)(2,1)S(1)} %get-tuple-element.42), channel_id=1, source_target_pairs={{0,13},{1,12},{2,15},{3,14},{4,9},{5,8},{6,11},{7,10},{8,5},{9,4},... | collective-permute-start | bytes 73736 | tf_op jit(solution)/shard_map/ppermute | solution.py:27
  17.8 16.2 %copy-start = (bf16[6,4096]{1,0:T(8,128)(2,1)S(1)}, bf16[6,4096]{1,0:T(8,128)(2,1)}, u32[]{:S(2)}) copy-start(bf16[6,4096]{1,0:T(8,128)(2,1)} %rows_ref.1) | copy-start | bytes 147460
  17.8 2.7 %collective-permute-start.6 = (bf16[48,2048]{1,0:T(8,128)(2,1)S(1)}, bf16[48,2048]{1,0:T(8,128)(2,1)S(1)}, u32[]{:S(2)}, u32[]{:S(2)}) collective-permute-start(bf16[48,2048]{1,0:T(8,128)(2,1)S(1)} %get-tuple-element.46), channel_id=1, source_target_pairs={{0,1},{1,0},{2,3},{3,2},{4,5},{5,4},{6,7},{7,6},{8,9},{9,8},{10,11... | collective-permute-start | bytes 589832 | tf_op jit(solution)/shard_map/ppermute | solution.py:27
  20.1 1.5 %collective-permute-start.11 = (bf16[48,2048]{1,0:T(8,128)(2,1)S(1)}, bf16[48,2048]{1,0:T(8,128)(2,1)S(1)}, u32[]{:S(2)}, u32[]{:S(2)}) collective-permute-start(bf16[48,2048]{1,0:T(8,128)(2,1)S(1)} %get-tuple-element.54), channel_id=1, source_target_pairs={{0,1},{1,0},{2,3},{3,2},{4,5},{5,4},{6,7},{7,6},{8,9},{9,8},{10,11... | collective-permute-start | bytes 589832 | tf_op jit(solution)/shard_map/ppermute | solution.py:27
  20.5 9.4 %collective-permute-start.7 = (bf16[24,2048]{1,0:T(8,128)(2,1)S(1)}, bf16[24,2048]{1,0:T(8,128)(2,1)S(1)}, u32[]{:S(2)}, u32[]{:S(2)}) collective-permute-start(bf16[24,2048]{1,0:T(8,128)(2,1)S(1)} %get-tuple-element.48), channel_id=1, source_target_pairs={{0,3},{1,2},{2,1},{3,0},{4,7},{5,6},{6,5},{7,4},{8,11},{9,10},{10,... | collective-permute-start | bytes 294920 | tf_op jit(solution)/shard_map/ppermute | solution.py:27
  21.8 4.1 %collective-permute-start.12 = (bf16[192,128]{1,0:T(8,128)(2,1)S(1)}, bf16[192,128]{1,0:T(8,128)(2,1)S(1)}, u32[]{:S(2)}, u32[]{:S(2)}) collective-permute-start(bf16[192,128]{1,0:T(8,128)(2,1)S(1)} %get-tuple-element.56), channel_id=1, source_target_pairs={{0,5},{1,4},{2,7},{3,6},{4,1},{5,0},{6,3},{7,2},{8,13},{9,12},{10,... | collective-permute-start | bytes 147464 | tf_op jit(solution)/shard_map/ppermute | solution.py:27
  21.9 4.6 %collective-permute-start.13 = (bf16[192,128]{1,0:T(8,128)(2,1)S(1)}, bf16[192,128]{1,0:T(8,128)(2,1)S(1)}, u32[]{:S(2)}, u32[]{:S(2)}) collective-permute-start(bf16[192,128]{1,0:T(8,128)(2,1)S(1)} %get-tuple-element.57), channel_id=1, source_target_pairs={{0,9},{1,8},{2,11},{3,10},{4,13},{5,12},{6,15},{7,14},{8,1},{9,0},... | collective-permute-start | bytes 147464 | tf_op jit(solution)/shard_map/ppermute | solution.py:27
  22.7 6.3 %collective-permute-start.14 = (bf16[192,128]{1,0:T(8,128)(2,1)S(1)}, bf16[192,128]{1,0:T(8,128)(2,1)S(1)}, u32[]{:S(2)}, u32[]{:S(2)}) collective-permute-start(bf16[192,128]{1,0:T(8,128)(2,1)S(1)} %get-tuple-element.58), channel_id=1, source_target_pairs={{0,13},{1,12},{2,15},{3,14},{4,9},{5,8},{6,11},{7,10},{8,5},{9,4},... | collective-permute-start | bytes 147464 | tf_op jit(solution)/shard_map/ppermute | solution.py:27
  29.1 4.9 %collective-permute-start.15 = (bf16[96,128]{1,0:T(8,128)(2,1)S(1)}, bf16[96,128]{1,0:T(8,128)(2,1)S(1)}, u32[]{:S(2)}, u32[]{:S(2)}) collective-permute-start(bf16[96,128]{1,0:T(8,128)(2,1)S(1)} %get-tuple-element.60), channel_id=1, source_target_pairs={{0,3},{1,2},{2,1},{3,0},{4,7},{5,6},{6,5},{7,4},{8,11},{9,10},{10,... | collective-permute-start | bytes 73736 | tf_op jit(solution)/shard_map/ppermute | solution.py:27
  30.0 4.0 %collective-permute-start.8 = (bf16[96,128]{1,0:T(8,128)(2,1)S(1)}, bf16[96,128]{1,0:T(8,128)(2,1)S(1)}, u32[]{:S(2)}, u32[]{:S(2)}) collective-permute-start(bf16[96,128]{1,0:T(8,128)(2,1)S(1)} %get-tuple-element.50), channel_id=1, source_target_pairs={{0,5},{1,4},{2,7},{3,6},{4,1},{5,0},{6,3},{7,2},{8,13},{9,12},{10,... | collective-permute-start | bytes 73736 | tf_op jit(solution)/shard_map/ppermute | solution.py:27
  30.9 4.2 %collective-permute-start.9 = (bf16[96,128]{1,0:T(8,128)(2,1)S(1)}, bf16[96,128]{1,0:T(8,128)(2,1)S(1)}, u32[]{:S(2)}, u32[]{:S(2)}) collective-permute-start(bf16[96,128]{1,0:T(8,128)(2,1)S(1)} %get-tuple-element.51), channel_id=1, source_target_pairs={{0,9},{1,8},{2,11},{3,10},{4,13},{5,12},{6,15},{7,14},{8,1},{9,0},... | collective-permute-start | bytes 73736 | tf_op jit(solution)/shard_map/ppermute | solution.py:27
  32.6 5.0 %collective-permute-start.10 = (bf16[96,128]{1,0:T(8,128)(2,1)S(1)}, bf16[96,128]{1,0:T(8,128)(2,1)S(1)}, u32[]{:S(2)}, u32[]{:S(2)}) collective-permute-start(bf16[96,128]{1,0:T(8,128)(2,1)S(1)} %get-tuple-element.52), channel_id=1, source_target_pairs={{0,13},{1,12},{2,15},{3,14},{4,9},{5,8},{6,11},{7,10},{8,5},{9,4},... | collective-permute-start | bytes 73736 | tf_op jit(solution)/shard_map/ppermute | solution.py:27
  37.8 5.6 %collective-permute-start.19 = (bf16[192,128]{1,0:T(8,128)(2,1)S(1)}, bf16[192,128]{1,0:T(8,128)(2,1)S(1)}, u32[]{:S(2)}, u32[]{:S(2)}) collective-permute-start(bf16[192,128]{1,0:T(8,128)(2,1)S(1)} %get-tuple-element.61.refs_0_), channel_id=1, source_target_pairs={{0,13},{1,12},{2,15},{3,14},{4,9},{5,8},{6,11},{7,10},{8,5},{9,4},... | collective-permute-start | bytes 147464 | tf_op jit(solution)/shard_map/ppermute | solution.py:27
  39.2 6.6 %collective-permute-start.18 = (bf16[192,128]{1,0:T(8,128)(2,1)S(1)}, bf16[192,128]{1,0:T(8,128)(2,1)S(1)}, u32[]{:S(2)}, u32[]{:S(2)}) collective-permute-start(bf16[192,128]{1,0:T(8,128)(2,1)S(1)} %get-tuple-element.61.refs_0_), channel_id=1, source_target_pairs={{0,9},{1,8},{2,11},{3,10},{4,13},{5,12},{6,15},{7,14},{8,1},{9,0},... | collective-permute-start | bytes 147464 | tf_op jit(solution)/shard_map/ppermute | solution.py:27
  39.2 6.6 %collective-permute-start.17 = (bf16[192,128]{1,0:T(8,128)(2,1)S(1)}, bf16[192,128]{1,0:T(8,128)(2,1)S(1)}, u32[]{:S(2)}, u32[]{:S(2)}) collective-permute-start(bf16[192,128]{1,0:T(8,128)(2,1)S(1)} %get-tuple-element.61.refs_0_), channel_id=1, source_target_pairs={{0,5},{1,4},{2,7},{3,6},{4,1},{5,0},{6,3},{7,2},{8,13},{9,12},{10,... | collective-permute-start | bytes 147464 | tf_op jit(solution)/shard_map/ppermute | solution.py:27
  41.8 7.6 %collective-permute-start.16 = (bf16[96,512]{1,0:T(8,128)(2,1)S(1)}, bf16[96,512]{1,0:T(8,128)(2,1)S(1)}, u32[]{:S(2)}, u32[]{:S(2)}) collective-permute-start(bf16[96,512]{1,0:T(8,128)(2,1)S(1)} %get-tuple-element.62.lhs_ref.own_ref), channel_id=1, source_target_pairs={{0,16},{1,17},{2,18},{3,19},{4,20},{5,21},{6,22},{7,23},{8,24},{9,... | collective-permute-start | bytes 294920 | tf_op jit(solution)/shard_map/ppermute | solution.py:27
  45.9 4.9 %collective-permute-start.23 = (bf16[24,2048]{1,0:T(8,128)(2,1)S(1)}, bf16[24,2048]{1,0:T(8,128)(2,1)S(1)}, u32[]{:S(2)}, u32[]{:S(2)}) collective-permute-start(bf16[24,2048]{1,0:T(8,128)(2,1)S(1)} %get-tuple-element.63.refs_0_), channel_id=1, source_target_pairs={{0,17},{1,16},{2,19},{3,18},{4,21},{5,20},{6,23},{7,22},{8,25},{9,... | collective-permute-start | bytes 294920 | tf_op jit(solution)/shard_map/ppermute | solution.py:27
  47.2 4.0 %collective-permute-start.21 = (bf16[24,2048]{1,0:T(8,128)(2,1)S(1)}, bf16[24,2048]{1,0:T(8,128)(2,1)S(1)}, u32[]{:S(2)}, u32[]{:S(2)}) collective-permute-start(bf16[24,2048]{1,0:T(8,128)(2,1)S(1)} %get-tuple-element.63.refs_0_), channel_id=1, source_target_pairs={{0,1},{1,0},{2,3},{3,2},{4,5},{5,4},{6,7},{7,6},{8,9},{9,8},{10,11... | collective-permute-start | bytes 294920 | tf_op jit(solution)/shard_map/ppermute | solution.py:27
  47.6 4.8 %collective-permute-start.20 = (bf16[24,2048]{1,0:T(8,128)(2,1)S(1)}, bf16[24,2048]{1,0:T(8,128)(2,1)S(1)}, u32[]{:S(2)}, u32[]{:S(2)}) collective-permute-start(bf16[24,2048]{1,0:T(8,128)(2,1)S(1)} %get-tuple-element.63.refs_0_), channel_id=1, source_target_pairs={{0,3},{1,2},{2,1},{3,0},{4,7},{5,6},{6,5},{7,4},{8,11},{9,10},{10,... | collective-permute-start | bytes 294920 | tf_op jit(solution)/shard_map/ppermute | solution.py:27
  48.5 6.0 %collective-permute-start.27 = (bf16[24,2048]{1,0:T(8,128)(2,1)S(1)}, bf16[24,2048]{1,0:T(8,128)(2,1)S(1)}, u32[]{:S(2)}, u32[]{:S(2)}) collective-permute-start(bf16[24,2048]{1,0:T(8,128)(2,1)S(1)} %get-tuple-element.64.refs_8_), channel_id=1, source_target_pairs={{0,3},{1,2},{2,1},{3,0},{4,7},{5,6},{6,5},{7,4},{8,11},{9,10},{10,... | collective-permute-start | bytes 294920 | tf_op jit(solution)/shard_map/ppermute | solution.py:27
  49.4 5.4 %collective-permute-start.30 = (bf16[24,2048]{1,0:T(8,128)(2,1)S(1)}, bf16[24,2048]{1,0:T(8,128)(2,1)S(1)}, u32[]{:S(2)}, u32[]{:S(2)}) collective-permute-start(bf16[24,2048]{1,0:T(8,128)(2,1)S(1)} %get-tuple-element.64.refs_8_), channel_id=1, source_target_pairs={{0,17},{1,16},{2,19},{3,18},{4,21},{5,20},{6,23},{7,22},{8,25},{9,... | collective-permute-start | bytes 294920 | tf_op jit(solution)/shard_map/ppermute | solution.py:27
  50.8 4.4 %collective-permute-start.28 = (bf16[24,2048]{1,0:T(8,128)(2,1)S(1)}, bf16[24,2048]{1,0:T(8,128)(2,1)S(1)}, u32[]{:S(2)}, u32[]{:S(2)}) collective-permute-start(bf16[24,2048]{1,0:T(8,128)(2,1)S(1)} %get-tuple-element.64.refs_8_), channel_id=1, source_target_pairs={{0,1},{1,0},{2,3},{3,2},{4,5},{5,4},{6,7},{7,6},{8,9},{9,8},{10,11... | collective-permute-start | bytes 294920 | tf_op jit(solution)/shard_map/ppermute | solution.py:27
  51.2 5.4 %collective-permute-start.25 = (bf16[24,2048]{1,0:T(8,128)(2,1)S(1)}, bf16[24,2048]{1,0:T(8,128)(2,1)S(1)}, u32[]{:S(2)}, u32[]{:S(2)}) collective-permute-start(bf16[24,2048]{1,0:T(8,128)(2,1)S(1)} %collective-permute-done.23.refs_6_), channel_id=1, source_target_pairs={{0,3},{1,2},{2,1},{3,0},{4,7},{5,6},{6,5},{7,4},{8,11},{9,10},{10,... | collective-permute-start | bytes 294920 | tf_op jit(solution)/shard_map/ppermute | solution.py:27
  52.4 4.3 %collective-permute-start.24 = (bf16[24,2048]{1,0:T(8,128)(2,1)S(1)}, bf16[24,2048]{1,0:T(8,128)(2,1)S(1)}, u32[]{:S(2)}, u32[]{:S(2)}) collective-permute-start(bf16[24,2048]{1,0:T(8,128)(2,1)S(1)} %collective-permute-done.23.refs_6_), channel_id=1, source_target_pairs={{0,1},{1,0},{2,3},{3,2},{4,5},{5,4},{6,7},{7,6},{8,9},{9,8},{10,11... | collective-permute-start | bytes 294920 | tf_op jit(solution)/shard_map/ppermute | solution.py:27
  54.5 4.2 %collective-permute-start.32 = (bf16[24,2048]{1,0:T(8,128)(2,1)S(1)}, bf16[24,2048]{1,0:T(8,128)(2,1)S(1)}, u32[]{:S(2)}, u32[]{:S(2)}) collective-permute-start(bf16[24,2048]{1,0:T(8,128)(2,1)S(1)} %collective-permute-done.27.refs_9_), channel_id=1, source_target_pairs={{0,17},{1,16},{2,19},{3,18},{4,21},{5,20},{6,23},{7,22},{8,25},{9,... | collective-permute-start | bytes 294920 | tf_op jit(solution)/shard_map/ppermute | solution.py:27
  54.8 5.6 %collective-permute-start.29 = (bf16[24,2048]{1,0:T(8,128)(2,1)S(1)}, bf16[24,2048]{1,0:T(8,128)(2,1)S(1)}, u32[]{:S(2)}, u32[]{:S(2)}) collective-permute-start(bf16[24,2048]{1,0:T(8,128)(2,1)S(1)} %collective-permute-done.27.refs_9_), channel_id=1, source_target_pairs={{0,1},{1,0},{2,3},{3,2},{4,5},{5,4},{6,7},{7,6},{8,9},{9,8},{10,11... | collective-permute-start | bytes 294920 | tf_op jit(solution)/shard_map/ppermute | solution.py:27
  55.2 5.1 %collective-permute-start.22 = (bf16[24,2048]{1,0:T(8,128)(2,1)S(1)}, bf16[24,2048]{1,0:T(8,128)(2,1)S(1)}, u32[]{:S(2)}, u32[]{:S(2)}) collective-permute-start(bf16[24,2048]{1,0:T(8,128)(2,1)S(1)} %collective-permute-done.20.refs_1_), channel_id=1, source_target_pairs={{0,1},{1,0},{2,3},{3,2},{4,5},{5,4},{6,7},{7,6},{8,9},{9,8},{10,11... | collective-permute-start | bytes 294920 | tf_op jit(solution)/shard_map/ppermute | solution.py:27
  56.6 3.7 %collective-permute-start.31 = (bf16[24,2048]{1,0:T(8,128)(2,1)S(1)}, bf16[24,2048]{1,0:T(8,128)(2,1)S(1)}, u32[]{:S(2)}, u32[]{:S(2)}) collective-permute-start(bf16[24,2048]{1,0:T(8,128)(2,1)S(1)} %collective-permute-done.30.refs_14_), channel_id=1, source_target_pairs={{0,1},{1,0},{2,3},{3,2},{4,5},{5,4},{6,7},{7,6},{8,9},{9,8},{10,11... | collective-permute-start | bytes 294920 | tf_op jit(solution)/shard_map/ppermute | solution.py:27
  56.7 3.6 %collective-permute-start.26 = (bf16[24,2048]{1,0:T(8,128)(2,1)S(1)}, bf16[24,2048]{1,0:T(8,128)(2,1)S(1)}, u32[]{:S(2)}, u32[]{:S(2)}) collective-permute-start(bf16[24,2048]{1,0:T(8,128)(2,1)S(1)} %collective-permute-done.25.refs_7_), channel_id=1, source_target_pairs={{0,1},{1,0},{2,3},{3,2},{4,5},{5,4},{6,7},{7,6},{8,9},{9,8},{10,11... | collective-permute-start | bytes 294920 | tf_op jit(solution)/shard_map/ppermute | solution.py:27
  58.7 1.7 %collective-permute-start.33 = (bf16[24,2048]{1,0:T(8,128)(2,1)S(1)}, bf16[24,2048]{1,0:T(8,128)(2,1)S(1)}, u32[]{:S(2)}, u32[]{:S(2)}) collective-permute-start(bf16[24,2048]{1,0:T(8,128)(2,1)S(1)} %collective-permute-done.32.refs_15_), channel_id=1, source_target_pairs={{0,1},{1,0},{2,3},{3,2},{4,5},{5,4},{6,7},{7,6},{8,9},{9,8},{10,11... | collective-permute-start | bytes 294920 | tf_op jit(solution)/shard_map/ppermute | solution.py:27

commit v3 on v2

--- a/solution.py
+++ b/solution.py
@@ -150,30 +150,32 @@
 
 
 def split_kernel(x_ref, *refs):
-    outs, sems = refs[:-1], refs[-1]
-    far, _, part = outs[0].shape
+    outs, (x, rows, sems) = refs[:-3], refs[-3:]
+    unit, part = x.shape[0], outs[0].shape[1]
     feat = lax.axis_index("dev")
     copies = []
-    for s, out in enumerate(outs):
-        for m in range(far):
-            first = pl.multiple_of((feat ^ s ^ path(0, 0, m)) * part, part)
-            copies.append(
-                pltpu.make_async_copy(
-                    x_ref.at[:, pl.ds(first, part)], out.at[m], sems.at[len(copies)]
-                )
-            )
-    for copy in copies:
-        copy.start()
+    width = x.shape[1] // sems.shape[0]
+    for i in range(sems.shape[0]):
+        cols = pl.ds(i * width, width)
+        copies.append(pltpu.make_async_copy(x_ref.at[:, cols], x.at[:, cols], sems.at[i]))
+        copies[-1].start()
     for copy in copies:
         copy.wait()
+    for s, out in enumerate(outs):
+        for m in range(out.shape[0] // unit):
+            first = pl.multiple_of((feat ^ s ^ path(0, 0, m)) * part, part)
+            rows[s, m * unit : (m + 1) * unit, :] = x[:, pl.ds(first, part)].astype(jnp.float32)
+        out[...] = rows[s].astype(jnp.bfloat16)
 
 
 def far_kernel(near, *refs):
-    sources, outs, rows = refs[:near], refs[near:-1], refs[-1]
-    unit = sources[0].shape[1]
+    sources, outs, (taken, rows) = refs[:near], refs[near:-2], refs[-2:]
+    unit = sources[0].shape[0] // len(outs)
+    for s, source in enumerate(sources):
+        taken[s] = source[...].astype(jnp.float32)
+        for m in range(len(outs)):
+            rows[m, s * unit : (s + 1) * unit, :] = taken[s, m * unit : (m + 1) * unit, :]
     for m, out in enumerate(outs):
-        for s, source in enumerate(sources):
-            rows[m, s * unit : (s + 1) * unit, :] = source[m].astype(jnp.float32)
         out[...] = rows[m].astype(jnp.bfloat16)
 
 
@@ -416,22 +418,29 @@
 
     place = [path(c, n, m) for c in range(2) for n in range(2) for m in range(far)]
 
-    block = (unit, block_teacher)
+    rows = (near * unit, block_teacher)
     packed = local_call(
         split_kernel,
-        [((far, *block), bf16)] * near,
+        [((far * unit, block_teacher), bf16)] * near,
         [pltpu.with_memory_space_constraint(teacher, pltpu.HBM)],
         specs=[IN_HBM],
-        scratch=[pltpu.SemaphoreType.DMA((FEAT_SPLIT,))],
+        scratch=[
+            pltpu.VMEM(teacher.shape, bf16),
+            pltpu.VMEM((near, far * unit, block_teacher), f32),
+            pltpu.SemaphoreType.DMA((4,)),
+        ],
     )
     slots = [packed[0]]
     for k in range(1, near):
         slots.append(across(packed[k], 0, k))
     held = local_call(
         functools.partial(far_kernel, near),
-        [((near * unit, block_teacher), bf16)] * far,
+        [(rows, bf16)] * far,
         slots,
-        scratch=[pltpu.VMEM((far, near * unit, block_teacher), f32)],
+        scratch=[
+            pltpu.VMEM((near, far * unit, block_teacher), f32),
+            pltpu.VMEM((far, *rows), f32),
+        ],
     )
     held = [held[0]] + far_across(held)
 
@@ -493,14 +502,13 @@
     )
     near_b = across(leaving, 0, path(0, 1, 0))
     (target,) = local_call(target_kernel, [((size, LANES), f32)], [student_tiles])
+    other_states = across(states, 1, 0)
     slope, grad = local_call(
         functools.partial(slope_kernel, unit),
         [((size, LANES), bf16), ((size, LANES), f32)],
         [own_a, *far_a, own_b, near_b, target],
     )
     (grad,) = local_call(rows_kernel, [((unit, block_student), bf16)], [grad])
-    states_too, _ = lax.optimization_barrier((states, slope))
-    other_states = across(states_too, 1, 0)
 
     line = [slope] + far_across([slope] * far)
     lines = local_call(

time: 63.1 us -> 62.8 us (level)
  no operation moved by 1% of the time
where the time goes in v3:
time: 62.8 us; the launch traced here: 62.5 us
  starting transfers between devices  30.4 us (48%)
  waiting for transfers between devices  22.2 us (35%)
  Pallas kernels  9.13 us (15%)
  between operations  0.8 us (1%)
    ppermute x34, starting transfers between devices, across(): return lax.ppermute(value, ('group', 'dev'), pairs)  30.4 us
    ppermute x34, waiting for transfers between devices, across(): return lax.ppermute(value, ('group', 'dev'), pairs)  22.2 us
    pallas_call x15, Pallas kernels, local_call(): pl.pallas_call(kernel, out_shape=[jax.ShapeDtypeStruct(shape, kind) for s...  6.75 us
    pallas_call x1, Pallas kernels, grad_call(): pl.pallas_call(functools.partial(grad_kernel, scale, step, per), out_shap...  2.37 us
  transfers between devices with their start and end apart: 34, of which 16 were waited for; matrix products, arithmetic and copies ran while one was open for 0% of the time, Pallas kernels for 8%

profile of v3, /device:TPU:0, one launch (start us, length us, event | category | flops | bytes accessed | tf_op | source)
XLA Modules:
  0.0 62.5 jit_solution(4532164957902073971)
XLA Ops:
  0.6 0.9 %shard_map.60 = (bf16[24,512]{1,0:T(8,128)(2,1)S(1)}, bf16[24,512]{1,0:T(8,128)(2,1)S(1)}, bf16[24,512]{1,0:T(8,128)(2,1)S(1)}, bf16[24,512]{1,0:T(8,128)(2,1)S(1)}) custom-call(bf16[6,8192]{1,0:T(8,128)(2,1)} %x_ref.1), custom_call_target="tpu_custom_call" | custom-call | tf_op jit(solution)/shard_map/pallas_call | solution.py:136
  1.5 0.6 collective-permute-start
  2.1 2.6 %collective-permute-start.1 = (bf16[24,512]{1,0:T(8,128)(2,1)S(1)}, bf16[24,512]{1,0:T(8,128)(2,1)S(1)}, u32[]{:S(2)}, u32[]{:S(2)}) collective-permute-start(bf16[24,512]{1,0:T(8,128)(2,1)S(1)} %get-tuple-element.36), channel_id=1, source_target_pairs={{0,2},{1,3},{2,0},{3,1},{4,6},{5,7},{6,4},{7,5},{8,10},{9,11},{10,... | collective-permute-start | bytes 73736 | tf_op jit(solution)/shard_map/ppermute | solution.py:27
  4.7 1.8 %collective-permute-done.1.refs_2_ = bf16[24,512]{1,0:T(8,128)(2,1)S(1)} collective-permute-done((bf16[24,512]{1,0:T(8,128)(2,1)S(1)}, bf16[24,512]{1,0:T(8,128)(2,1)S(1)}, u32[]{:S(2)}, u32[]{:S(2)}) %collective-permute-start.1) | collective-permute-done | bytes 24608 | tf_op jit(solution)/shard_map/ppermute | solution.py:27
  6.5 1.4 %collective-permute-done.2.refs_3_ = bf16[24,512]{1,0:T(8,128)(2,1)S(1)} collective-permute-done((bf16[24,512]{1,0:T(8,128)(2,1)S(1)}, bf16[24,512]{1,0:T(8,128)(2,1)S(1)}, u32[]{:S(2)}, u32[]{:S(2)}) %collective-permute-start.2) | collective-permute-done | bytes 24608 | tf_op jit(solution)/shard_map/ppermute | solution.py:27
  8.0 1.4 %collective-permute-start.3 = (bf16[24,512]{1,0:T(8,128)(2,1)S(1)}, bf16[24,512]{1,0:T(8,128)(2,1)S(1)}, u32[]{:S(2)}, u32[]{:S(2)}) collective-permute-start(bf16[24,512]{1,0:T(8,128)(2,1)S(1)} %get-tuple-element.39), channel_id=1, source_target_pairs={{0,5},{1,4},{2,7},{3,6},{4,1},{5,0},{6,3},{7,2},{8,13},{9,12},{10,... | collective-permute-start | bytes 73736 | tf_op jit(solution)/shard_map/ppermute | solution.py:27
  9.4 2.6 %collective-permute-start.4 = (bf16[24,512]{1,0:T(8,128)(2,1)S(1)}, bf16[24,512]{1,0:T(8,128)(2,1)S(1)}, u32[]{:S(2)}, u32[]{:S(2)}) collective-permute-start(bf16[24,512]{1,0:T(8,128)(2,1)S(1)} %get-tuple-element.40), channel_id=1, source_target_pairs={{0,9},{1,8},{2,11},{3,10},{4,13},{5,12},{6,15},{7,14},{8,1},{9,0},... | collective-permute-start | bytes 73736 | tf_op jit(solution)/shard_map/ppermute | solution.py:27
  11.9 1.6 %shard_map.59 = (bf16[96,96]{1,0:T(8,128)(2,1)S(1)}, bf16[512,2048]{1,0:T(8,128)(2,1)S(1)}) custom-call(s32[2,16]{1,0:T(2,128)} %owner_ref.1, bf16[512,4096]{1,0:T(8,128)(2,1)} %tiles_ref.3), custom_call_target="tpu_custom_call" | custom-call | flops 201326592 | bytes 2097152 | tf_op jit(solution)/shard_map/pallas_call | solution.py:136
  13.8 3.2 %collective-permute-done.5.refs_3_ = bf16[24,512]{1,0:T(8,128)(2,1)S(1)} collective-permute-done((bf16[24,512]{1,0:T(8,128)(2,1)S(1)}, bf16[24,512]{1,0:T(8,128)(2,1)S(1)}, u32[]{:S(2)}, u32[]{:S(2)}) %collective-permute-start.5) | collective-permute-done | bytes 24608 | tf_op jit(solution)/shard_map/ppermute | solution.py:27
  17.0 0.6 shard_map.62
  17.8 1.6 %shard_map.66.tiles_ref = bf16[512,2048]{1,0:T(8,128)(2,1)S(1)} custom-call(bf16[512,4096]{1,0:T(8,128)(2,1)} %tiles_ref.3), custom_call_target="tpu_custom_call" | custom-call | flops 201326592 | bytes 2097152 | tf_op jit(solution)/shard_map/pallas_call | solution.py:136
  19.4 0.5 shard_map.67
  19.8 0.4 collective-permute-start.12
  20.3 0.6 collective-permute-start.8
  20.9 0.5 collective-permute-done.12.arrived_ref
  21.6 0.9 %collective-permute-start.14 = (bf16[192,128]{1,0:T(8,128)(2,1)S(1)}, bf16[192,128]{1,0:T(8,128)(2,1)S(1)}, u32[]{:S(2)}, u32[]{:S(2)}) collective-permute-start(bf16[192,128]{1,0:T(8,128)(2,1)S(1)} %get-tuple-element.56), channel_id=1, source_target_pairs={{0,9},{1,8},{2,11},{3,10},{4,13},{5,12},{6,15},{7,14},{8,1},{9,0},... | collective-permute-start | bytes 147464 | tf_op jit(solution)/shard_map/ppermute | solution.py:27
  22.5 3.2 %collective-permute-start.15 = (bf16[192,128]{1,0:T(8,128)(2,1)S(1)}, bf16[192,128]{1,0:T(8,128)(2,1)S(1)}, u32[]{:S(2)}, u32[]{:S(2)}) collective-permute-start(bf16[192,128]{1,0:T(8,128)(2,1)S(1)} %get-tuple-element.57), channel_id=1, source_target_pairs={{0,13},{1,12},{2,15},{3,14},{4,9},{5,8},{6,11},{7,10},{8,5},{9,4},... | collective-permute-start | bytes 147464 | tf_op jit(solution)/shard_map/ppermute | solution.py:27
  25.7 0.5 collective-permute-done.14.refs_2_
  26.2 2.6 %collective-permute-done.15.refs_3_ = bf16[192,128]{1,0:T(8,128)(2,1)S(1)} collective-permute-done((bf16[192,128]{1,0:T(8,128)(2,1)S(1)}, bf16[192,128]{1,0:T(8,128)(2,1)S(1)}, u32[]{:S(2)}, u32[]{:S(2)}) %collective-permute-start.15) | collective-permute-done | bytes 49184 | tf_op jit(solution)/shard_map/ppermute | solution.py:27
  28.9 0.8 %collective-permute-start.16 = (bf16[96,128]{1,0:T(8,128)(2,1)S(1)}, bf16[96,128]{1,0:T(8,128)(2,1)S(1)}, u32[]{:S(2)}, u32[]{:S(2)}) collective-permute-start(bf16[96,128]{1,0:T(8,128)(2,1)S(1)} %get-tuple-element.59), channel_id=1, source_target_pairs={{0,3},{1,2},{2,1},{3,0},{4,7},{5,6},{6,5},{7,4},{8,11},{9,10},{10,... | collective-permute-start | bytes 73736 | tf_op jit(solution)/shard_map/ppermute | solution.py:27
  29.7 0.9 %collective-permute-start.9 = (bf16[96,128]{1,0:T(8,128)(2,1)S(1)}, bf16[96,128]{1,0:T(8,128)(2,1)S(1)}, u32[]{:S(2)}, u32[]{:S(2)}) collective-permute-start(bf16[96,128]{1,0:T(8,128)(2,1)S(1)} %get-tuple-element.49), channel_id=1, source_target_pairs={{0,5},{1,4},{2,7},{3,6},{4,1},{5,0},{6,3},{7,2},{8,13},{9,12},{10,... | collective-permute-start | bytes 73736 | tf_op jit(solution)/shard_map/ppermute | solution.py:27
  30.6 1.8 %collective-permute-start.10 = (bf16[96,128]{1,0:T(8,128)(2,1)S(1)}, bf16[96,128]{1,0:T(8,128)(2,1)S(1)}, u32[]{:S(2)}, u32[]{:S(2)}) collective-permute-start(bf16[96,128]{1,0:T(8,128)(2,1)S(1)} %get-tuple-element.50), channel_id=1, source_target_pairs={{0,9},{1,8},{2,11},{3,10},{4,13},{5,12},{6,15},{7,14},{8,1},{9,0},... | collective-permute-start | bytes 73736 | tf_op jit(solution)/shard_map/ppermute | solution.py:27
  32.4 1.4 %collective-permute-start.11 = (bf16[96,128]{1,0:T(8,128)(2,1)S(1)}, bf16[96,128]{1,0:T(8,128)(2,1)S(1)}, u32[]{:S(2)}, u32[]{:S(2)}) collective-permute-start(bf16[96,128]{1,0:T(8,128)(2,1)S(1)} %get-tuple-element.51), channel_id=1, source_target_pairs={{0,13},{1,12},{2,15},{3,14},{4,9},{5,8},{6,11},{7,10},{8,5},{9,4},... | collective-permute-start | bytes 73736 | tf_op jit(solution)/shard_map/ppermute | solution.py:27
  33.8 1.0 %collective-permute-done.10.refs_2_ = bf16[96,128]{1,0:T(8,128)(2,1)S(1)} collective-permute-done((bf16[96,128]{1,0:T(8,128)(2,1)S(1)}, bf16[96,128]{1,0:T(8,128)(2,1)S(1)}, u32[]{:S(2)}, u32[]{:S(2)}) %collective-permute-start.10) | collective-permute-done | bytes 24608 | tf_op jit(solution)/shard_map/ppermute | solution.py:27
  34.8 2.6 %collective-permute-done.11.refs_3_ = bf16[96,128]{1,0:T(8,128)(2,1)S(1)} collective-permute-done((bf16[96,128]{1,0:T(8,128)(2,1)S(1)}, bf16[96,128]{1,0:T(8,128)(2,1)S(1)}, u32[]{:S(2)}, u32[]{:S(2)}) %collective-permute-start.11) | collective-permute-done | bytes 24608 | tf_op jit(solution)/shard_map/ppermute | solution.py:27
  37.6 1.4 %collective-permute-start.19 = (bf16[192,128]{1,0:T(8,128)(2,1)S(1)}, bf16[192,128]{1,0:T(8,128)(2,1)S(1)}, u32[]{:S(2)}, u32[]{:S(2)}) collective-permute-start(bf16[192,128]{1,0:T(8,128)(2,1)S(1)} %get-tuple-element.60.refs_0_), channel_id=1, source_target_pairs={{0,13},{1,12},{2,15},{3,14},{4,9},{5,8},{6,11},{7,10},{8,5},{9,4},... | collective-permute-start | bytes 147464 | tf_op jit(solution)/shard_map/ppermute | solution.py:27
  39.0 2.5 %collective-permute-start.17 = (bf16[192,128]{1,0:T(8,128)(2,1)S(1)}, bf16[192,128]{1,0:T(8,128)(2,1)S(1)}, u32[]{:S(2)}, u32[]{:S(2)}) collective-permute-start(bf16[192,128]{1,0:T(8,128)(2,1)S(1)} %get-tuple-element.60.refs_0_), channel_id=1, source_target_pairs={{0,5},{1,4},{2,7},{3,6},{4,1},{5,0},{6,3},{7,2},{8,13},{9,12},{10,... | collective-permute-start | bytes 147464 | tf_op jit(solution)/shard_map/ppermute | solution.py:27
  41.5 1.5 %collective-permute-start.6 = (bf16[96,512]{1,0:T(8,128)(2,1)S(1)}, bf16[96,512]{1,0:T(8,128)(2,1)S(1)}, u32[]{:S(2)}, u32[]{:S(2)}) collective-permute-start(bf16[96,512]{1,0:T(8,128)(2,1)S(1)} %get-tuple-element.43.own_ref.lhs_ref), channel_id=1, source_target_pairs={{0,16},{1,17},{2,18},{3,19},{4,20},{5,21},{6,22},{7,23},{8,24},{9,... | collective-permute-start | bytes 294920 | tf_op jit(solution)/shard_map/ppermute | solution.py:27
  43.2 2.3 %collective-permute-done.18.refs_2_ = bf16[192,128]{1,0:T(8,128)(2,1)S(1)} collective-permute-done((bf16[192,128]{1,0:T(8,128)(2,1)S(1)}, bf16[192,128]{1,0:T(8,128)(2,1)S(1)}, u32[]{:S(2)}, u32[]{:S(2)}) %collective-permute-start.18) | collective-permute-done | bytes 49184 | tf_op jit(solution)/shard_map/ppermute | solution.py:27
  45.7 1.3 %collective-permute-start.23 = (bf16[24,2048]{1,0:T(8,128)(2,1)S(1)}, bf16[24,2048]{1,0:T(8,128)(2,1)S(1)}, u32[]{:S(2)}, u32[]{:S(2)}) collective-permute-start(bf16[24,2048]{1,0:T(8,128)(2,1)S(1)} %get-tuple-element.61.refs_0_), channel_id=1, source_target_pairs={{0,17},{1,16},{2,19},{3,18},{4,21},{5,20},{6,23},{7,22},{8,25},{9,... | collective-permute-start | bytes 294920 | tf_op jit(solution)/shard_map/ppermute | solution.py:27
  47.0 0.4 collective-permute-start.21
  47.4 0.9 %collective-permute-start.20 = (bf16[24,2048]{1,0:T(8,128)(2,1)S(1)}, bf16[24,2048]{1,0:T(8,128)(2,1)S(1)}, u32[]{:S(2)}, u32[]{:S(2)}) collective-permute-start(bf16[24,2048]{1,0:T(8,128)(2,1)S(1)} %get-tuple-element.61.refs_0_), channel_id=1, source_target_pairs={{0,3},{1,2},{2,1},{3,0},{4,7},{5,6},{6,5},{7,4},{8,11},{9,10},{10,... | collective-permute-start | bytes 294920 | tf_op jit(solution)/shard_map/ppermute | solution.py:27
  48.3 0.8 %collective-permute-start.27 = (bf16[24,2048]{1,0:T(8,128)(2,1)S(1)}, bf16[24,2048]{1,0:T(8,128)(2,1)S(1)}, u32[]{:S(2)}, u32[]{:S(2)}) collective-permute-start(bf16[24,2048]{1,0:T(8,128)(2,1)S(1)} %get-tuple-element.62.refs_8_), channel_id=1, source_target_pairs={{0,3},{1,2},{2,1},{3,0},{4,7},{5,6},{6,5},{7,4},{8,11},{9,10},{10,... | collective-permute-start | bytes 294920 | tf_op jit(solution)/shard_map/ppermute | solution.py:27
  49.1 0.3 collective-permute-start.30
  49.4 1.2 %collective-permute-done.23.refs_6_ = bf16[24,2048]{1,0:T(8,128)(2,1)S(1)} collective-permute-done((bf16[24,2048]{1,0:T(8,128)(2,1)S(1)}, bf16[24,2048]{1,0:T(8,128)(2,1)S(1)}, u32[]{:S(2)}, u32[]{:S(2)}) %collective-permute-start.23) | collective-permute-done | bytes 98336 | tf_op jit(solution)/shard_map/ppermute | solution.py:27
  50.6 0.4 collective-permute-start.28
  51.0 0.9 %collective-permute-start.25 = (bf16[24,2048]{1,0:T(8,128)(2,1)S(1)}, bf16[24,2048]{1,0:T(8,128)(2,1)S(1)}, u32[]{:S(2)}, u32[]{:S(2)}) collective-permute-start(bf16[24,2048]{1,0:T(8,128)(2,1)S(1)} %collective-permute-done.23.refs_6_), channel_id=1, source_target_pairs={{0,3},{1,2},{2,1},{3,0},{4,7},{5,6},{6,5},{7,4},{8,11},{9,10},{10,... | collective-permute-start | bytes 294920 | tf_op jit(solution)/shard_map/ppermute | solution.py:27
  51.9 0.3 collective-permute-done.20.refs_1_
  52.2 0.7 %collective-permute-start.24 = (bf16[24,2048]{1,0:T(8,128)(2,1)S(1)}, bf16[24,2048]{1,0:T(8,128)(2,1)S(1)}, u32[]{:S(2)}, u32[]{:S(2)}) collective-permute-start(bf16[24,2048]{1,0:T(8,128)(2,1)S(1)} %collective-permute-done.23.refs_6_), channel_id=1, source_target_pairs={{0,1},{1,0},{2,3},{3,2},{4,5},{5,4},{6,7},{7,6},{8,9},{9,8},{10,11... | collective-permute-start | bytes 294920 | tf_op jit(solution)/shard_map/ppermute | solution.py:27
  52.9 1.4 %collective-permute-done.27.refs_9_ = bf16[24,2048]{1,0:T(8,128)(2,1)S(1)} collective-permute-done((bf16[24,2048]{1,0:T(8,128)(2,1)S(1)}, bf16[24,2048]{1,0:T(8,128)(2,1)S(1)}, u32[]{:S(2)}, u32[]{:S(2)}) %collective-permute-start.27) | collective-permute-done | bytes 98336 | tf_op jit(solution)/shard_map/ppermute | solution.py:27
  54.3 0.3 collective-permute-start.32
  54.5 0.4 collective-permute-start.29
  55.1 1.3 %collective-permute-done.25.refs_7_ = bf16[24,2048]{1,0:T(8,128)(2,1)S(1)} collective-permute-done((bf16[24,2048]{1,0:T(8,128)(2,1)S(1)}, bf16[24,2048]{1,0:T(8,128)(2,1)S(1)}, u32[]{:S(2)}, u32[]{:S(2)}) %collective-permute-start.25) | collective-permute-done | bytes 98336 | tf_op jit(solution)/shard_map/ppermute | solution.py:27
  56.5 0.4 collective-permute-start.26
  56.9 1.6 %collective-permute-done.32.refs_15_ = bf16[24,2048]{1,0:T(8,128)(2,1)S(1)} collective-permute-done((bf16[24,2048]{1,0:T(8,128)(2,1)S(1)}, bf16[24,2048]{1,0:T(8,128)(2,1)S(1)}, u32[]{:S(2)}, u32[]{:S(2)}) %collective-permute-start.32) | collective-permute-done | bytes 98336 | tf_op jit(solution)/shard_map/ppermute | solution.py:27
  58.5 0.7 %collective-permute-start.33 = (bf16[24,2048]{1,0:T(8,128)(2,1)S(1)}, bf16[24,2048]{1,0:T(8,128)(2,1)S(1)}, u32[]{:S(2)}, u32[]{:S(2)}) collective-permute-start(bf16[24,2048]{1,0:T(8,128)(2,1)S(1)} %collective-permute-done.32.refs_15_), channel_id=1, source_target_pairs={{0,1},{1,0},{2,3},{3,2},{4,5},{5,4},{6,7},{7,6},{8,9},{9,8},{10,11... | collective-permute-start | bytes 294920 | tf_op jit(solution)/shard_map/ppermute | solution.py:27
  59.5 0.7 %shard_map.74 = bf16[6,4096]{1,0:T(8,128)(2,1)} custom-call(f32[192,128]{1,0:T(8,128)S(1)} %get-tuple-element.63.lines_ref), custom_call_target="tpu_custom_call" | custom-call | tf_op jit(solution)/shard_map/pallas_call | solution.py:136
  60.2 2.4 %shard_map.73 = bf16[512,4096]{1,0:T(8,128)(2,1)} custom-call(bf16[512,192]{1,0:T(8,128)(2,1)S(1)} %shard_map.63.states_ref, bf16[24,2048]{1,0:T(8,128)(2,1)S(1)} %get-tuple-element.61.refs_0_, bf16[24,2048]{1,0:T(8,128)(2,1)S(1)} %collective-permute-done.20.refs_1_, bf16[24,2048]{1,0:T(8,128)(2,1)S(1)} %collective-permute-done.21.refs_2_, ...), custom_call_target="tpu_custom_call" | custom-call | flops 805306368 | bytes 4194304 | tf_op jit(solution)/shard_map/pallas_call | solution.py:383
  (38 shorter events, 2.1 us)
Async XLA Ops:
  1.5 3.2 %collective-permute-start = (bf16[24,512]{1,0:T(8,128)(2,1)S(1)}, bf16[24,512]{1,0:T(8,128)(2,1)S(1)}, u32[]{:S(2)}, u32[]{:S(2)}) collective-permute-start(bf16[24,512]{1,0:T(8,128)(2,1)S(1)} %get-tuple-element.35), channel_id=1, source_target_pairs={{0,1},{1,0},{2,3},{3,2},{4,5},{5,4},{6,7},{7,6},{8,9},{9,8},{10,11... | collective-permute-start | bytes 73736 | tf_op jit(solution)/shard_map/ppermute | solution.py:27
  2.1 4.4 %collective-permute-start.1 = (bf16[24,512]{1,0:T(8,128)(2,1)S(1)}, bf16[24,512]{1,0:T(8,128)(2,1)S(1)}, u32[]{:S(2)}, u32[]{:S(2)}) collective-permute-start(bf16[24,512]{1,0:T(8,128)(2,1)S(1)} %get-tuple-element.36), channel_id=1, source_target_pairs={{0,2},{1,3},{2,0},{3,1},{4,6},{5,7},{6,4},{7,5},{8,10},{9,11},{10,... | collective-permute-start | bytes 73736 | tf_op jit(solution)/shard_map/ppermute | solution.py:27
  4.7 3.3 %collective-permute-start.2 = (bf16[24,512]{1,0:T(8,128)(2,1)S(1)}, bf16[24,512]{1,0:T(8,128)(2,1)S(1)}, u32[]{:S(2)}, u32[]{:S(2)}) collective-permute-start(bf16[24,512]{1,0:T(8,128)(2,1)S(1)} %get-tuple-element.37), channel_id=1, source_target_pairs={{0,3},{1,2},{2,1},{3,0},{4,7},{5,6},{6,5},{7,4},{8,11},{9,10},{10,... | collective-permute-start | bytes 73736 | tf_op jit(solution)/shard_map/ppermute | solution.py:27
  8.0 5.5 %collective-permute-start.3 = (bf16[24,512]{1,0:T(8,128)(2,1)S(1)}, bf16[24,512]{1,0:T(8,128)(2,1)S(1)}, u32[]{:S(2)}, u32[]{:S(2)}) collective-permute-start(bf16[24,512]{1,0:T(8,128)(2,1)S(1)} %get-tuple-element.39), channel_id=1, source_target_pairs={{0,5},{1,4},{2,7},{3,6},{4,1},{5,0},{6,3},{7,2},{8,13},{9,12},{10,... | collective-permute-start | bytes 73736 | tf_op jit(solution)/shard_map/ppermute | solution.py:27
  9.4 4.4 %collective-permute-start.4 = (bf16[24,512]{1,0:T(8,128)(2,1)S(1)}, bf16[24,512]{1,0:T(8,128)(2,1)S(1)}, u32[]{:S(2)}, u32[]{:S(2)}) collective-permute-start(bf16[24,512]{1,0:T(8,128)(2,1)S(1)} %get-tuple-element.40), channel_id=1, source_target_pairs={{0,9},{1,8},{2,11},{3,10},{4,13},{5,12},{6,15},{7,14},{8,1},{9,0},... | collective-permute-start | bytes 73736 | tf_op jit(solution)/shard_map/ppermute | solution.py:27
  11.9 5.0 %collective-permute-start.5 = (bf16[24,512]{1,0:T(8,128)(2,1)S(1)}, bf16[24,512]{1,0:T(8,128)(2,1)S(1)}, u32[]{:S(2)}, u32[]{:S(2)}) collective-permute-start(bf16[24,512]{1,0:T(8,128)(2,1)S(1)} %get-tuple-element.41), channel_id=1, source_target_pairs={{0,13},{1,12},{2,15},{3,14},{4,9},{5,8},{6,11},{7,10},{8,5},{9,4},... | collective-permute-start | bytes 73736 | tf_op jit(solution)/shard_map/ppermute | solution.py:27
  17.6 16.2 %copy-start = (bf16[6,4096]{1,0:T(8,128)(2,1)S(1)}, bf16[6,4096]{1,0:T(8,128)(2,1)}, u32[]{:S(2)}) copy-start(bf16[6,4096]{1,0:T(8,128)(2,1)} %rows_ref.1) | copy-start | bytes 147460
  17.6 2.7 %collective-permute-start.7 = (bf16[48,2048]{1,0:T(8,128)(2,1)S(1)}, bf16[48,2048]{1,0:T(8,128)(2,1)S(1)}, u32[]{:S(2)}, u32[]{:S(2)}) collective-permute-start(bf16[48,2048]{1,0:T(8,128)(2,1)S(1)} %get-tuple-element.45), channel_id=1, source_target_pairs={{0,1},{1,0},{2,3},{3,2},{4,5},{5,4},{6,7},{7,6},{8,9},{9,8},{10,11... | collective-permute-start | bytes 589832 | tf_op jit(solution)/shard_map/ppermute | solution.py:27
  19.8 1.5 %collective-permute-start.12 = (bf16[48,2048]{1,0:T(8,128)(2,1)S(1)}, bf16[48,2048]{1,0:T(8,128)(2,1)S(1)}, u32[]{:S(2)}, u32[]{:S(2)}) collective-permute-start(bf16[48,2048]{1,0:T(8,128)(2,1)S(1)} %get-tuple-element.53), channel_id=1, source_target_pairs={{0,1},{1,0},{2,3},{3,2},{4,5},{5,4},{6,7},{7,6},{8,9},{9,8},{10,11... | collective-permute-start | bytes 589832 | tf_op jit(solution)/shard_map/ppermute | solution.py:27
  20.3 9.3 %collective-permute-start.8 = (bf16[24,2048]{1,0:T(8,128)(2,1)S(1)}, bf16[24,2048]{1,0:T(8,128)(2,1)S(1)}, u32[]{:S(2)}, u32[]{:S(2)}) collective-permute-start(bf16[24,2048]{1,0:T(8,128)(2,1)S(1)} %get-tuple-element.47), channel_id=1, source_target_pairs={{0,3},{1,2},{2,1},{3,0},{4,7},{5,6},{6,5},{7,4},{8,11},{9,10},{10,... | collective-permute-start | bytes 294920 | tf_op jit(solution)/shard_map/ppermute | solution.py:27
  21.6 4.1 %collective-permute-start.13 = (bf16[192,128]{1,0:T(8,128)(2,1)S(1)}, bf16[192,128]{1,0:T(8,128)(2,1)S(1)}, u32[]{:S(2)}, u32[]{:S(2)}) collective-permute-start(bf16[192,128]{1,0:T(8,128)(2,1)S(1)} %get-tuple-element.55), channel_id=1, source_target_pairs={{0,5},{1,4},{2,7},{3,6},{4,1},{5,0},{6,3},{7,2},{8,13},{9,12},{10,... | collective-permute-start | bytes 147464 | tf_op jit(solution)/shard_map/ppermute | solution.py:27
  21.6 4.6 %collective-permute-start.14 = (bf16[192,128]{1,0:T(8,128)(2,1)S(1)}, bf16[192,128]{1,0:T(8,128)(2,1)S(1)}, u32[]{:S(2)}, u32[]{:S(2)}) collective-permute-start(bf16[192,128]{1,0:T(8,128)(2,1)S(1)} %get-tuple-element.56), channel_id=1, source_target_pairs={{0,9},{1,8},{2,11},{3,10},{4,13},{5,12},{6,15},{7,14},{8,1},{9,0},... | collective-permute-start | bytes 147464 | tf_op jit(solution)/shard_map/ppermute | solution.py:27
  22.5 6.3 %collective-permute-start.15 = (bf16[192,128]{1,0:T(8,128)(2,1)S(1)}, bf16[192,128]{1,0:T(8,128)(2,1)S(1)}, u32[]{:S(2)}, u32[]{:S(2)}) collective-permute-start(bf16[192,128]{1,0:T(8,128)(2,1)S(1)} %get-tuple-element.57), channel_id=1, source_target_pairs={{0,13},{1,12},{2,15},{3,14},{4,9},{5,8},{6,11},{7,10},{8,5},{9,4},... | collective-permute-start | bytes 147464 | tf_op jit(solution)/shard_map/ppermute | solution.py:27
  28.9 4.9 %collective-permute-start.16 = (bf16[96,128]{1,0:T(8,128)(2,1)S(1)}, bf16[96,128]{1,0:T(8,128)(2,1)S(1)}, u32[]{:S(2)}, u32[]{:S(2)}) collective-permute-start(bf16[96,128]{1,0:T(8,128)(2,1)S(1)} %get-tuple-element.59), channel_id=1, source_target_pairs={{0,3},{1,2},{2,1},{3,0},{4,7},{5,6},{6,5},{7,4},{8,11},{9,10},{10,... | collective-permute-start | bytes 73736 | tf_op jit(solution)/shard_map/ppermute | solution.py:27
  29.7 4.1 %collective-permute-start.9 = (bf16[96,128]{1,0:T(8,128)(2,1)S(1)}, bf16[96,128]{1,0:T(8,128)(2,1)S(1)}, u32[]{:S(2)}, u32[]{:S(2)}) collective-permute-start(bf16[96,128]{1,0:T(8,128)(2,1)S(1)} %get-tuple-element.49), channel_id=1, source_target_pairs={{0,5},{1,4},{2,7},{3,6},{4,1},{5,0},{6,3},{7,2},{8,13},{9,12},{10,... | collective-permute-start | bytes 73736 | tf_op jit(solution)/shard_map/ppermute | solution.py:27
  30.6 4.2 %collective-permute-start.10 = (bf16[96,128]{1,0:T(8,128)(2,1)S(1)}, bf16[96,128]{1,0:T(8,128)(2,1)S(1)}, u32[]{:S(2)}, u32[]{:S(2)}) collective-permute-start(bf16[96,128]{1,0:T(8,128)(2,1)S(1)} %get-tuple-element.50), channel_id=1, source_target_pairs={{0,9},{1,8},{2,11},{3,10},{4,13},{5,12},{6,15},{7,14},{8,1},{9,0},... | collective-permute-start | bytes 73736 | tf_op jit(solution)/shard_map/ppermute | solution.py:27
  32.4 5.0 %collective-permute-start.11 = (bf16[96,128]{1,0:T(8,128)(2,1)S(1)}, bf16[96,128]{1,0:T(8,128)(2,1)S(1)}, u32[]{:S(2)}, u32[]{:S(2)}) collective-permute-start(bf16[96,128]{1,0:T(8,128)(2,1)S(1)} %get-tuple-element.51), channel_id=1, source_target_pairs={{0,13},{1,12},{2,15},{3,14},{4,9},{5,8},{6,11},{7,10},{8,5},{9,4},... | collective-permute-start | bytes 73736 | tf_op jit(solution)/shard_map/ppermute | solution.py:27
  37.6 5.6 %collective-permute-start.19 = (bf16[192,128]{1,0:T(8,128)(2,1)S(1)}, bf16[192,128]{1,0:T(8,128)(2,1)S(1)}, u32[]{:S(2)}, u32[]{:S(2)}) collective-permute-start(bf16[192,128]{1,0:T(8,128)(2,1)S(1)} %get-tuple-element.60.refs_0_), channel_id=1, source_target_pairs={{0,13},{1,12},{2,15},{3,14},{4,9},{5,8},{6,11},{7,10},{8,5},{9,4},... | collective-permute-start | bytes 147464 | tf_op jit(solution)/shard_map/ppermute | solution.py:27
  39.0 6.5 %collective-permute-start.18 = (bf16[192,128]{1,0:T(8,128)(2,1)S(1)}, bf16[192,128]{1,0:T(8,128)(2,1)S(1)}, u32[]{:S(2)}, u32[]{:S(2)}) collective-permute-start(bf16[192,128]{1,0:T(8,128)(2,1)S(1)} %get-tuple-element.60.refs_0_), channel_id=1, source_target_pairs={{0,9},{1,8},{2,11},{3,10},{4,13},{5,12},{6,15},{7,14},{8,1},{9,0},... | collective-permute-start | bytes 147464 | tf_op jit(solution)/shard_map/ppermute | solution.py:27
  39.0 6.5 %collective-permute-start.17 = (bf16[192,128]{1,0:T(8,128)(2,1)S(1)}, bf16[192,128]{1,0:T(8,128)(2,1)S(1)}, u32[]{:S(2)}, u32[]{:S(2)}) collective-permute-start(bf16[192,128]{1,0:T(8,128)(2,1)S(1)} %get-tuple-element.60.refs_0_), channel_id=1, source_target_pairs={{0,5},{1,4},{2,7},{3,6},{4,1},{5,0},{6,3},{7,2},{8,13},{9,12},{10,... | collective-permute-start | bytes 147464 | tf_op jit(solution)/shard_map/ppermute | solution.py:27
  41.5 7.6 %collective-permute-start.6 = (bf16[96,512]{1,0:T(8,128)(2,1)S(1)}, bf16[96,512]{1,0:T(8,128)(2,1)S(1)}, u32[]{:S(2)}, u32[]{:S(2)}) collective-permute-start(bf16[96,512]{1,0:T(8,128)(2,1)S(1)} %get-tuple-element.43.own_ref.lhs_ref), channel_id=1, source_target_pairs={{0,16},{1,17},{2,18},{3,19},{4,20},{5,21},{6,22},{7,23},{8,24},{9,... | collective-permute-start | bytes 294920 | tf_op jit(solution)/shard_map/ppermute | solution.py:27
  45.7 4.9 %collective-permute-start.23 = (bf16[24,2048]{1,0:T(8,128)(2,1)S(1)}, bf16[24,2048]{1,0:T(8,128)(2,1)S(1)}, u32[]{:S(2)}, u32[]{:S(2)}) collective-permute-start(bf16[24,2048]{1,0:T(8,128)(2,1)S(1)} %get-tuple-element.61.refs_0_), channel_id=1, source_target_pairs={{0,17},{1,16},{2,19},{3,18},{4,21},{5,20},{6,23},{7,22},{8,25},{9,... | collective-permute-start | bytes 294920 | tf_op jit(solution)/shard_map/ppermute | solution.py:27
  47.0 4.0 %collective-permute-start.21 = (bf16[24,2048]{1,0:T(8,128)(2,1)S(1)}, bf16[24,2048]{1,0:T(8,128)(2,1)S(1)}, u32[]{:S(2)}, u32[]{:S(2)}) collective-permute-start(bf16[24,2048]{1,0:T(8,128)(2,1)S(1)} %get-tuple-element.61.refs_0_), channel_id=1, source_target_pairs={{0,1},{1,0},{2,3},{3,2},{4,5},{5,4},{6,7},{7,6},{8,9},{9,8},{10,11... | collective-permute-start | bytes 294920 | tf_op jit(solution)/shard_map/ppermute | solution.py:27
  47.4 4.8 %collective-permute-start.20 = (bf16[24,2048]{1,0:T(8,128)(2,1)S(1)}, bf16[24,2048]{1,0:T(8,128)(2,1)S(1)}, u32[]{:S(2)}, u32[]{:S(2)}) collective-permute-start(bf16[24,2048]{1,0:T(8,128)(2,1)S(1)} %get-tuple-element.61.refs_0_), channel_id=1, source_target_pairs={{0,3},{1,2},{2,1},{3,0},{4,7},{5,6},{6,5},{7,4},{8,11},{9,10},{10,... | collective-permute-start | bytes 294920 | tf_op jit(solution)/shard_map/ppermute | solution.py:27
  48.3 6.0 %collective-permute-start.27 = (bf16[24,2048]{1,0:T(8,128)(2,1)S(1)}, bf16[24,2048]{1,0:T(8,128)(2,1)S(1)}, u32[]{:S(2)}, u32[]{:S(2)}) collective-permute-start(bf16[24,2048]{1,0:T(8,128)(2,1)S(1)} %get-tuple-element.62.refs_8_), channel_id=1, source_target_pairs={{0,3},{1,2},{2,1},{3,0},{4,7},{5,6},{6,5},{7,4},{8,11},{9,10},{10,... | collective-permute-start | bytes 294920 | tf_op jit(solution)/shard_map/ppermute | solution.py:27
  49.1 5.4 %collective-permute-start.30 = (bf16[24,2048]{1,0:T(8,128)(2,1)S(1)}, bf16[24,2048]{1,0:T(8,128)(2,1)S(1)}, u32[]{:S(2)}, u32[]{:S(2)}) collective-permute-start(bf16[24,2048]{1,0:T(8,128)(2,1)S(1)} %get-tuple-element.62.refs_8_), channel_id=1, source_target_pairs={{0,17},{1,16},{2,19},{3,18},{4,21},{5,20},{6,23},{7,22},{8,25},{9,... | collective-permute-start | bytes 294920 | tf_op jit(solution)/shard_map/ppermute | solution.py:27
  50.6 4.4 %collective-permute-start.28 = (bf16[24,2048]{1,0:T(8,128)(2,1)S(1)}, bf16[24,2048]{1,0:T(8,128)(2,1)S(1)}, u32[]{:S(2)}, u32[]{:S(2)}) collective-permute-start(bf16[24,2048]{1,0:T(8,128)(2,1)S(1)} %get-tuple-element.62.refs_8_), channel_id=1, source_target_pairs={{0,1},{1,0},{2,3},{3,2},{4,5},{5,4},{6,7},{7,6},{8,9},{9,8},{10,11... | collective-permute-start | bytes 294920 | tf_op jit(solution)/shard_map/ppermute | solution.py:27
  51.0 5.4 %collective-permute-start.25 = (bf16[24,2048]{1,0:T(8,128)(2,1)S(1)}, bf16[24,2048]{1,0:T(8,128)(2,1)S(1)}, u32[]{:S(2)}, u32[]{:S(2)}) collective-permute-start(bf16[24,2048]{1,0:T(8,128)(2,1)S(1)} %collective-permute-done.23.refs_6_), channel_id=1, source_target_pairs={{0,3},{1,2},{2,1},{3,0},{4,7},{5,6},{6,5},{7,4},{8,11},{9,10},{10,... | collective-permute-start | bytes 294920 | tf_op jit(solution)/shard_map/ppermute | solution.py:27
  52.2 4.3 %collective-permute-start.24 = (bf16[24,2048]{1,0:T(8,128)(2,1)S(1)}, bf16[24,2048]{1,0:T(8,128)(2,1)S(1)}, u32[]{:S(2)}, u32[]{:S(2)}) collective-permute-start(bf16[24,2048]{1,0:T(8,128)(2,1)S(1)} %collective-permute-done.23.refs_6_), channel_id=1, source_target_pairs={{0,1},{1,0},{2,3},{3,2},{4,5},{5,4},{6,7},{7,6},{8,9},{9,8},{10,11... | collective-permute-start | bytes 294920 | tf_op jit(solution)/shard_map/ppermute | solution.py:27
  54.3 4.2 %collective-permute-start.32 = (bf16[24,2048]{1,0:T(8,128)(2,1)S(1)}, bf16[24,2048]{1,0:T(8,128)(2,1)S(1)}, u32[]{:S(2)}, u32[]{:S(2)}) collective-permute-start(bf16[24,2048]{1,0:T(8,128)(2,1)S(1)} %collective-permute-done.27.refs_9_), channel_id=1, source_target_pairs={{0,17},{1,16},{2,19},{3,18},{4,21},{5,20},{6,23},{7,22},{8,25},{9,... | collective-permute-start | bytes 294920 | tf_op jit(solution)/shard_map/ppermute | solution.py:27
  54.5 5.6 %collective-permute-start.29 = (bf16[24,2048]{1,0:T(8,128)(2,1)S(1)}, bf16[24,2048]{1,0:T(8,128)(2,1)S(1)}, u32[]{:S(2)}, u32[]{:S(2)}) collective-permute-start(bf16[24,2048]{1,0:T(8,128)(2,1)S(1)} %collective-permute-done.27.refs_9_), channel_id=1, source_target_pairs={{0,1},{1,0},{2,3},{3,2},{4,5},{5,4},{6,7},{7,6},{8,9},{9,8},{10,11... | collective-permute-start | bytes 294920 | tf_op jit(solution)/shard_map/ppermute | solution.py:27
  55.0 5.1 %collective-permute-start.22 = (bf16[24,2048]{1,0:T(8,128)(2,1)S(1)}, bf16[24,2048]{1,0:T(8,128)(2,1)S(1)}, u32[]{:S(2)}, u32[]{:S(2)}) collective-permute-start(bf16[24,2048]{1,0:T(8,128)(2,1)S(1)} %collective-permute-done.20.refs_1_), channel_id=1, source_target_pairs={{0,1},{1,0},{2,3},{3,2},{4,5},{5,4},{6,7},{7,6},{8,9},{9,8},{10,11... | collective-permute-start | bytes 294920 | tf_op jit(solution)/shard_map/ppermute | solution.py:27
  56.4 3.7 %collective-permute-start.31 = (bf16[24,2048]{1,0:T(8,128)(2,1)S(1)}, bf16[24,2048]{1,0:T(8,128)(2,1)S(1)}, u32[]{:S(2)}, u32[]{:S(2)}) collective-permute-start(bf16[24,2048]{1,0:T(8,128)(2,1)S(1)} %collective-permute-done.30.refs_14_), channel_id=1, source_target_pairs={{0,1},{1,0},{2,3},{3,2},{4,5},{5,4},{6,7},{7,6},{8,9},{9,8},{10,11... | collective-permute-start | bytes 294920 | tf_op jit(solution)/shard_map/ppermute | solution.py:27
  56.5 3.6 %collective-permute-start.26 = (bf16[24,2048]{1,0:T(8,128)(2,1)S(1)}, bf16[24,2048]{1,0:T(8,128)(2,1)S(1)}, u32[]{:S(2)}, u32[]{:S(2)}) collective-permute-start(bf16[24,2048]{1,0:T(8,128)(2,1)S(1)} %collective-permute-done.25.refs_7_), channel_id=1, source_target_pairs={{0,1},{1,0},{2,3},{3,2},{4,5},{5,4},{6,7},{7,6},{8,9},{9,8},{10,11... | collective-permute-start | bytes 294920 | tf_op jit(solution)/shard_map/ppermute | solution.py:27
  58.5 1.7 %collective-permute-start.33 = (bf16[24,2048]{1,0:T(8,128)(2,1)S(1)}, bf16[24,2048]{1,0:T(8,128)(2,1)S(1)}, u32[]{:S(2)}, u32[]{:S(2)}) collective-permute-start(bf16[24,2048]{1,0:T(8,128)(2,1)S(1)} %collective-permute-done.32.refs_15_), channel_id=1, source_target_pairs={{0,1},{1,0},{2,3},{3,2},{4,5},{5,4},{6,7},{7,6},{8,9},{9,8},{10,11... | collective-permute-start | bytes 294920 | tf_op jit(solution)/shard_map/ppermute | solution.py:27

commit v4 on v3

--- a/solution.py
+++ b/solution.py
@@ -333,19 +333,23 @@
         out_ref[:, t * LANES : (t + 1) * LANES] = tile.astype(jnp.bfloat16)
 
 
-def line_kernel(units, *refs):
-    sources, outs, lines = refs[:units], refs[units:-1], refs[-1]
-    size = sources[0].shape[0] // 2
-    count, width = outs[0].shape
+def rest_lines_kernel(*refs):
+    units, outs = refs[:-2], refs[-2:]
+    size = units[0].shape[0] // 2
+    for half, out in enumerate(outs):
+        for m, source in enumerate(units):
+            out[m * size : (m + 1) * size, :] = source[half * size : (half + 1) * size]
+
+
+def join_kernel(half, head_ref, rest_ref, out_ref, lines):
+    size = head_ref.shape[0] // 2
+    count, width = out_ref.shape
     depth = width // LANES
-    for m, source in enumerate(sources):
-        for half in range(2):
-            rows = slice(m * size, (m + 1) * size)
-            lines[half, rows, :] = source[half * size : (half + 1) * size].astype(jnp.float32)
-    for half, out in enumerate(outs):
-        for t in range(depth):
-            tile = lines[half, pl.ds(t, count, stride=depth), :]
-            out[:, t * LANES : (t + 1) * LANES] = tile.astype(jnp.bfloat16)
+    lines[:size] = head_ref[half * size : (half + 1) * size].astype(jnp.float32)
+    lines[size:] = rest_ref[...].astype(jnp.float32)
+    for t in range(depth):
+        tile = lines[pl.ds(t, count, stride=depth), :]
+        out_ref[:, t * LANES : (t + 1) * LANES] = tile.astype(jnp.bfloat16)
 
 
 def turn_kernel(own_ref, other_ref, out_ref):
@@ -510,18 +514,33 @@
     )
     (grad,) = local_call(rows_kernel, [((unit, block_student), bf16)], [grad])
 
-    line = [slope] + far_across([slope] * far)
-    lines = local_call(
-        functools.partial(line_kernel, far),
-        [((far * unit, cut), bf16)] * 2,
-        line,
-        scratch=[pltpu.VMEM((2, far * small, LANES), f32)],
-    )
+    arrived = far_across([slope] * far)
+    head_x = across(slope, 1, 1)
+    head_y = across(slope, 0, 3)
+    head_both = across(slope, 1, 2)
+    rest_a, rest_b = local_call(
+        rest_lines_kernel, [(((far - 1) * small, LANES), bf16)] * 2, arrived
+    )
+
+    def join(half_index, head, rest):
+        (rows_of,) = local_call(
+            functools.partial(join_kernel, half_index),
+            [((far * unit, cut), bf16)],
+            [head, rest],
+            scratch=[pltpu.VMEM((far * small, LANES), f32)],
+        )
+        return rows_of
+
     scale = 1.0 / math.sqrt(lax.axis_size("group") * half)
-    first, second = lines
-    first_group, second_near = across(first, 1, 1), across(second, 0, 3)
-    second_group, first_near = across(second, 1, 1), across(first, 0, 3)
-    first_both, second_both = across(first_group, 0, 3), across(second_near, 1, 1)
+    group_a = across(rest_a, 1, 1)
+    near_b_rest = across(rest_b, 0, 3)
+    group_b, near_a_rest = across(rest_b, 1, 1), across(rest_a, 0, 3)
+    first, second = join(0, slope, rest_a), join(1, slope, rest_b)
+    first_group, second_near = join(0, head_x, group_a), join(1, head_y, near_b_rest)
+    second_group, first_near = join(1, head_x, group_b), join(0, head_y, near_a_rest)
+    both_a = across(group_a, 0, 3)
+    both_b = across(near_b_rest, 1, 1)
+    first_both, second_both = join(0, head_both, both_a), join(1, head_both, both_b)
     (turned,) = local_call(turn_kernel, [((block_teacher, 2 * half), bf16)], [states, other_states])
     pieces = []
     for own, other in (
@@ -529,7 +548,9 @@
         ((second, second_near), (second_group, second_both)),
     ):
         pieces += [*own, *[across(piece, 0, 1) for piece in own]]
-        pieces += [*[across(piece, 0, 1) for piece in other], *other]
+        pieces.append(across(other[0], 0, 1))
+        pieces.append(across(other[1], 0, 1))
+        pieces += other
     grad_proj = grad_call(scale, turned, pieces, len(pieces) // 2, (block_teacher, block_student))
     return grad_proj, grad
 

time: 62.8 us -> 68.4 us (1.089)
  starting transfers between devices: 30.4 us -> 33.7 us
  waiting for transfers between devices: 22.2 us -> 24 us
    ppermute x34 -> x37, starting transfers between devices: 30.4 us -> 33.7 us  [across(): return lax.ppermute(value, ('group', 'dev'), pairs)]
    ppermute x34 -> x37, waiting for transfers between devices: 22.2 us -> 24 us  [across(): return lax.ppermute(value, ('group', 'dev'), pairs)]
    pallas_call x15 -> x23, Pallas kernels: 6.75 us -> 7.28 us  [local_call(): pl.pallas_call(kernel, out_shape=[jax.ShapeDtypeStruct(shape, kind) for s...]
  transfers between devices with their start and end apart: 34 -> 37, of which waited for: 16 -> 16; matrix products, arithmetic and copies ran while one was open for 0% -> 0% of each run, Pallas kernels for 8% -> 8%
where the time goes in v4:
time: 68.4 us; the launch traced here: 68.2 us
  starting transfers between devices  33.7 us (49%)
  waiting for transfers between devices  24 us (35%)
  Pallas kernels  9.65 us (14%)
  between operations  0.82 us (1%)
    ppermute x37, starting transfers between devices, across(): return lax.ppermute(value, ('group', 'dev'), pairs)  33.7 us
    ppermute x37, waiting for transfers between devices, across(): return lax.ppermute(value, ('group', 'dev'), pairs)  24 us
    pallas_call x23, Pallas kernels, local_call(): pl.pallas_call(kernel, out_shape=[jax.ShapeDtypeStruct(shape, kind) for s...  7.28 us
    pallas_call x1, Pallas kernels, grad_call(): pl.pallas_call(functools.partial(grad_kernel, scale, step, per), out_shap...  2.37 us
  transfers between devices with their start and end apart: 37, of which 16 were waited for; matrix products, arithmetic and copies ran while one was open for 0% of the time, Pallas kernels for 8%

profile of v4, /device:TPU:0, one launch (start us, length us, event | category | flops | bytes accessed | tf_op | source)
XLA Modules:
  0.0 68.2 jit_solution(4593720153010727901)
XLA Ops:
  0.6 0.9 %shard_map.60 = (bf16[24,512]{1,0:T(8,128)(2,1)S(1)}, bf16[24,512]{1,0:T(8,128)(2,1)S(1)}, bf16[24,512]{1,0:T(8,128)(2,1)S(1)}, bf16[24,512]{1,0:T(8,128)(2,1)S(1)}) custom-call(bf16[6,8192]{1,0:T(8,128)(2,1)} %x_ref.1), custom_call_target="tpu_custom_call" | custom-call | tf_op jit(solution)/shard_map/pallas_call | solution.py:136
  1.5 0.6 collective-permute-start
  2.1 2.6 %collective-permute-start.1 = (bf16[24,512]{1,0:T(8,128)(2,1)S(1)}, bf16[24,512]{1,0:T(8,128)(2,1)S(1)}, u32[]{:S(2)}, u32[]{:S(2)}) collective-permute-start(bf16[24,512]{1,0:T(8,128)(2,1)S(1)} %get-tuple-element.36), channel_id=1, source_target_pairs={{0,2},{1,3},{2,0},{3,1},{4,6},{5,7},{6,4},{7,5},{8,10},{9,11},{10,... | collective-permute-start | bytes 73736 | tf_op jit(solution)/shard_map/ppermute | solution.py:27
  4.7 1.8 %collective-permute-done.1.refs_2_ = bf16[24,512]{1,0:T(8,128)(2,1)S(1)} collective-permute-done((bf16[24,512]{1,0:T(8,128)(2,1)S(1)}, bf16[24,512]{1,0:T(8,128)(2,1)S(1)}, u32[]{:S(2)}, u32[]{:S(2)}) %collective-permute-start.1) | collective-permute-done | bytes 24608 | tf_op jit(solution)/shard_map/ppermute | solution.py:27
  6.5 1.4 %collective-permute-done.2.refs_3_ = bf16[24,512]{1,0:T(8,128)(2,1)S(1)} collective-permute-done((bf16[24,512]{1,0:T(8,128)(2,1)S(1)}, bf16[24,512]{1,0:T(8,128)(2,1)S(1)}, u32[]{:S(2)}, u32[]{:S(2)}) %collective-permute-start.2) | collective-permute-done | bytes 24608 | tf_op jit(solution)/shard_map/ppermute | solution.py:27
  8.0 1.4 %collective-permute-start.3 = (bf16[24,512]{1,0:T(8,128)(2,1)S(1)}, bf16[24,512]{1,0:T(8,128)(2,1)S(1)}, u32[]{:S(2)}, u32[]{:S(2)}) collective-permute-start(bf16[24,512]{1,0:T(8,128)(2,1)S(1)} %get-tuple-element.39), channel_id=1, source_target_pairs={{0,5},{1,4},{2,7},{3,6},{4,1},{5,0},{6,3},{7,2},{8,13},{9,12},{10,... | collective-permute-start | bytes 73736 | tf_op jit(solution)/shard_map/ppermute | solution.py:27
  9.4 2.6 %collective-permute-start.4 = (bf16[24,512]{1,0:T(8,128)(2,1)S(1)}, bf16[24,512]{1,0:T(8,128)(2,1)S(1)}, u32[]{:S(2)}, u32[]{:S(2)}) collective-permute-start(bf16[24,512]{1,0:T(8,128)(2,1)S(1)} %get-tuple-element.40), channel_id=1, source_target_pairs={{0,9},{1,8},{2,11},{3,10},{4,13},{5,12},{6,15},{7,14},{8,1},{9,0},... | collective-permute-start | bytes 73736 | tf_op jit(solution)/shard_map/ppermute | solution.py:27
  11.9 1.6 %shard_map.59 = (bf16[96,96]{1,0:T(8,128)(2,1)S(1)}, bf16[512,2048]{1,0:T(8,128)(2,1)S(1)}) custom-call(s32[2,16]{1,0:T(2,128)} %owner_ref.1, bf16[512,4096]{1,0:T(8,128)(2,1)} %tiles_ref.3), custom_call_target="tpu_custom_call" | custom-call | flops 201326592 | bytes 2097152 | tf_op jit(solution)/shard_map/pallas_call | solution.py:136
  13.8 3.2 %collective-permute-done.5.refs_3_ = bf16[24,512]{1,0:T(8,128)(2,1)S(1)} collective-permute-done((bf16[24,512]{1,0:T(8,128)(2,1)S(1)}, bf16[24,512]{1,0:T(8,128)(2,1)S(1)}, u32[]{:S(2)}, u32[]{:S(2)}) %collective-permute-start.5) | collective-permute-done | bytes 24608 | tf_op jit(solution)/shard_map/ppermute | solution.py:27
  17.0 0.6 shard_map.62
  17.8 1.6 %shard_map.66.tiles_ref = bf16[512,2048]{1,0:T(8,128)(2,1)S(1)} custom-call(bf16[512,4096]{1,0:T(8,128)(2,1)} %tiles_ref.3), custom_call_target="tpu_custom_call" | custom-call | flops 201326592 | bytes 2097152 | tf_op jit(solution)/shard_map/pallas_call | solution.py:136
  19.4 0.5 shard_map.67
  19.8 0.4 collective-permute-start.12
  20.3 0.6 collective-permute-start.8
  20.9 0.5 collective-permute-done.12.arrived_ref
  21.6 0.9 %collective-permute-start.14 = (bf16[192,128]{1,0:T(8,128)(2,1)S(1)}, bf16[192,128]{1,0:T(8,128)(2,1)S(1)}, u32[]{:S(2)}, u32[]{:S(2)}) collective-permute-start(bf16[192,128]{1,0:T(8,128)(2,1)S(1)} %get-tuple-element.56), channel_id=1, source_target_pairs={{0,9},{1,8},{2,11},{3,10},{4,13},{5,12},{6,15},{7,14},{8,1},{9,0},... | collective-permute-start | bytes 147464 | tf_op jit(solution)/shard_map/ppermute | solution.py:27
  22.5 3.2 %collective-permute-start.15 = (bf16[192,128]{1,0:T(8,128)(2,1)S(1)}, bf16[192,128]{1,0:T(8,128)(2,1)S(1)}, u32[]{:S(2)}, u32[]{:S(2)}) collective-permute-start(bf16[192,128]{1,0:T(8,128)(2,1)S(1)} %get-tuple-element.57), channel_id=1, source_target_pairs={{0,13},{1,12},{2,15},{3,14},{4,9},{5,8},{6,11},{7,10},{8,5},{9,4},... | collective-permute-start | bytes 147464 | tf_op jit(solution)/shard_map/ppermute | solution.py:27
  25.7 0.5 collective-permute-done.14.refs_2_
  26.2 2.6 %collective-permute-done.15.refs_3_ = bf16[192,128]{1,0:T(8,128)(2,1)S(1)} collective-permute-done((bf16[192,128]{1,0:T(8,128)(2,1)S(1)}, bf16[192,128]{1,0:T(8,128)(2,1)S(1)}, u32[]{:S(2)}, u32[]{:S(2)}) %collective-permute-start.15) | collective-permute-done | bytes 49184 | tf_op jit(solution)/shard_map/ppermute | solution.py:27
  28.9 0.8 %collective-permute-start.16 = (bf16[96,128]{1,0:T(8,128)(2,1)S(1)}, bf16[96,128]{1,0:T(8,128)(2,1)S(1)}, u32[]{:S(2)}, u32[]{:S(2)}) collective-permute-start(bf16[96,128]{1,0:T(8,128)(2,1)S(1)} %get-tuple-element.59), channel_id=1, source_target_pairs={{0,3},{1,2},{2,1},{3,0},{4,7},{5,6},{6,5},{7,4},{8,11},{9,10},{10,... | collective-permute-start | bytes 73736 | tf_op jit(solution)/shard_map/ppermute | solution.py:27
  29.7 0.9 %collective-permute-start.9 = (bf16[96,128]{1,0:T(8,128)(2,1)S(1)}, bf16[96,128]{1,0:T(8,128)(2,1)S(1)}, u32[]{:S(2)}, u32[]{:S(2)}) collective-permute-start(bf16[96,128]{1,0:T(8,128)(2,1)S(1)} %get-tuple-element.49), channel_id=1, source_target_pairs={{0,5},{1,4},{2,7},{3,6},{4,1},{5,0},{6,3},{7,2},{8,13},{9,12},{10,... | collective-permute-start | bytes 73736 | tf_op jit(solution)/shard_map/ppermute | solution.py:27
  30.6 1.8 %collective-permute-start.10 = (bf16[96,128]{1,0:T(8,128)(2,1)S(1)}, bf16[96,128]{1,0:T(8,128)(2,1)S(1)}, u32[]{:S(2)}, u32[]{:S(2)}) collective-permute-start(bf16[96,128]{1,0:T(8,128)(2,1)S(1)} %get-tuple-element.50), channel_id=1, source_target_pairs={{0,9},{1,8},{2,11},{3,10},{4,13},{5,12},{6,15},{7,14},{8,1},{9,0},... | collective-permute-start | bytes 73736 | tf_op jit(solution)/shard_map/ppermute | solution.py:27
  32.4 1.4 %collective-permute-start.11 = (bf16[96,128]{1,0:T(8,128)(2,1)S(1)}, bf16[96,128]{1,0:T(8,128)(2,1)S(1)}, u32[]{:S(2)}, u32[]{:S(2)}) collective-permute-start(bf16[96,128]{1,0:T(8,128)(2,1)S(1)} %get-tuple-element.51), channel_id=1, source_target_pairs={{0,13},{1,12},{2,15},{3,14},{4,9},{5,8},{6,11},{7,10},{8,5},{9,4},... | collective-permute-start | bytes 73736 | tf_op jit(solution)/shard_map/ppermute | solution.py:27
  33.8 1.0 %collective-permute-done.10.refs_2_ = bf16[96,128]{1,0:T(8,128)(2,1)S(1)} collective-permute-done((bf16[96,128]{1,0:T(8,128)(2,1)S(1)}, bf16[96,128]{1,0:T(8,128)(2,1)S(1)}, u32[]{:S(2)}, u32[]{:S(2)}) %collective-permute-start.10) | collective-permute-done | bytes 24608 | tf_op jit(solution)/shard_map/ppermute | solution.py:27
  34.8 2.6 %collective-permute-done.11.refs_3_ = bf16[96,128]{1,0:T(8,128)(2,1)S(1)} collective-permute-done((bf16[96,128]{1,0:T(8,128)(2,1)S(1)}, bf16[96,128]{1,0:T(8,128)(2,1)S(1)}, u32[]{:S(2)}, u32[]{:S(2)}) %collective-permute-start.11) | collective-permute-done | bytes 24608 | tf_op jit(solution)/shard_map/ppermute | solution.py:27
  37.6 1.4 %collective-permute-start.19 = (bf16[192,128]{1,0:T(8,128)(2,1)S(1)}, bf16[192,128]{1,0:T(8,128)(2,1)S(1)}, u32[]{:S(2)}, u32[]{:S(2)}) collective-permute-start(bf16[192,128]{1,0:T(8,128)(2,1)S(1)} %get-tuple-element.60.head_ref), channel_id=1, source_target_pairs={{0,13},{1,12},{2,15},{3,14},{4,9},{5,8},{6,11},{7,10},{8,5},{9,4},... | collective-permute-start | bytes 147464 | tf_op jit(solution)/shard_map/ppermute | solution.py:27
  39.0 2.5 %collective-permute-start.17 = (bf16[192,128]{1,0:T(8,128)(2,1)S(1)}, bf16[192,128]{1,0:T(8,128)(2,1)S(1)}, u32[]{:S(2)}, u32[]{:S(2)}) collective-permute-start(bf16[192,128]{1,0:T(8,128)(2,1)S(1)} %get-tuple-element.60.head_ref), channel_id=1, source_target_pairs={{0,5},{1,4},{2,7},{3,6},{4,1},{5,0},{6,3},{7,2},{8,13},{9,12},{10,... | collective-permute-start | bytes 147464 | tf_op jit(solution)/shard_map/ppermute | solution.py:27
  41.5 1.7 %collective-permute-done.19.refs_2_ = bf16[192,128]{1,0:T(8,128)(2,1)S(1)} collective-permute-done((bf16[192,128]{1,0:T(8,128)(2,1)S(1)}, bf16[192,128]{1,0:T(8,128)(2,1)S(1)}, u32[]{:S(2)}, u32[]{:S(2)}) %collective-permute-start.19) | collective-permute-done | bytes 49184 | tf_op jit(solution)/shard_map/ppermute | solution.py:27
  43.2 2.3 %collective-permute-done.18.refs_1_ = bf16[192,128]{1,0:T(8,128)(2,1)S(1)} collective-permute-done((bf16[192,128]{1,0:T(8,128)(2,1)S(1)}, bf16[192,128]{1,0:T(8,128)(2,1)S(1)}, u32[]{:S(2)}, u32[]{:S(2)}) %collective-permute-start.18) | collective-permute-done | bytes 49184 | tf_op jit(solution)/shard_map/ppermute | solution.py:27
  45.6 1.3 %collective-permute-start.25 = (bf16[288,128]{1,0:T(8,128)(2,1)S(1)}, bf16[288,128]{1,0:T(8,128)(2,1)S(1)}, u32[]{:S(2)}, u32[]{:S(2)}) collective-permute-start(bf16[288,128]{1,0:T(8,128)(2,1)S(1)} %get-tuple-element.61.rest_ref), channel_id=1, source_target_pairs={{0,17},{1,16},{2,19},{3,18},{4,21},{5,20},{6,23},{7,22},{8,25},{9,... | collective-permute-start | bytes 221192 | tf_op jit(solution)/shard_map/ppermute | solution.py:27
  46.8 1.2 %collective-permute-start.30 = (bf16[288,128]{1,0:T(8,128)(2,1)S(1)}, bf16[288,128]{1,0:T(8,128)(2,1)S(1)}, u32[]{:S(2)}, u32[]{:S(2)}) collective-permute-start(bf16[288,128]{1,0:T(8,128)(2,1)S(1)} %get-tuple-element.62.rest_ref), channel_id=1, source_target_pairs={{0,3},{1,2},{2,1},{3,0},{4,7},{5,6},{6,5},{7,4},{8,11},{9,10},{10,... | collective-permute-start | bytes 221192 | tf_op jit(solution)/shard_map/ppermute | solution.py:27
  48.0 0.5 collective-permute-start.20
  48.6 1.2 %collective-permute-start.21 = (bf16[288,128]{1,0:T(8,128)(2,1)S(1)}, bf16[288,128]{1,0:T(8,128)(2,1)S(1)}, u32[]{:S(2)}, u32[]{:S(2)}) collective-permute-start(bf16[288,128]{1,0:T(8,128)(2,1)S(1)} %get-tuple-element.61.rest_ref), channel_id=1, source_target_pairs={{0,3},{1,2},{2,1},{3,0},{4,7},{5,6},{6,5},{7,4},{8,11},{9,10},{10,... | collective-permute-start | bytes 221192 | tf_op jit(solution)/shard_map/ppermute | solution.py:27
  50.1 1.1 %collective-permute-start.28 = (bf16[288,128]{1,0:T(8,128)(2,1)S(1)}, bf16[288,128]{1,0:T(8,128)(2,1)S(1)}, u32[]{:S(2)}, u32[]{:S(2)}) collective-permute-start(bf16[288,128]{1,0:T(8,128)(2,1)S(1)} %collective-permute-done.25.rest_ref), channel_id=1, source_target_pairs={{0,3},{1,2},{2,1},{3,0},{4,7},{5,6},{6,5},{7,4},{8,11},{9,10},{10,... | collective-permute-start | bytes 221192 | tf_op jit(solution)/shard_map/ppermute | solution.py:27
  51.1 1.0 %collective-permute-done.20.head_ref = bf16[192,128]{1,0:T(8,128)(2,1)S(1)} collective-permute-done((bf16[192,128]{1,0:T(8,128)(2,1)S(1)}, bf16[192,128]{1,0:T(8,128)(2,1)S(1)}, u32[]{:S(2)}, u32[]{:S(2)}) %collective-permute-start.20) | collective-permute-done | bytes 49184 | tf_op jit(solution)/shard_map/ppermute | solution.py:27
  52.1 1.0 %collective-permute-start.27 = (bf16[192,128]{1,0:T(8,128)(2,1)S(1)}, bf16[192,128]{1,0:T(8,128)(2,1)S(1)}, u32[]{:S(2)}, u32[]{:S(2)}) collective-permute-start(bf16[192,128]{1,0:T(8,128)(2,1)S(1)} %get-tuple-element.60.head_ref), channel_id=1, source_target_pairs={{0,18},{1,19},{2,16},{3,17},{4,22},{5,23},{6,20},{7,21},{8,26},{9,... | collective-permute-start | bytes 147464 | tf_op jit(solution)/shard_map/ppermute | solution.py:27
  53.1 2.1 %collective-permute-start.24 = (bf16[192,128]{1,0:T(8,128)(2,1)S(1)}, bf16[192,128]{1,0:T(8,128)(2,1)S(1)}, u32[]{:S(2)}, u32[]{:S(2)}) collective-permute-start(bf16[192,128]{1,0:T(8,128)(2,1)S(1)} %get-tuple-element.60.head_ref), channel_id=1, source_target_pairs={{0,17},{1,16},{2,19},{3,18},{4,21},{5,20},{6,23},{7,22},{8,25},{9,... | collective-permute-start | bytes 147464 | tf_op jit(solution)/shard_map/ppermute | solution.py:27
  55.4 2.2 %collective-permute-done.27.head_ref = bf16[192,128]{1,0:T(8,128)(2,1)S(1)} collective-permute-done((bf16[192,128]{1,0:T(8,128)(2,1)S(1)}, bf16[192,128]{1,0:T(8,128)(2,1)S(1)}, u32[]{:S(2)}, u32[]{:S(2)}) %collective-permute-start.27) | collective-permute-done | bytes 49184 | tf_op jit(solution)/shard_map/ppermute | solution.py:27
  57.6 0.4 collective-permute-start.6
  58.2 0.4 collective-permute-start.22
  58.8 1.5 %collective-permute-start.35 = (bf16[288,128]{1,0:T(8,128)(2,1)S(1)}, bf16[288,128]{1,0:T(8,128)(2,1)S(1)}, u32[]{:S(2)}, u32[]{:S(2)}) collective-permute-start(bf16[288,128]{1,0:T(8,128)(2,1)S(1)} %collective-permute-done.30.rest_ref), channel_id=1, source_target_pairs={{0,17},{1,16},{2,19},{3,18},{4,21},{5,20},{6,23},{7,22},{8,25},{9,... | collective-permute-start | bytes 221192 | tf_op jit(solution)/shard_map/ppermute | solution.py:27
  60.6 2.7 %collective-permute-done.35.rest_ref = bf16[288,128]{1,0:T(8,128)(2,1)S(1)} collective-permute-done((bf16[288,128]{1,0:T(8,128)(2,1)S(1)}, bf16[288,128]{1,0:T(8,128)(2,1)S(1)}, u32[]{:S(2)}, u32[]{:S(2)}) %collective-permute-start.35) | collective-permute-done | bytes 73760 | tf_op jit(solution)/shard_map/ppermute | solution.py:27
  63.3 0.3 collective-permute-start.26
  63.7 0.3 collective-permute-start.34
  64.0 0.3 collective-permute-start.23
  64.5 0.3 collective-permute-start.29
  65.1 0.7 shard_map.82
  65.8 2.4 %shard_map.81 = bf16[512,4096]{1,0:T(8,128)(2,1)} custom-call(bf16[512,192]{1,0:T(8,128)(2,1)S(1)} %shard_map.63.states_ref, bf16[24,2048]{1,0:T(8,128)(2,1)S(1)} %shard_map.73.refs_0_, bf16[24,2048]{1,0:T(8,128)(2,1)S(1)} %shard_map.74.refs_1_, bf16[24,2048]{1,0:T(8,128)(2,1)S(1)} %collective-permute-done.22.refs_2_, ...), custom_call_target="tpu_custom_call" | custom-call | flops 805306368 | bytes 4194304 | tf_op jit(solution)/shard_map/pallas_call | solution.py:387
  (52 shorter events, 3.0 us)
Async XLA Ops:
  1.5 3.2 %collective-permute-start = (bf16[24,512]{1,0:T(8,128)(2,1)S(1)}, bf16[24,512]{1,0:T(8,128)(2,1)S(1)}, u32[]{:S(2)}, u32[]{:S(2)}) collective-permute-start(bf16[24,512]{1,0:T(8,128)(2,1)S(1)} %get-tuple-element.35), channel_id=1, source_target_pairs={{0,1},{1,0},{2,3},{3,2},{4,5},{5,4},{6,7},{7,6},{8,9},{9,8},{10,11... | collective-permute-start | bytes 73736 | tf_op jit(solution)/shard_map/ppermute | solution.py:27
  2.1 4.4 %collective-permute-start.1 = (bf16[24,512]{1,0:T(8,128)(2,1)S(1)}, bf16[24,512]{1,0:T(8,128)(2,1)S(1)}, u32[]{:S(2)}, u32[]{:S(2)}) collective-permute-start(bf16[24,512]{1,0:T(8,128)(2,1)S(1)} %get-tuple-element.36), channel_id=1, source_target_pairs={{0,2},{1,3},{2,0},{3,1},{4,6},{5,7},{6,4},{7,5},{8,10},{9,11},{10,... | collective-permute-start | bytes 73736 | tf_op jit(solution)/shard_map/ppermute | solution.py:27
  4.7 3.3 %collective-permute-start.2 = (bf16[24,512]{1,0:T(8,128)(2,1)S(1)}, bf16[24,512]{1,0:T(8,128)(2,1)S(1)}, u32[]{:S(2)}, u32[]{:S(2)}) collective-permute-start(bf16[24,512]{1,0:T(8,128)(2,1)S(1)} %get-tuple-element.37), channel_id=1, source_target_pairs={{0,3},{1,2},{2,1},{3,0},{4,7},{5,6},{6,5},{7,4},{8,11},{9,10},{10,... | collective-permute-start | bytes 73736 | tf_op jit(solution)/shard_map/ppermute | solution.py:27
  8.0 5.5 %collective-permute-start.3 = (bf16[24,512]{1,0:T(8,128)(2,1)S(1)}, bf16[24,512]{1,0:T(8,128)(2,1)S(1)}, u32[]{:S(2)}, u32[]{:S(2)}) collective-permute-start(bf16[24,512]{1,0:T(8,128)(2,1)S(1)} %get-tuple-element.39), channel_id=1, source_target_pairs={{0,5},{1,4},{2,7},{3,6},{4,1},{5,0},{6,3},{7,2},{8,13},{9,12},{10,... | collective-permute-start | bytes 73736 | tf_op jit(solution)/shard_map/ppermute | solution.py:27
  9.4 4.4 %collective-permute-start.4 = (bf16[24,512]{1,0:T(8,128)(2,1)S(1)}, bf16[24,512]{1,0:T(8,128)(2,1)S(1)}, u32[]{:S(2)}, u32[]{:S(2)}) collective-permute-start(bf16[24,512]{1,0:T(8,128)(2,1)S(1)} %get-tuple-element.40), channel_id=1, source_target_pairs={{0,9},{1,8},{2,11},{3,10},{4,13},{5,12},{6,15},{7,14},{8,1},{9,0},... | collective-permute-start | bytes 73736 | tf_op jit(solution)/shard_map/ppermute | solution.py:27
  11.9 5.0 %collective-permute-start.5 = (bf16[24,512]{1,0:T(8,128)(2,1)S(1)}, bf16[24,512]{1,0:T(8,128)(2,1)S(1)}, u32[]{:S(2)}, u32[]{:S(2)}) collective-permute-start(bf16[24,512]{1,0:T(8,128)(2,1)S(1)} %get-tuple-element.41), channel_id=1, source_target_pairs={{0,13},{1,12},{2,15},{3,14},{4,9},{5,8},{6,11},{7,10},{8,5},{9,4},... | collective-permute-start | bytes 73736 | tf_op jit(solution)/shard_map/ppermute | solution.py:27
  17.6 16.2 %copy-start = (bf16[6,4096]{1,0:T(8,128)(2,1)S(1)}, bf16[6,4096]{1,0:T(8,128)(2,1)}, u32[]{:S(2)}) copy-start(bf16[6,4096]{1,0:T(8,128)(2,1)} %rows_ref.1) | copy-start | bytes 147460
  17.6 2.7 %collective-permute-start.7 = (bf16[48,2048]{1,0:T(8,128)(2,1)S(1)}, bf16[48,2048]{1,0:T(8,128)(2,1)S(1)}, u32[]{:S(2)}, u32[]{:S(2)}) collective-permute-start(bf16[48,2048]{1,0:T(8,128)(2,1)S(1)} %get-tuple-element.45), channel_id=1, source_target_pairs={{0,1},{1,0},{2,3},{3,2},{4,5},{5,4},{6,7},{7,6},{8,9},{9,8},{10,11... | collective-permute-start | bytes 589832 | tf_op jit(solution)/shard_map/ppermute | solution.py:27
  19.8 1.5 %collective-permute-start.12 = (bf16[48,2048]{1,0:T(8,128)(2,1)S(1)}, bf16[48,2048]{1,0:T(8,128)(2,1)S(1)}, u32[]{:S(2)}, u32[]{:S(2)}) collective-permute-start(bf16[48,2048]{1,0:T(8,128)(2,1)S(1)} %get-tuple-element.53), channel_id=1, source_target_pairs={{0,1},{1,0},{2,3},{3,2},{4,5},{5,4},{6,7},{7,6},{8,9},{9,8},{10,11... | collective-permute-start | bytes 589832 | tf_op jit(solution)/shard_map/ppermute | solution.py:27
  20.3 9.3 %collective-permute-start.8 = (bf16[24,2048]{1,0:T(8,128)(2,1)S(1)}, bf16[24,2048]{1,0:T(8,128)(2,1)S(1)}, u32[]{:S(2)}, u32[]{:S(2)}) collective-permute-start(bf16[24,2048]{1,0:T(8,128)(2,1)S(1)} %get-tuple-element.47), channel_id=1, source_target_pairs={{0,3},{1,2},{2,1},{3,0},{4,7},{5,6},{6,5},{7,4},{8,11},{9,10},{10,... | collective-permute-start | bytes 294920 | tf_op jit(solution)/shard_map/ppermute | solution.py:27
  21.6 4.1 %collective-permute-start.13 = (bf16[192,128]{1,0:T(8,128)(2,1)S(1)}, bf16[192,128]{1,0:T(8,128)(2,1)S(1)}, u32[]{:S(2)}, u32[]{:S(2)}) collective-permute-start(bf16[192,128]{1,0:T(8,128)(2,1)S(1)} %get-tuple-element.55), channel_id=1, source_target_pairs={{0,5},{1,4},{2,7},{3,6},{4,1},{5,0},{6,3},{7,2},{8,13},{9,12},{10,... | collective-permute-start | bytes 147464 | tf_op jit(solution)/shard_map/ppermute | solution.py:27
  21.6 4.6 %collective-permute-start.14 = (bf16[192,128]{1,0:T(8,128)(2,1)S(1)}, bf16[192,128]{1,0:T(8,128)(2,1)S(1)}, u32[]{:S(2)}, u32[]{:S(2)}) collective-permute-start(bf16[192,128]{1,0:T(8,128)(2,1)S(1)} %get-tuple-element.56), channel_id=1, source_target_pairs={{0,9},{1,8},{2,11},{3,10},{4,13},{5,12},{6,15},{7,14},{8,1},{9,0},... | collective-permute-start | bytes 147464 | tf_op jit(solution)/shard_map/ppermute | solution.py:27
  22.5 6.3 %collective-permute-start.15 = (bf16[192,128]{1,0:T(8,128)(2,1)S(1)}, bf16[192,128]{1,0:T(8,128)(2,1)S(1)}, u32[]{:S(2)}, u32[]{:S(2)}) collective-permute-start(bf16[192,128]{1,0:T(8,128)(2,1)S(1)} %get-tuple-element.57), channel_id=1, source_target_pairs={{0,13},{1,12},{2,15},{3,14},{4,9},{5,8},{6,11},{7,10},{8,5},{9,4},... | collective-permute-start | bytes 147464 | tf_op jit(solution)/shard_map/ppermute | solution.py:27
  28.9 4.9 %collective-permute-start.16 = (bf16[96,128]{1,0:T(8,128)(2,1)S(1)}, bf16[96,128]{1,0:T(8,128)(2,1)S(1)}, u32[]{:S(2)}, u32[]{:S(2)}) collective-permute-start(bf16[96,128]{1,0:T(8,128)(2,1)S(1)} %get-tuple-element.59), channel_id=1, source_target_pairs={{0,3},{1,2},{2,1},{3,0},{4,7},{5,6},{6,5},{7,4},{8,11},{9,10},{10,... | collective-permute-start | bytes 73736 | tf_op jit(solution)/shard_map/ppermute | solution.py:27
  29.7 4.1 %collective-permute-start.9 = (bf16[96,128]{1,0:T(8,128)(2,1)S(1)}, bf16[96,128]{1,0:T(8,128)(2,1)S(1)}, u32[]{:S(2)}, u32[]{:S(2)}) collective-permute-start(bf16[96,128]{1,0:T(8,128)(2,1)S(1)} %get-tuple-element.49), channel_id=1, source_target_pairs={{0,5},{1,4},{2,7},{3,6},{4,1},{5,0},{6,3},{7,2},{8,13},{9,12},{10,... | collective-permute-start | bytes 73736 | tf_op jit(solution)/shard_map/ppermute | solution.py:27
  30.6 4.2 %collective-permute-start.10 = (bf16[96,128]{1,0:T(8,128)(2,1)S(1)}, bf16[96,128]{1,0:T(8,128)(2,1)S(1)}, u32[]{:S(2)}, u32[]{:S(2)}) collective-permute-start(bf16[96,128]{1,0:T(8,128)(2,1)S(1)} %get-tuple-element.50), channel_id=1, source_target_pairs={{0,9},{1,8},{2,11},{3,10},{4,13},{5,12},{6,15},{7,14},{8,1},{9,0},... | collective-permute-start | bytes 73736 | tf_op jit(solution)/shard_map/ppermute | solution.py:27
  32.4 5.0 %collective-permute-start.11 = (bf16[96,128]{1,0:T(8,128)(2,1)S(1)}, bf16[96,128]{1,0:T(8,128)(2,1)S(1)}, u32[]{:S(2)}, u32[]{:S(2)}) collective-permute-start(bf16[96,128]{1,0:T(8,128)(2,1)S(1)} %get-tuple-element.51), channel_id=1, source_target_pairs={{0,13},{1,12},{2,15},{3,14},{4,9},{5,8},{6,11},{7,10},{8,5},{9,4},... | collective-permute-start | bytes 73736 | tf_op jit(solution)/shard_map/ppermute | solution.py:27
  37.6 5.6 %collective-permute-start.19 = (bf16[192,128]{1,0:T(8,128)(2,1)S(1)}, bf16[192,128]{1,0:T(8,128)(2,1)S(1)}, u32[]{:S(2)}, u32[]{:S(2)}) collective-permute-start(bf16[192,128]{1,0:T(8,128)(2,1)S(1)} %get-tuple-element.60.head_ref), channel_id=1, source_target_pairs={{0,13},{1,12},{2,15},{3,14},{4,9},{5,8},{6,11},{7,10},{8,5},{9,4},... | collective-permute-start | bytes 147464 | tf_op jit(solution)/shard_map/ppermute | solution.py:27
  39.0 6.5 %collective-permute-start.18 = (bf16[192,128]{1,0:T(8,128)(2,1)S(1)}, bf16[192,128]{1,0:T(8,128)(2,1)S(1)}, u32[]{:S(2)}, u32[]{:S(2)}) collective-permute-start(bf16[192,128]{1,0:T(8,128)(2,1)S(1)} %get-tuple-element.60.head_ref), channel_id=1, source_target_pairs={{0,9},{1,8},{2,11},{3,10},{4,13},{5,12},{6,15},{7,14},{8,1},{9,0},... | collective-permute-start | bytes 147464 | tf_op jit(solution)/shard_map/ppermute | solution.py:27
  39.0 6.5 %collective-permute-start.17 = (bf16[192,128]{1,0:T(8,128)(2,1)S(1)}, bf16[192,128]{1,0:T(8,128)(2,1)S(1)}, u32[]{:S(2)}, u32[]{:S(2)}) collective-permute-start(bf16[192,128]{1,0:T(8,128)(2,1)S(1)} %get-tuple-element.60.head_ref), channel_id=1, source_target_pairs={{0,5},{1,4},{2,7},{3,6},{4,1},{5,0},{6,3},{7,2},{8,13},{9,12},{10,... | collective-permute-start | bytes 147464 | tf_op jit(solution)/shard_map/ppermute | solution.py:27
  45.6 4.5 %collective-permute-start.25 = (bf16[288,128]{1,0:T(8,128)(2,1)S(1)}, bf16[288,128]{1,0:T(8,128)(2,1)S(1)}, u32[]{:S(2)}, u32[]{:S(2)}) collective-permute-start(bf16[288,128]{1,0:T(8,128)(2,1)S(1)} %get-tuple-element.61.rest_ref), channel_id=1, source_target_pairs={{0,17},{1,16},{2,19},{3,18},{4,21},{5,20},{6,23},{7,22},{8,25},{9,... | collective-permute-start | bytes 221192 | tf_op jit(solution)/shard_map/ppermute | solution.py:27
  46.8 6.2 %collective-permute-start.30 = (bf16[288,128]{1,0:T(8,128)(2,1)S(1)}, bf16[288,128]{1,0:T(8,128)(2,1)S(1)}, u32[]{:S(2)}, u32[]{:S(2)}) collective-permute-start(bf16[288,128]{1,0:T(8,128)(2,1)S(1)} %get-tuple-element.62.rest_ref), channel_id=1, source_target_pairs={{0,3},{1,2},{2,1},{3,0},{4,7},{5,6},{6,5},{7,4},{8,11},{9,10},{10,... | collective-permute-start | bytes 221192 | tf_op jit(solution)/shard_map/ppermute | solution.py:27
  48.0 4.0 %collective-permute-start.20 = (bf16[192,128]{1,0:T(8,128)(2,1)S(1)}, bf16[192,128]{1,0:T(8,128)(2,1)S(1)}, u32[]{:S(2)}, u32[]{:S(2)}) collective-permute-start(bf16[192,128]{1,0:T(8,128)(2,1)S(1)} %get-tuple-element.60.head_ref), channel_id=1, source_target_pairs={{0,3},{1,2},{2,1},{3,0},{4,7},{5,6},{6,5},{7,4},{8,11},{9,10},{10,... | collective-permute-start | bytes 147464 | tf_op jit(solution)/shard_map/ppermute | solution.py:27
  48.6 9.7 %collective-permute-start.21 = (bf16[288,128]{1,0:T(8,128)(2,1)S(1)}, bf16[288,128]{1,0:T(8,128)(2,1)S(1)}, u32[]{:S(2)}, u32[]{:S(2)}) collective-permute-start(bf16[288,128]{1,0:T(8,128)(2,1)S(1)} %get-tuple-element.61.rest_ref), channel_id=1, source_target_pairs={{0,3},{1,2},{2,1},{3,0},{4,7},{5,6},{6,5},{7,4},{8,11},{9,10},{10,... | collective-permute-start | bytes 221192 | tf_op jit(solution)/shard_map/ppermute | solution.py:27
  49.8 8.8 %collective-permute-start.33 = (bf16[288,128]{1,0:T(8,128)(2,1)S(1)}, bf16[288,128]{1,0:T(8,128)(2,1)S(1)}, u32[]{:S(2)}, u32[]{:S(2)}) collective-permute-start(bf16[288,128]{1,0:T(8,128)(2,1)S(1)} %get-tuple-element.62.rest_ref), channel_id=1, source_target_pairs={{0,17},{1,16},{2,19},{3,18},{4,21},{5,20},{6,23},{7,22},{8,25},{9,... | collective-permute-start | bytes 221192 | tf_op jit(solution)/shard_map/ppermute | solution.py:27
  50.1 8.7 %collective-permute-start.28 = (bf16[288,128]{1,0:T(8,128)(2,1)S(1)}, bf16[288,128]{1,0:T(8,128)(2,1)S(1)}, u32[]{:S(2)}, u32[]{:S(2)}) collective-permute-start(bf16[288,128]{1,0:T(8,128)(2,1)S(1)} %collective-permute-done.25.rest_ref), channel_id=1, source_target_pairs={{0,3},{1,2},{2,1},{3,0},{4,7},{5,6},{6,5},{7,4},{8,11},{9,10},{10,... | collective-permute-start | bytes 221192 | tf_op jit(solution)/shard_map/ppermute | solution.py:27
  52.1 5.5 %collective-permute-start.27 = (bf16[192,128]{1,0:T(8,128)(2,1)S(1)}, bf16[192,128]{1,0:T(8,128)(2,1)S(1)}, u32[]{:S(2)}, u32[]{:S(2)}) collective-permute-start(bf16[192,128]{1,0:T(8,128)(2,1)S(1)} %get-tuple-element.60.head_ref), channel_id=1, source_target_pairs={{0,18},{1,19},{2,16},{3,17},{4,22},{5,23},{6,20},{7,21},{8,26},{9,... | collective-permute-start | bytes 147464 | tf_op jit(solution)/shard_map/ppermute | solution.py:27
  53.1 5.1 %collective-permute-start.24 = (bf16[192,128]{1,0:T(8,128)(2,1)S(1)}, bf16[192,128]{1,0:T(8,128)(2,1)S(1)}, u32[]{:S(2)}, u32[]{:S(2)}) collective-permute-start(bf16[192,128]{1,0:T(8,128)(2,1)S(1)} %get-tuple-element.60.head_ref), channel_id=1, source_target_pairs={{0,17},{1,16},{2,19},{3,18},{4,21},{5,20},{6,23},{7,22},{8,25},{9,... | collective-permute-start | bytes 147464 | tf_op jit(solution)/shard_map/ppermute | solution.py:27
  57.6 6.1 %collective-permute-start.6 = (bf16[96,512]{1,0:T(8,128)(2,1)S(1)}, bf16[96,512]{1,0:T(8,128)(2,1)S(1)}, u32[]{:S(2)}, u32[]{:S(2)}) collective-permute-start(bf16[96,512]{1,0:T(8,128)(2,1)S(1)} %get-tuple-element.43.own_ref.lhs_ref), channel_id=1, source_target_pairs={{0,16},{1,17},{2,18},{3,19},{4,20},{5,21},{6,22},{7,23},{8,24},{9,... | collective-permute-start | bytes 294920 | tf_op jit(solution)/shard_map/ppermute | solution.py:27
  58.1 5.9 %collective-permute-start.31 = (bf16[24,2048]{1,0:T(8,128)(2,1)S(1)}, bf16[24,2048]{1,0:T(8,128)(2,1)S(1)}, u32[]{:S(2)}, u32[]{:S(2)}) collective-permute-start(bf16[24,2048]{1,0:T(8,128)(2,1)S(1)} %shard_map.77.refs_8_), channel_id=1, source_target_pairs={{0,1},{1,0},{2,3},{3,2},{4,5},{5,4},{6,7},{7,6},{8,9},{9,8},{10,11... | collective-permute-start | bytes 294920 | tf_op jit(solution)/shard_map/ppermute | solution.py:27
  58.2 6.1 %collective-permute-start.22 = (bf16[24,2048]{1,0:T(8,128)(2,1)S(1)}, bf16[24,2048]{1,0:T(8,128)(2,1)S(1)}, u32[]{:S(2)}, u32[]{:S(2)}) collective-permute-start(bf16[24,2048]{1,0:T(8,128)(2,1)S(1)} %shard_map.73.refs_0_), channel_id=1, source_target_pairs={{0,1},{1,0},{2,3},{3,2},{4,5},{5,4},{6,7},{7,6},{8,9},{9,8},{10,11... | collective-permute-start | bytes 294920 | tf_op jit(solution)/shard_map/ppermute | solution.py:27
  58.6 5.9 %collective-permute-start.32 = (bf16[24,2048]{1,0:T(8,128)(2,1)S(1)}, bf16[24,2048]{1,0:T(8,128)(2,1)S(1)}, u32[]{:S(2)}, u32[]{:S(2)}) collective-permute-start(bf16[24,2048]{1,0:T(8,128)(2,1)S(1)} %shard_map.78.refs_9_), channel_id=1, source_target_pairs={{0,1},{1,0},{2,3},{3,2},{4,5},{5,4},{6,7},{7,6},{8,9},{9,8},{10,11... | collective-permute-start | bytes 294920 | tf_op jit(solution)/shard_map/ppermute | solution.py:27
  58.8 4.6 %collective-permute-start.35 = (bf16[288,128]{1,0:T(8,128)(2,1)S(1)}, bf16[288,128]{1,0:T(8,128)(2,1)S(1)}, u32[]{:S(2)}, u32[]{:S(2)}) collective-permute-start(bf16[288,128]{1,0:T(8,128)(2,1)S(1)} %collective-permute-done.30.rest_ref), channel_id=1, source_target_pairs={{0,17},{1,16},{2,19},{3,18},{4,21},{5,20},{6,23},{7,22},{8,25},{9,... | collective-permute-start | bytes 221192 | tf_op jit(solution)/shard_map/ppermute | solution.py:27
  63.3 2.4 %collective-permute-start.26 = (bf16[24,2048]{1,0:T(8,128)(2,1)S(1)}, bf16[24,2048]{1,0:T(8,128)(2,1)S(1)}, u32[]{:S(2)}, u32[]{:S(2)}) collective-permute-start(bf16[24,2048]{1,0:T(8,128)(2,1)S(1)} %shard_map.75.refs_6_), channel_id=1, source_target_pairs={{0,1},{1,0},{2,3},{3,2},{4,5},{5,4},{6,7},{7,6},{8,9},{9,8},{10,11... | collective-permute-start | bytes 294920 | tf_op jit(solution)/shard_map/ppermute | solution.py:27
  63.7 2.0 %collective-permute-start.34 = (bf16[24,2048]{1,0:T(8,128)(2,1)S(1)}, bf16[24,2048]{1,0:T(8,128)(2,1)S(1)}, u32[]{:S(2)}, u32[]{:S(2)}) collective-permute-start(bf16[24,2048]{1,0:T(8,128)(2,1)S(1)} %shard_map.79.refs_14_), channel_id=1, source_target_pairs={{0,1},{1,0},{2,3},{3,2},{4,5},{5,4},{6,7},{7,6},{8,9},{9,8},{10,11... | collective-permute-start | bytes 294920 | tf_op jit(solution)/shard_map/ppermute | solution.py:27
  64.0 1.7 %collective-permute-start.23 = (bf16[24,2048]{1,0:T(8,128)(2,1)S(1)}, bf16[24,2048]{1,0:T(8,128)(2,1)S(1)}, u32[]{:S(2)}, u32[]{:S(2)}) collective-permute-start(bf16[24,2048]{1,0:T(8,128)(2,1)S(1)} %shard_map.74.refs_1_), channel_id=1, source_target_pairs={{0,1},{1,0},{2,3},{3,2},{4,5},{5,4},{6,7},{7,6},{8,9},{9,8},{10,11... | collective-permute-start | bytes 294920 | tf_op jit(solution)/shard_map/ppermute | solution.py:27
  64.3 1.5 %collective-permute-start.36 = (bf16[24,2048]{1,0:T(8,128)(2,1)S(1)}, bf16[24,2048]{1,0:T(8,128)(2,1)S(1)}, u32[]{:S(2)}, u32[]{:S(2)}) collective-permute-start(bf16[24,2048]{1,0:T(8,128)(2,1)S(1)} %shard_map.80.refs_15_), channel_id=1, source_target_pairs={{0,1},{1,0},{2,3},{3,2},{4,5},{5,4},{6,7},{7,6},{8,9},{9,8},{10,11... | collective-permute-start | bytes 294920 | tf_op jit(solution)/shard_map/ppermute | solution.py:27
  64.5 1.3 %collective-permute-start.29 = (bf16[24,2048]{1,0:T(8,128)(2,1)S(1)}, bf16[24,2048]{1,0:T(8,128)(2,1)S(1)}, u32[]{:S(2)}, u32[]{:S(2)}) collective-permute-start(bf16[24,2048]{1,0:T(8,128)(2,1)S(1)} %shard_map.76.refs_7_), channel_id=1, source_target_pairs={{0,1},{1,0},{2,3},{3,2},{4,5},{5,4},{6,7},{7,6},{8,9},{9,8},{10,11... | collective-permute-start | bytes 294920 | tf_op jit(solution)/shard_map/ppermute | solution.py:27
